TPU v7x, 32 devices: a whole 2x2x4 slice. The times are simulated.
32 devices in a mesh: grp: 4 (over z), seq: 8 (over y, x, core).
Axes of the slice: x: 2, y: 2, z: 4, core: 2. Of those that a mesh axis runs over, the one named last changes fastest.
Arguments:
- hist_keys: bfloat16 [4, 1024, 1024], P('grp', 'seq'), may hold values from -4 to 4
- hist_values: bfloat16 [4, 1024, 1024], P('grp', 'seq'), may hold values from -6 to 6
- latent_queries: bfloat16 [4, 64, 1024], P('grp', 'seq'), may hold values from -48 to 48
- latent_pos: int32 [4, 64], P('grp'), may hold values from 128 to 1023
- targets: int32 [4, 64], P('grp', 'seq'), may hold values from 0 to 127
- out_proj: bfloat16 [1024, 2048], P('seq'), may hold values from -0.1875 to 0.1875
- norm_gain: float32 [2048], replicated, may hold values from 0.1 to 1.9
- unembed: bfloat16 [2048, 128], replicated, may hold values from -0.125 to 0.125
Outputs:
- loss: float32 [4], P('grp')
- grad_queries: bfloat16 [4, 64, 1024], P('grp', 'seq')
- grad_keys: bfloat16 [4, 1024, 1024], P('grp', 'seq')
- grad_values: bfloat16 [4, 1024, 1024], P('grp', 'seq')
- proj_update: float32 [1024, 2048], P('seq')
All inputs are finite; a program needn't handle non-finite values.
Results may differ from a plain program's by a relative error of at most 0.03.
Values may be sent and summed in bfloat16 or wider, within the bound.
No kernel may reach another device: no remote copies, remote signals or barrier semaphores. Data moves between devices by JAX's collectives and lax.ppermute only.
A program may use at most 64 MiB of HBM per device.

v0:
```python
import jax
import jax.numpy as jnp
from jax import lax
from jax.sharding import PartitionSpec as P

D = 2048
HD = 128


epsilon = 1e-06
loss_factor = 64.0


def joined(part, axis, combine):
    gathered = jax.tree.map(lambda a: lax.all_gather(a, axis), part)

    def take(source):
        return jax.tree.map(lambda a: lax.dynamic_index_in_dim(a, source, 0, False), gathered)

    return lax.fori_loop(
        1, lax.axis_size(axis), lambda source, state: combine(state, take(source)), take(0)
    )


def repeat_heads(stat):
    return jnp.repeat(stat, HD, axis=-1)


def combine(earlier, later):
    best = jnp.maximum(earlier[0], later[0])
    factor_one = jnp.exp(earlier[0] - best)
    factor_two = jnp.exp(later[0] - best)
    denom = earlier[1] * factor_one + later[1] * factor_two
    summed = earlier[2] * repeat_heads(factor_one) + later[2] * repeat_heads(factor_two)
    return (best, denom, summed)


def body(hist_keys, hist_values, latent_queries, latent_pos, targets, out_proj, norm_gain, unembed):
    softmax_scale = HD ** (-0.5)
    seq_keys = hist_keys[0]
    seq_values = hist_values[0]
    position = lax.axis_index("seq")
    tok_rows = seq_keys.shape[0]
    channels = seq_keys.shape[1]
    head_count = channels // HD
    own_rows = latent_queries.shape[1]
    queries = lax.all_gather(latent_queries[0], "seq", axis=0, tiled=True)
    latents = queries.shape[0]
    query_heads = queries.reshape(latents, head_count, HD)
    key_heads = seq_keys.reshape(tok_rows, head_count, HD)
    value_heads = seq_values.reshape(tok_rows, head_count, HD)
    places = position * tok_rows + jnp.arange(tok_rows, dtype=jnp.int32)
    visible = (places[None, :] <= latent_pos[0][:, None])[None]
    scores = (
        jnp.einsum("ihd,jhd->hij", query_heads, key_heads, preferred_element_type=jnp.float32)
        * softmax_scale
    )
    largest = jnp.max(jnp.where(visible, scores, -1e30), axis=-1)
    weights = jnp.where(visible, jnp.exp(scores - largest[..., None]), 0.0)
    summed = jnp.sum(weights, axis=-1)
    partial_out = jnp.einsum(
        "hij,jhd->ihd",
        weights.astype(jnp.bfloat16),
        value_heads,
        preferred_element_type=jnp.float32,
    ).reshape(latents, channels)
    best, denom, combined = joined((largest.T, summed.T, partial_out), "seq", combine)
    attn_all = (combined / repeat_heads(denom)).astype(jnp.bfloat16)
    log_norm = best + jnp.log(denom)
    slab = out_proj.shape[0]
    attn_cols = lax.dynamic_slice_in_dim(attn_all, position * slab, slab, 1)
    proj_columns = lax.all_to_all(out_proj, "seq", split_axis=1, concat_axis=0, tiled=True)
    column_block = jnp.dot(attn_all, proj_columns, preferred_element_type=jnp.float32)
    hidden = lax.all_to_all(column_block, "seq", split_axis=0, concat_axis=1, tiled=True)
    inverse = lax.rsqrt(jnp.mean(hidden * hidden, axis=-1, keepdims=True) + epsilon)
    normed = (hidden * inverse * norm_gain).astype(jnp.bfloat16)
    logits = jnp.dot(normed, unembed, preferred_element_type=jnp.float32)
    log_total = jax.nn.logsumexp(logits, axis=-1, keepdims=True)
    onehot = (jnp.arange(logits.shape[1], dtype=jnp.int32)[None, :] == targets[0][:, None]).astype(
        jnp.float32
    )
    local_loss = jnp.sum(log_total[:, 0] - jnp.sum(logits * onehot, axis=-1))
    grad_logits = (loss_factor * (jnp.exp(logits - log_total) - onehot)).astype(jnp.bfloat16)
    grad_normed = lax.dot_general(
        grad_logits, unembed, (((1,), (1,)), ((), ())), preferred_element_type=jnp.float32
    )
    scaled = norm_gain * grad_normed
    grad_hidden = (
        inverse * scaled - hidden * inverse**3 * jnp.mean(hidden * scaled, axis=-1, keepdims=True)
    ).astype(jnp.bfloat16)
    grad_all = lax.all_gather(grad_hidden, "seq", axis=0, tiled=True)
    weight_part = lax.dot_general(
        attn_cols, grad_all, (((0,), (0,)), ((), ())), preferred_element_type=jnp.float32
    )
    grad_cols = lax.dot_general(
        grad_all, out_proj, (((1,), (1,)), ((), ())), preferred_element_type=jnp.float32
    ).astype(jnp.bfloat16)
    grad_attn = lax.all_gather(grad_cols, "seq", axis=1, tiled=True)
    grad_heads = grad_attn.reshape(latents, head_count, HD)
    product = grad_attn.astype(jnp.float32) * attn_all.astype(jnp.float32)
    delta = jnp.sum(product.reshape(latents, head_count, HD), axis=-1)
    probs = jnp.where(visible, jnp.exp(scores - log_norm.T[..., None]), 0.0)
    grad_probs = jnp.einsum(
        "ihd,jhd->hij", grad_heads, value_heads, preferred_element_type=jnp.float32
    )
    grad_scores = (probs * (grad_probs - delta.T[..., None])).astype(jnp.bfloat16)
    grad_values = (
        jnp.einsum(
            "hij,ihd->jhd",
            probs.astype(jnp.bfloat16),
            grad_heads,
            preferred_element_type=jnp.float32,
        )
        .reshape(tok_rows, channels)
        .astype(jnp.bfloat16)
    )
    grad_keys = (
        (
            jnp.einsum("hij,ihd->jhd", grad_scores, query_heads, preferred_element_type=jnp.float32)
            * softmax_scale
        )
        .reshape(tok_rows, channels)
        .astype(jnp.bfloat16)
    )
    terms = jnp.einsum("hij,jhd->ihd", grad_scores, key_heads, preferred_element_type=jnp.float32)
    grad_queries = lax.psum_scatter(
        (terms.reshape(lax.axis_size("seq") * own_rows, channels) * softmax_scale).astype(
            jnp.bfloat16
        ),
        "seq",
        scatter_dimension=0,
        tiled=True,
    )
    entries = channels * D
    weight_sum = lax.psum(weight_part.astype(jnp.bfloat16), "grp").astype(jnp.float32)
    loss_sum, square_sum = lax.psum((local_loss, jnp.sum(weight_sum * weight_sum)), "seq")
    proj_update = weight_sum * lax.rsqrt(square_sum / entries + epsilon)
    return (
        loss_sum.reshape(1),
        grad_queries[None],
        grad_keys[None],
        grad_values[None],
        proj_update,
    )


def solution(mesh):
    placed = (
        P("grp", "seq", None),
        P("grp", "seq", None),
        P("grp", "seq", None),
        P("grp", None),
        P("grp", "seq"),
        P("seq", None),
        P(),
        P(),
    )
    return jax.shard_map(
        body,
        mesh=mesh,
        in_specs=placed,
        out_specs=(
            P("grp"),
            P("grp", "seq", None),
            P("grp", "seq", None),
            P("grp", "seq", None),
            P("seq", None),
        ),
        check_vma=False,
    )
```

profile of v0, /device:TPU:0, one launch (start us, length us, event | category | flops | bytes accessed | tf_op | source)
XLA Modules:
  0.0 178.7 jit_solution(14543328704458842982)
XLA Ops:
  7.2 11.0 %all-gather = bf16[1,64,1024]{2,1,0:T(8,128)(2,1)S(1)} all-gather(bf16[1,8,1024]{2,1,0:T(8,128)(2,1)} %param.12), channel_id=2, replica_groups=mesh['grp'=4,'seq'=8] {'seq'}, dimensions={1}, use_global_device_ids=true | all-gather | bytes 147456 | tf_op jit(solution)/shard_map/all_gather | solution.py:47
  18.3 1.0 copy.64
  23.5 3.5 %all-to-all-start = ((bf16[128,8,256]{2,0,1:T(8,128)(2,1)}), bf16[128,8,256]{2,0,1:T(8,128)(2,1)S(1)}, u32[]{:S(2)}, u32[]{:S(2)}) async-start(bf16[128,8,256]{2,0,1:T(8,128)(2,1)} %bitcast.109), calls=%async_computation | async-start | bytes 1048576 | tf_op jit(solution)/shard_map/all_to_all | solution.py:72
  27.3 14.3 %all-gather.4 = f32[8,64,8]{1,2,0:T(8,128)S(1)} all-gather(f32[1,64,8]{1,2,0:T(8,128)S(1)} %bitcast.146), channel_id=4, replica_groups=mesh['grp'=4,'seq'=8] {'seq'}, dimensions={0}, use_global_device_ids=true | all-gather | bytes 18432 | tf_op jit(solution)/shard_map/all_gather | solution.py:15
  41.5 9.5 %all-gather.3 = f32[8,64,8]{1,2,0:T(8,128)S(1)} all-gather(f32[1,64,8]{1,2,0:T(8,128)S(1)} %bitcast.145), channel_id=3, replica_groups=mesh['grp'=4,'seq'=8] {'seq'}, dimensions={0}, use_global_device_ids=true | all-gather | bytes 18432 | tf_op jit(solution)/shard_map/all_gather | solution.py:15
  51.0 2.8 %all-gather.7.cloned.1.call-done = f32[8,64,1024]{2,1,0:T(8,128)} async-done(((f32[1,64,1024]{2,1,0:T(8,128)}), f32[8,64,1024]{2,1,0:T(8,128)}) %all-gather.7.cloned.1.call-update) | async-done | bytes 2097168 | tf_op jit(solution)/shard_map/all_gather | solution.py:15
  54.7 11.5 %while.19 = (s32[]{:T(128)}, f32[64,8]{0,1:T(8,128)S(1)}, f32[64,8]{0,1:T(8,128)S(1)}, f32[64,1024]{1,0:T(8,128)S(1)}, f32[8,64,8]{1,2,0:T(8,128)S(1)}, /*index=...) while((s32[]{:T(128)}, f32[64,8]{0,1:T(8,128)S(1)}, ...), condition=%wide.region_3.4_spmd, body=%wide.region_2.3_spmd.sunk | while | flops 199685 | bytes 1863823 | solution.py:20
  55.2 1.2 fusion.60
  56.9 1.2 fusion.60
  58.5 1.2 fusion.60
  60.1 1.2 fusion.60
  61.8 1.2 fusion.60
  63.4 1.2 fusion.60
  65.1 1.2 fusion.60
  67.4 3.4 %all-to-all-start.1 = ((f32[8,8,256]{2,1,0:T(8,128)}), f32[8,8,256]{2,1,0:T(8,128)S(1)}, u32[]{:S(2)}, u32[]{:S(2)}) async-start(f32[8,8,256]{2,1,0:T(8,128)} %fusion.21), calls=%async_computation.1 | async-start | bytes 131072 | tf_op jit(solution)/shard_map/all_to_all | solution.py:74
  70.8 4.9 %all-to-all-done.1 = f32[8,8,256]{2,1,0:T(8,128)S(1)} async-done(((f32[8,8,256]{2,1,0:T(8,128)}), f32[8,8,256]{2,1,0:T(8,128)S(1)}, u32[]{:S(2)}, u32[]{:S(2)}) %all-to-all-start.1) | async-done | bytes 65568 | tf_op jit(solution)/shard_map/all_to_all | solution.py:74
  77.6 8.3 %all_gather.30 = bf16[64,2048]{1,0:T(8,128)(2,1)S(1)} all-gather(bf16[8,2048]{1,0:T(8,128)(2,1)S(1)} %subtract_convert_fusion), channel_id=1, replica_groups=mesh['grp'=4,'seq'=8] {'seq'}, dimensions={0}, use_global_device_ids=true | all-gather | bytes 294912 | tf_op jit(solution)/shard_map/all_gather | solution.py:91
  86.3 9.0 %all_gather.31 = bf16[64,1024]{1,0:T(8,128)(2,1)S(1)} all-gather(bf16[64,128]{1,0:T(8,128)(2,1)S(1)} %convolution_convert_fusion.2), channel_id=1, replica_groups=mesh['grp'=4,'seq'=8] {'seq'}, dimensions={1}, use_global_device_ids=true | all-gather | bytes 147456 | tf_op jit(solution)/shard_map/all_gather | solution.py:98
  95.3 1.1 convolution_convert_fusion
  100.4 34.9 %all-reduce.3.cloned.1.call-done = bf16[128,2048]{1,0:T(8,128)(2,1)} async-done(((bf16[128,2048]{1,0:T(8,128)(2,1)}), bf16[128,2048]{1,0:T(8,128)(2,1)}) %all-reduce.3.cloned.1.call-update) | async-done | bytes 524304 | tf_op jit(solution)/shard_map/psum | solution.py:135
  135.2 1.9 %fusion.8 = f32[]{:T(128)} fusion(bf16[128,2048]{1,0:T(8,128)(2,1)} %all-reduce.3.cloned.1.call-done), kind=kLoop, calls=%fused_computation.25 | loop fusion | flops 786431 | bytes 524292 | tf_op jit(solution)/shard_map/reduce_sum | solution.py:136
  137.1 13.3 %all-reduce = (f32[1]{0:T(128)}, f32[]{:T(128)}) all-reduce(f32[1]{0:T(128)} %bitcast.19, f32[]{:T(128)} %fusion.8), channel_id=1, replica_groups=mesh['grp'=4,'seq'=8] {'seq'}, use_global_device_ids=true, to_apply=%region_9.10 | all-reduce | flops 2 | bytes 16 | tf_op jit(solution)/shard_map/psum | solution.py:136
  151.2 2.1 %convert_multiply_fusion = f32[128,2048]{1,0:T(8,128)} fusion(bf16[128,2048]{1,0:T(8,128)(2,1)} %all-reduce.3.cloned.1.call-done, f32[]{:T(128)S(6)} %rsqrt.15), kind=kLoop, calls=%fused_computation.11 | loop fusion | flops 524288 | bytes 1572868 | tf_op jit(solution)/shard_map/mul | solution.py:137
  153.3 18.9 %reduce-scatter.2.cloned.1.call-done = bf16[8,1024]{1,0:T(8,128)(2,1)} async-done(((bf16[64,1024]{1,0:T(8,128)(2,1)}), bf16[8,1024]{1,0:T(8,128)(2,1)}) %reduce-scatter.2.cloned.1.call-update) | async-done | bytes 16400 | tf_op jit(solution)/shard_map/reduce_scatter | solution.py:126
  (89 shorter events, 15.6 us)
Async XLA Ops:
  7.2 68.7 %copy-start = (bf16[2048,128]{1,0:T(8,128)(2,1)S(1)}, bf16[2048,128]{1,0:T(8,128)(2,1)}, u32[]{:S(2)}) copy-start(bf16[2048,128]{1,0:T(8,128)(2,1)} %param.17) | copy-start | bytes 1572868
  7.2 46.6 %all-gather.7.cloned.1.call-start = ((), (), s32[]{:S(2)}) async-start(), calls=%async_computation.3 | async-start | bytes 2359296 | tf_op jit(solution)/shard_map/all_gather | solution.py:15
  18.2 4.4 %copy-start.1 = (bf16[128,2048]{1,0:T(8,128)(2,1)S(1)}, bf16[128,2048]{1,0:T(8,128)(2,1)}, u32[]{:S(2)}) copy-start(bf16[128,2048]{1,0:T(8,128)(2,1)} %param.15) | copy-start | bytes 1572868
  23.5 43.1 %all-to-all-start = ((bf16[128,8,256]{2,0,1:T(8,128)(2,1)}), bf16[128,8,256]{2,0,1:T(8,128)(2,1)S(1)}, u32[]{:S(2)}, u32[]{:S(2)}) async-start(bf16[128,8,256]{2,0,1:T(8,128)(2,1)} %bitcast.109), calls=%async_computation | async-start | bytes 1048576 | tf_op jit(solution)/shard_map/all_to_all | solution.py:72
  54.7 21.2 %copy-start.2 = (f32[2048]{0:T(1024)S(1)}, f32[2048]{0:T(1024)}, u32[]{:S(2)}) copy-start(f32[2048]{0:T(1024)} %param.16) | copy-start | bytes 24580
  66.3 10.0 %copy-start.3 = (s32[1,8]{1,0:T(1,128)S(1)}, s32[1,8]{1,0:T(1,128)}, u32[]{:S(2)}) copy-start(s32[1,8]{1,0:T(1,128)} %param.14) | copy-start | bytes 100
  67.4 8.3 %all-to-all-start.1 = ((f32[8,8,256]{2,1,0:T(8,128)}), f32[8,8,256]{2,1,0:T(8,128)S(1)}, u32[]{:S(2)}, u32[]{:S(2)}) async-start(f32[8,8,256]{2,1,0:T(8,128)} %fusion.21), calls=%async_computation.1 | async-start | bytes 131072 | tf_op jit(solution)/shard_map/all_to_all | solution.py:74
  70.8 64.4 %all-reduce.3.cloned.1.call-start = ((), (), s32[]{:S(2)}) async-start(), calls=%async_computation.5 | async-start | bytes 1048576 | tf_op jit(solution)/shard_map/psum | solution.py:135
  96.4 75.8 %reduce-scatter.2.cloned.1.call-start = ((), (), s32[]{:S(2)}) async-start(), calls=%async_computation.4 | async-start | bytes 147456 | tf_op jit(solution)/shard_map/reduce_scatter | solution.py:126
Sparse Core Ops, SparseCore 0:
  22.8 30.9 all-gather.6
  96.5 38.6 all-reduce.2
  138.8 33.3 reduce-scatter.1
where the time goes:
time: 180 us; the launch traced here: 179 us
  blocking collectives  65.4 us (36%)
  waiting for transfers between devices  61.5 us (34%)
  other arithmetic  14.7 us (8%)
  between operations  14.7 us (8%)
  local copies, waits for them, and re-layouts  10.4 us (6%)
  starting transfers between devices  6.97 us (4%)
  matrix products  4.78 us (3%)
    psum x1, waiting for transfers between devices, body(): lax.psum(weight_part.astype(jnp.bfloat16), 'grp').astype(jnp.float32)  34.9 us
    all_gather x2, blocking collectives, joined(): gathered = jax.tree.map(lambda a: lax.all_gather(a, axis), part)  23.7 us
    reduce_scatter x1, waiting for transfers between devices, body(): lax.psum_scatter((terms.reshape(lax.axis_size('seq') * own_rows, channels...  18.9 us
    psum x1, blocking collectives, body(): lax.psum((local_loss, jnp.sum(weight_sum * weight_sum)), 'seq')  13.3 us
    all_gather x1, blocking collectives, body(): queries = lax.all_gather(latent_queries[0], 'seq', axis=0, tiled=True)  11 us
    all_gather x1, blocking collectives, body(): grad_attn = lax.all_gather(grad_cols, 'seq', axis=1, tiled=True)  9.03 us
    all_gather x1, blocking collectives, body(): grad_all = lax.all_gather(grad_hidden, 'seq', axis=0, tiled=True)  8.34 us
    add x7, other arithmetic, combine(): earlier[2] * repeat_heads(factor_one) + later[2] * repeat_heads(factor_two)  8.21 us
  transfers between devices with their start and end apart: 5, of which 4 were waited for; matrix products, arithmetic and copies ran while one was open for 12% of the time, Pallas kernels for 0%

commit v1 on v0

--- a/solution.py
+++ b/solution.py
@@ -1,6 +1,10 @@
+from functools import partial
+
 import jax
 import jax.numpy as jnp
 from jax import lax
+from jax.experimental import pallas as pl
+from jax.experimental.pallas import tpu as pltpu
 from jax.sharding import PartitionSpec as P
 
 D = 2048
@@ -35,7 +39,7 @@
     return (best, denom, summed)
 
 
-def body(hist_keys, hist_values, latent_queries, latent_pos, targets, out_proj, norm_gain, unembed):
+def general_body(hist_keys, hist_values, latent_queries, latent_pos, targets, out_proj, norm_gain, unembed):
     softmax_scale = HD ** (-0.5)
     seq_keys = hist_keys[0]
     seq_values = hist_values[0]
@@ -144,6 +148,286 @@
     )
 
 
+VMEM = pl.BlockSpec(memory_space=pltpu.VMEM)
+SMEM = pl.BlockSpec(memory_space=pltpu.SMEM)
+ROWS_T = (((1,), (1,)), ((), ()))
+COLS_T = (((0,), (0,)), ((), ()))
+
+
+def matmul(one, two, dims=(((1,), (0,)), ((), ()))):
+    return lax.dot_general(one, two, dims, preferred_element_type=jnp.float32)
+
+
+def kernel_call(kernel, name, in_specs, outs, scratch=()):
+    return pl.pallas_call(
+        kernel,
+        name=name,
+        in_specs=in_specs,
+        out_specs=[VMEM] * len(outs),
+        out_shape=[jax.ShapeDtypeStruct(shape, dtype) for shape, dtype in outs],
+        scratch_shapes=list(scratch),
+    )
+
+
+def pack_kernel(targets, keys, values, queries, packed):
+    heads = packed.shape[0]
+    tok = keys.shape[0]
+    own = queries.shape[0]
+    lanes = lax.broadcasted_iota(jnp.int32, (own, HD), 1)
+    rows = lax.broadcasted_iota(jnp.int32, (own, HD), 0)
+    wanted = jnp.zeros((own, HD), jnp.int32)
+    for row in range(own):
+        wanted = jnp.where(rows == row, targets[0, row], wanted)
+    onehot = (lanes == wanted).astype(jnp.float32)
+    for head in range(heads):
+        cols = slice(head * HD, (head + 1) * HD)
+        packed[head, 0:tok, :] = keys[:, cols]
+        packed[head, tok : 2 * tok, :] = values[:, cols]
+        tail = jnp.concatenate([queries[:, cols].astype(jnp.float32), onehot], axis=0)
+        packed[head, 2 * tok : 2 * tok + 2 * own, :] = tail.astype(jnp.bfloat16)
+
+
+def split_packed(packed, tok, own):
+    heads = packed.shape[0]
+    keys = packed[:, 0:tok, :].reshape(heads * tok, HD)
+    values = packed[:, tok : 2 * tok, :].reshape(heads * tok, HD)
+    queries = packed[:, 2 * tok : 2 * tok + own, :].astype(jnp.float32).reshape(heads * own, HD)
+    return keys, values, queries.astype(jnp.bfloat16)
+
+
+def visible_scores(keys, queries, positions):
+    latents = queries.shape[0]
+    length = keys.shape[0]
+    diagonal = lax.broadcasted_iota(jnp.int32, (latents, latents), 0) == lax.broadcasted_iota(
+        jnp.int32, (latents, latents), 1
+    )
+    last = jnp.sum(
+        jnp.where(diagonal, positions[...].astype(jnp.float32), 0.0), axis=1, keepdims=True
+    )
+    places = lax.broadcasted_iota(jnp.int32, (latents, length), 1).astype(jnp.float32)
+    scores = matmul(queries, keys, ROWS_T) * HD ** (-0.5)
+    return scores, places <= last
+
+
+def forward_kernel(side, positions, packed, out_proj, attn, log_norm, onehot, kept, sent, *, tok, own):
+    keys, values, queries = split_packed(packed, tok, own)
+    scores, visible = visible_scores(keys, queries, positions)
+    best = jnp.max(jnp.where(visible, scores, -1e30), axis=-1, keepdims=True)
+    weights = jnp.where(visible, jnp.exp(scores - best), 0.0)
+    denom = jnp.sum(weights, axis=-1, keepdims=True)
+    summed = matmul(weights.astype(jnp.bfloat16), values)
+    attn[...] = (summed / denom).astype(jnp.bfloat16)
+    log_norm[...] = jnp.broadcast_to(best + jnp.log(denom), log_norm.shape)
+    half = kept.shape[0]
+    mine = side[0]
+    pieces = half // own
+    onehot[...] = (
+        packed[pl.ds(mine * pieces, pieces), 2 * tok + own : 2 * tok + 2 * own, :]
+        .astype(jnp.float32)
+        .reshape(half, HD)
+    )
+    proj = out_proj[...]
+    kept[...] = matmul(attn[pl.ds(pl.multiple_of(mine * half, half), half), :], proj)
+    sent[...] = matmul(attn[pl.ds(pl.multiple_of((1 - mine) * half, half), half), :], proj).astype(
+        sent.dtype
+    )
+
+
+def loss_kernel(parts, gain, unembed, onehot_ref, attn, message, stats):
+    half = parts.shape[1]
+    hidden = parts[0].astype(jnp.float32)
+    for part in range(1, parts.shape[0]):
+        hidden = hidden + parts[part].astype(jnp.float32)
+    onehot = onehot_ref[...]
+    inverse = lax.rsqrt(jnp.mean(hidden * hidden, axis=-1, keepdims=True) + epsilon)
+    normed = (hidden * inverse * gain[...]).astype(jnp.bfloat16)
+    logits = matmul(normed, unembed[...])
+    top = jnp.max(logits, axis=-1, keepdims=True)
+    log_total = top + jnp.log(jnp.sum(jnp.exp(logits - top), axis=-1, keepdims=True))
+    losses = log_total - jnp.sum(logits * onehot, axis=-1, keepdims=True)
+    stats[...] = jnp.broadcast_to(jnp.sum(losses, axis=0, keepdims=True), stats.shape)
+    grad_logits = (loss_factor * (jnp.exp(logits - log_total) - onehot)).astype(jnp.bfloat16)
+    scaled = gain[...] * matmul(grad_logits, unembed[...], ROWS_T)
+    mean = jnp.mean(hidden * scaled, axis=-1, keepdims=True)
+    grad_hidden = (inverse * scaled - hidden * (inverse * inverse * inverse) * mean).astype(
+        jnp.bfloat16
+    )
+    blocks = hidden.shape[1] // HD
+    for block in range(blocks):
+        message[block * half : (block + 1) * half, :] = grad_hidden[:, block * HD : (block + 1) * HD]
+    message[blocks * half :, :] = attn[...]
+
+
+def fill_rows(target, row, message, half):
+    for block in range(target.shape[1] // HD):
+        target[pl.ds(row, half), block * HD : (block + 1) * HD] = message[
+            block * half : (block + 1) * half, :
+        ]
+
+
+def backward_kernel(
+    side, positions, packed, out_proj, attn, log_norm, own_msg, pair_msg, grads, grad_hidden, *, tok, own
+):
+    half = grad_hidden.shape[0] // 2
+    mine = side[0]
+    fill_rows(grad_hidden, pl.multiple_of(mine * half, half), own_msg, half)
+    fill_rows(grad_hidden, pl.multiple_of((1 - mine) * half, half), pair_msg, half)
+    keys, values, queries = split_packed(packed, tok, own)
+    scores, visible = visible_scores(keys, queries, positions)
+    heads = packed.shape[0]
+    grad_attn = matmul(grad_hidden[...], out_proj[...], ROWS_T).astype(jnp.bfloat16)
+    delta = jnp.sum(
+        grad_attn.astype(jnp.float32) * attn[...].astype(jnp.float32), axis=-1, keepdims=True
+    )
+    probs = jnp.where(visible, jnp.exp(scores - log_norm[:, 0:1]), 0.0)
+    grad_probs = matmul(grad_attn, values, ROWS_T)
+    grad_scores = (probs * (grad_probs - delta)).astype(jnp.bfloat16)
+    grad_values = matmul(probs.astype(jnp.bfloat16), grad_attn, COLS_T).astype(jnp.bfloat16)
+    scale = HD ** (-0.5)
+    grad_keys = (matmul(grad_scores, queries, COLS_T) * scale).astype(jnp.bfloat16)
+    grad_queries = matmul(grad_scores, keys) * scale
+    grads[:, 0:tok, :] = grad_keys.reshape(heads, tok, HD)
+    grads[:, tok : 2 * tok, :] = grad_values.reshape(heads, tok, HD)
+    tail = grad_queries.reshape(heads, own, HD)
+    grads[:, 2 * tok : 2 * tok + 2 * own, :] = jnp.concatenate([tail, tail], axis=1).astype(
+        jnp.bfloat16
+    )
+
+
+def unpack_kernel(packed, grad_queries, grad_keys, grad_values):
+    heads = packed.shape[0]
+    tok = grad_keys.shape[0]
+    own = grad_queries.shape[0]
+    for head in range(heads):
+        cols = slice(head * HD, (head + 1) * HD)
+        grad_keys[:, cols] = packed[head, 0:tok, :]
+        grad_values[:, cols] = packed[head, tok : 2 * tok, :]
+        grad_queries[:, cols] = packed[head, 2 * tok : 2 * tok + own, :]
+
+
+def weight_kernel(side, *refs, count):
+    messages = refs[: 2 * count]
+    loss, weights, stats, attn_rows, grad_rows = refs[2 * count :]
+    half = grad_rows.shape[0] // (2 * count)
+    blocks = grad_rows.shape[1] // HD
+    mine = side[0]
+    for index in range(count):
+        attn_at = blocks * half
+        for place, message, part in (
+            (0, messages[index], mine),
+            (1, messages[count + index], 1 - mine),
+        ):
+            row = (2 * index + place) * half
+            for block in range(blocks):
+                grad_rows[row : row + half, block * HD : (block + 1) * HD] = message[
+                    block * half : (block + 1) * half, :
+                ]
+            attn_rows[row : row + half, :] = messages[index][
+                pl.ds(pl.multiple_of(attn_at + part * half, half), half), :
+            ]
+    total = matmul(attn_rows[...], grad_rows[...], COLS_T)
+    weights[...] = total
+    squares = jnp.sum(jnp.sum(total * total, axis=0, keepdims=True), axis=1, keepdims=True)
+    lanes = lax.broadcasted_iota(jnp.int32, stats.shape, 1)
+    stats[...] = jnp.where(lanes < HD // 2, squares, loss[...])
+
+
+def body(hist_keys, hist_values, latent_queries, latent_pos, targets, out_proj, norm_gain, unembed):
+    n_seq = lax.axis_size("seq")
+    n_grp = lax.axis_size("grp")
+    seq_keys = hist_keys[0]
+    tok, channels = seq_keys.shape
+    own = latent_queries.shape[1]
+    latents = n_seq * own
+    heads = channels // HD
+    vocab = unembed.shape[1]
+    if not (
+        heads == n_seq
+        and out_proj.shape[0] == HD
+        and vocab == HD
+        and tok % 16 == 0
+        and own == 8
+        and n_seq % 2 == 0
+    ):
+        return general_body(
+            hist_keys, hist_values, latent_queries, latent_pos, targets, out_proj, norm_gain, unembed
+        )
+    bf16, f32 = jnp.bfloat16, jnp.float32
+    half = latents // 2
+    width = out_proj.shape[1]
+    span = 2 * tok + 2 * own
+    side = (lax.axis_index("seq") % 2).reshape(1)
+    swap = [(i, i ^ 1) for i in range(n_seq)]
+    sides = [[i for i in range(n_seq) if i % 2 == k] for k in range(2)]
+
+    (packed,) = kernel_call(
+        pack_kernel, "pack", [SMEM, VMEM, VMEM, VMEM], [((heads, span, HD), bf16)]
+    )(targets, seq_keys, hist_values[0], latent_queries[0])
+    packed = lax.all_to_all(packed, "seq", 0, 0)
+
+    attn, log_norm, onehot, kept, sent = kernel_call(
+        partial(forward_kernel, tok=tok, own=own),
+        "forward",
+        [SMEM, VMEM, VMEM, VMEM],
+        [
+            ((latents, HD), bf16),
+            ((latents, HD), f32),
+            ((half, HD), f32),
+            ((half, width), f32),
+            ((half, width), bf16),
+        ],
+    )(side, latent_pos, packed, out_proj)
+    pair_sum = (kept + lax.ppermute(sent, "seq", swap).astype(f32)).astype(bf16)
+    parts = lax.all_gather(pair_sum, "seq", axis_index_groups=sides)
+    message, loss = kernel_call(
+        loss_kernel,
+        "loss",
+        [VMEM] * 5,
+        [((width // HD * half + latents, HD), bf16), ((1, HD), f32)],
+    )(parts, norm_gain.reshape(1, width), unembed, onehot, attn)
+    pair_msg = lax.ppermute(message, "seq", swap)
+    others = [
+        lax.ppermute(message, "grp", [(i, (i + step) % n_grp) for i in range(n_grp)])
+        for step in range(1, n_grp)
+    ]
+    (grads,) = kernel_call(
+        partial(backward_kernel, tok=tok, own=own),
+        "backward",
+        [SMEM] + [VMEM] * 7,
+        [((heads, span, HD), bf16)],
+        [pltpu.VMEM((latents, width), bf16)],
+    )(side, latent_pos, packed, out_proj, attn, log_norm, message, pair_msg)
+    grads = lax.all_to_all(grads, "seq", 0, 0)
+    pair_others = [lax.ppermute(other, "seq", swap) for other in others]
+    weights, stats = kernel_call(
+        partial(weight_kernel, count=n_grp),
+        "weights",
+        [SMEM] + [VMEM] * (2 * n_grp + 1),
+        [((channels // n_seq, width), f32), ((1, HD), f32)],
+        [
+            pltpu.VMEM((n_grp * latents, HD), bf16),
+            pltpu.VMEM((n_grp * latents, width), bf16),
+        ],
+    )(side, message, *others, pair_msg, *pair_others, loss)
+    grad_queries, grad_keys, grad_values = kernel_call(
+        unpack_kernel,
+        "unpack",
+        [VMEM],
+        [((own, channels), bf16), ((tok, channels), bf16), ((tok, channels), bf16)],
+    )(grads)
+    gathered = lax.all_gather(stats, "seq", axis=0, tiled=True)
+    totals = jnp.sum(gathered, axis=0)
+    loss_sum = totals[HD - 1] / (n_seq // 2)
+    proj_update = weights * lax.rsqrt(totals[0] / (channels * width) + epsilon)
+    return (
+        loss_sum.reshape(1),
+        grad_queries[None],
+        grad_keys[None],
+        grad_values[None],
+        proj_update,
+    )
+
+
 def solution(mesh):
     placed = (
         P("grp", "seq", None),

time: 180 us -> 82.6 us (0.46)
  blocking collectives: 65.4 us -> 19.4 us
  waiting for transfers between devices: 61.5 us -> 22.9 us
  Pallas kernels: 0 us -> 15.1 us
  between operations: 14.7 us -> 3.2 us
  other arithmetic: 14.7 us -> 3.3 us
  starting transfers between devices: 6.97 us -> 13.9 us
  local copies, waits for them, and re-layouts: 10.4 us -> 4.25 us
  matrix products: 4.78 us -> 0 us
    psum x1 -> x0, waiting for transfers between devices: 34.9 us -> none  [body(): lax.psum(weight_part.astype(jnp.bfloat16), 'grp').astype(jnp.float32)]
    all_gather x5 -> x2, blocking collectives: 52.1 us -> 19.4 us  [the longest x1 10.2 us: body(): parts = lax.all_gather(pair_sum, 'seq', axis_index_groups=sides)]
    reduce_scatter x1 -> x0, waiting for transfers between devices: 18.9 us -> none  [body(): lax.psum_scatter((terms.reshape(lax.axis_size('seq') * own_rows, channels...]
    pallas_call x0 -> x6, Pallas kernels: none -> 15.1 us  [the longest x1 3.06 us: body(): kernel_call(partial(backward_kernel, tok=tok, own=own), 'backward', [SMEM...]
    psum x1 -> x0, blocking collectives: 13.3 us -> none  [body(): lax.psum((local_loss, jnp.sum(weight_sum * weight_sum)), 'seq')]
    ppermute x0 -> x8, waiting for transfers between devices: none -> 12.8 us  [the longest x3 11.2 us: body(): lax.ppermute(message, 'grp', [(i, (i + step) % n_grp) for i in range(n_gr...]
    add x15 -> x0, other arithmetic: 8.33 us -> none  [the longest x7 8.21 us: combine(): earlier[2] * repeat_heads(factor_one) + later[2] * repeat_heads(factor_two)]
    all_to_all x2, waiting for transfers between devices: 4.89 us -> 10.1 us  [the longest x1 10.1 us: body(): packed = lax.all_to_all(packed, 'seq', 0, 0)]
  transfers between devices with their start and end apart: 5 -> 10, of which waited for: 4 -> 4; matrix products, arithmetic and copies ran while one was open for 12% -> 4% of each run, Pallas kernels for 0% -> 7%
where the time goes in v1:
time: 82.6 us; the launch traced here: 82 us
  waiting for transfers between devices  22.9 us (28%)
  blocking collectives  19.4 us (23%)
  Pallas kernels  15.1 us (18%)
  starting transfers between devices  13.9 us (17%)
  local copies, waits for them, and re-layouts  4.25 us (5%)
  other arithmetic  3.3 us (4%)
  between operations  3.2 us (4%)
    ppermute x3, waiting for transfers between devices, body(): lax.ppermute(message, 'grp', [(i, (i + step) % n_grp) for i in range(n_gr...  11.2 us
    all_gather x1, blocking collectives, body(): parts = lax.all_gather(pair_sum, 'seq', axis_index_groups=sides)  10.2 us
    all_to_all x1, waiting for transfers between devices, body(): packed = lax.all_to_all(packed, 'seq', 0, 0)  10.1 us
    all_gather x1, blocking collectives, body(): gathered = lax.all_gather(stats, 'seq', axis=0, tiled=True)  9.2 us
    all_to_all x1, starting transfers between devices, body(): packed = lax.all_to_all(packed, 'seq', 0, 0)  5.2 us
    ppermute x3, starting transfers between devices, body(): lax.ppermute(message, 'grp', [(i, (i + step) % n_grp) for i in range(n_gr...  4.62 us
    unnamed x20, local copies, waits for them, and re-layouts  3.67 us
    all_to_all x1, starting transfers between devices, body(): grads = lax.all_to_all(grads, 'seq', 0, 0)  3.55 us
  transfers between devices with their start and end apart: 10, of which 4 were waited for; matrix products, arithmetic and copies ran while one was open for 4% of the time, Pallas kernels for 7%

profile of v1, /device:TPU:0, one launch (start us, length us, event | category | flops | bytes accessed | tf_op | source)
XLA Modules:
  0.0 82.0 jit_solution(10828885445945758633)
XLA Ops:
  0.6 1.9 %pack.1 = bf16[8,272,128]{2,1,0:T(8,128)(2,1)} custom-call(s32[1,8]{1,0:T(1,128)} %targets.1, bf16[128,1024]{1,0:T(8,128)(2,1)} %bitcast.12, bf16[128,1024]{1,0:T(8,128)(2,1)} %bitcast.13, bf16[8,1024]{1,0:T(8,128)(2,1)} %bitcast.14), custom_call_target="tpu_custom_call" | custom-call | tf_op jit(solution)/shard_map/pack/pallas_call | solution.py:363
  2.6 5.2 %all-to-all-start = ((bf16[8,272,128]{2,1,0:T(8,128)(2,1)}), bf16[8,272,128]{2,1,0:T(8,128)(2,1)S(1)}, u32[]{:S(2)}, u32[]{:S(2)}) async-start(bf16[8,272,128]{2,1,0:T(8,128)(2,1)} %pack.1), calls=%async_computation | async-start | bytes 1114112 | tf_op jit(solution)/shard_map/all_to_all | solution.py:366
  7.8 10.1 %all-to-all-done.packed = bf16[8,272,128]{2,1,0:T(8,128)(2,1)S(1)} async-done(((bf16[8,272,128]{2,1,0:T(8,128)(2,1)}), bf16[8,272,128]{2,1,0:T(8,128)(2,1)S(1)}, u32[]{:S(2)}, u32[]{:S(2)}) %all-to-all-start) | async-done | bytes 557088 | tf_op jit(solution)/shard_map/all_to_all | solution.py:366
  17.8 0.8 copy-done
  18.6 2.6 %forward.1 = (bf16[64,128]{1,0:T(8,128)(2,1)}, f32[64,128]{1,0:T(8,128)}, f32[32,128]{1,0:T(8,128)}, f32[32,2048]{1,0:T(8,128)}, bf16[32,2048]{1,0:T(8,128)(2,1)}) custom-call(s32[1]{0:T(128)} %bitcast.side, s32[1,64]{1,0:T(1,128)} %positions.3, bf16[8,272,128]{2,1,0:T(8,128)(2,1)} %copy-done, bf16[128,2048]{1,0:T(8,128)(2,1)} %out_proj.3), custom_call_target="tpu_custom_call" | custom-call | tf_op jit(solution)/shard_map/forward/pallas_call | solution.py:368
  21.3 1.6 %collective-permute-done = bf16[32,2048]{1,0:T(8,128)(2,1)S(1)} collective-permute-done((bf16[32,2048]{1,0:T(8,128)(2,1)}, bf16[32,2048]{1,0:T(8,128)(2,1)S(1)}, u32[]{:S(2)}, u32[]{:S(2)}) %collective-permute-start) | collective-permute-done | bytes 131104 | tf_op jit(solution)/shard_map/ppermute | solution.py:380
  22.8 1.0 %add_convert_fusion = bf16[32,2048]{1,0:T(8,128)(2,1)S(1)} fusion(f32[32,2048]{1,0:T(8,128)} %get-tuple-element.17, bf16[32,2048]{1,0:T(8,128)(2,1)S(1)} %collective-permute-done), kind=kLoop, calls=%fused_computation.1 | loop fusion | flops 196608 | bytes 524288 | tf_op jit(solution)/shard_map/convert_element_type | solution.py:380
  23.8 10.2 %all-gather = bf16[128,2048]{1,0:T(8,128)(2,1)} all-gather(bf16[32,2048]{1,0:T(8,128)(2,1)S(1)} %add_convert_fusion), channel_id=2, replica_groups={{0,2,4,6},{1,3,5,7},{8,10,12,14},{9,11,13,15},{16,18,20,22},{17,19,21,2..., dimensions={0}, use_global_device_ids=true | all-gather | bytes 655360 | tf_op jit(solution)/shard_map/all_gather | solution.py:381
  34.0 2.8 %loss.1 = (bf16[576,128]{1,0:T(8,128)(2,1)}, f32[1,128]{1,0:T(1,128)}) custom-call(bf16[4,32,2048]{2,1,0:T(8,128)(2,1)} %bitcast.11, f32[1,2048]{1,0:T(1,128)} %bitcast.15, bf16[2048,128]{1,0:T(8,128)(2,1)} %unembed.1, f32[32,128]{1,0:T(8,128)} %get-tuple-element.19.onehot_ref, bf16[64,128]{1,0:T(8,128)(2,1)} %get-tuple-element.20.attn), custom_call_target="tpu_custom_call" | custom-call | tf_op jit(solution)/shard_map/loss/pallas_call | solution.py:382
  36.8 3.6 %collective-permute-start.3 = (bf16[576,128]{1,0:T(8,128)(2,1)}, bf16[576,128]{1,0:T(8,128)(2,1)S(1)}, u32[]{:S(2)}, u32[]{:S(2)}) collective-permute-start(bf16[576,128]{1,0:T(8,128)(2,1)} %get-tuple-element.21.refs_0_.own_msg), channel_id=1, source_target_pairs={{0,24},{8,0},{16,8},{24,16},{1,25},{9,1},{17,9},{25,17},{2,26},{10... | collective-permute-start | bytes 442376 | tf_op jit(solution)/shard_map/ppermute | solution.py:390
  40.4 1.0 %collective-permute-start.1 = (bf16[576,128]{1,0:T(8,128)(2,1)}, bf16[576,128]{1,0:T(8,128)(2,1)S(1)}, u32[]{:S(2)}, u32[]{:S(2)}) collective-permute-start(bf16[576,128]{1,0:T(8,128)(2,1)} %get-tuple-element.21.refs_0_.own_msg), channel_id=1, source_target_pairs={{0,8},{8,16},{16,24},{24,0},{1,9},{9,17},{17,25},{25,1},{2,10},{10... | collective-permute-start | bytes 442376 | tf_op jit(solution)/shard_map/ppermute | solution.py:390
  41.4 3.5 %collective-permute-done.3.refs_3_ = bf16[576,128]{1,0:T(8,128)(2,1)S(1)} collective-permute-done((bf16[576,128]{1,0:T(8,128)(2,1)}, bf16[576,128]{1,0:T(8,128)(2,1)S(1)}, u32[]{:S(2)}, u32[]{:S(2)}) %collective-permute-start.3) | collective-permute-done | bytes 147488 | tf_op jit(solution)/shard_map/ppermute | solution.py:390
  45.0 7.7 %collective-permute-done.2.refs_2_ = bf16[576,128]{1,0:T(8,128)(2,1)S(1)} collective-permute-done((bf16[576,128]{1,0:T(8,128)(2,1)}, bf16[576,128]{1,0:T(8,128)(2,1)S(1)}, u32[]{:S(2)}, u32[]{:S(2)}) %collective-permute-start.2) | collective-permute-done | bytes 147488 | tf_op jit(solution)/shard_map/ppermute | solution.py:390
  53.2 0.6 copy-done.2
  53.8 3.1 %backward.1 = bf16[8,272,128]{2,1,0:T(8,128)(2,1)} custom-call(s32[1]{0:T(128)} %bitcast.side, s32[1,64]{1,0:T(1,128)} %positions.3, bf16[8,272,128]{2,1,0:T(8,128)(2,1)} %copy-done, bf16[128,2048]{1,0:T(8,128)(2,1)} %out_proj.3, bf16[64,128]{1,0:T(8,128)(2,1)} %get-tuple-element.20.attn, f32[64,128]{1,0:T(8,128)} %get-tuple-element.24.log_norm, ...), custom_call_target="tpu_custom_call" | custom-call | tf_op jit(solution)/shard_map/backward/pallas_call | solution.py:393
  56.9 3.5 %all-to-all-start.1 = ((bf16[8,272,128]{2,1,0:T(8,128)(2,1)}), bf16[8,272,128]{2,1,0:T(8,128)(2,1)S(1)}, u32[]{:S(2)}, u32[]{:S(2)}) async-start(bf16[8,272,128]{2,1,0:T(8,128)(2,1)} %backward.1), calls=%async_computation.1 | async-start | bytes 1114112 | tf_op jit(solution)/shard_map/all_to_all | solution.py:400
  60.5 0.6 copy-done.6
  61.3 2.7 %weights.1 = (f32[128,2048]{1,0:T(8,128)}, f32[1,128]{1,0:T(1,128)}) custom-call(s32[1]{0:T(128)} %bitcast.side, bf16[576,128]{1,0:T(8,128)(2,1)} %get-tuple-element.21.refs_0_.own_msg, bf16[576,128]{1,0:T(8,128)(2,1)} %copy-done.5, bf16[576,128]{1,0:T(8,128)(2,1)} %copy-done.4, bf16[576,128]{1,0:T(8,128)(2,1)} %copy-done.3, bf16[576,128]{1,0:T(8,128)(2,1)} %copy-done.2, ...), custom_call_target="tpu_custom_call" | custom-call | tf_op jit(solution)/shard_map/weights/pallas_call | solution.py:402
  64.0 0.7 copy-done.9
  64.7 9.2 %all-gather.1 = f32[8,1,128]{2,1,0:T(1,128)S(1)} all-gather(f32[1,1,128]{2,1,0:T(1,128)S(1)} %bitcast.16), channel_id=1, replica_groups=mesh['grp'=4,'seq'=8] {'seq'}, dimensions={0}, use_global_device_ids=true | all-gather | bytes 4608 | tf_op jit(solution)/shard_map/all_gather | solution.py:418
  73.9 0.6 fusion
  75.8 2.3 %broadcast_multiply_fusion = f32[128,2048]{1,0:T(8,128)} fusion(f32[128,2048]{1,0:T(8,128)} %get-tuple-element.28, f32[]{:T(128)} %bitcast.10), kind=kLoop, calls=%fused_computation | loop fusion | flops 262144 | bytes 2097156 | tf_op jit(solution)/shard_map/mul | solution.py:421
  78.1 0.8 copy-done.1
  78.9 2.0 %unpack.1 = (bf16[8,1024]{1,0:T(8,128)(2,1)}, bf16[128,1024]{1,0:T(8,128)(2,1)}, bf16[128,1024]{1,0:T(8,128)(2,1)}) custom-call(bf16[8,272,128]{2,1,0:T(8,128)(2,1)} %copy-done.1), custom_call_target="tpu_custom_call" | custom-call | tf_op jit(solution)/shard_map/unpack/pallas_call | solution.py:412
  (28 shorter events, 0.7 us)
Async XLA Ops:
  2.6 15.3 %all-to-all-start = ((bf16[8,272,128]{2,1,0:T(8,128)(2,1)}), bf16[8,272,128]{2,1,0:T(8,128)(2,1)S(1)}, u32[]{:S(2)}, u32[]{:S(2)}) async-start(bf16[8,272,128]{2,1,0:T(8,128)(2,1)} %pack.1), calls=%async_computation | async-start | bytes 1114112 | tf_op jit(solution)/shard_map/all_to_all | solution.py:366
  17.8 0.8 copy-start
  21.3 1.6 %collective-permute-start = (bf16[32,2048]{1,0:T(8,128)(2,1)}, bf16[32,2048]{1,0:T(8,128)(2,1)S(1)}, u32[]{:S(2)}, u32[]{:S(2)}) collective-permute-start(bf16[32,2048]{1,0:T(8,128)(2,1)} %get-tuple-element.18), channel_id=1, source_target_pairs={{0,1},{1,0},{2,3},{3,2},{4,5},{5,4},{6,7},{7,6},{8,9},{9,8},{10,11... | collective-permute-start | bytes 393224 | tf_op jit(solution)/shard_map/ppermute | solution.py:380
  36.8 8.2 %collective-permute-start.3 = (bf16[576,128]{1,0:T(8,128)(2,1)}, bf16[576,128]{1,0:T(8,128)(2,1)S(1)}, u32[]{:S(2)}, u32[]{:S(2)}) collective-permute-start(bf16[576,128]{1,0:T(8,128)(2,1)} %get-tuple-element.21.refs_0_.own_msg), channel_id=1, source_target_pairs={{0,24},{8,0},{16,8},{24,16},{1,25},{9,1},{17,9},{25,17},{2,26},{10... | collective-permute-start | bytes 442376 | tf_op jit(solution)/shard_map/ppermute | solution.py:390
  40.4 12.2 %collective-permute-start.2 = (bf16[576,128]{1,0:T(8,128)(2,1)}, bf16[576,128]{1,0:T(8,128)(2,1)S(1)}, u32[]{:S(2)}, u32[]{:S(2)}) collective-permute-start(bf16[576,128]{1,0:T(8,128)(2,1)} %get-tuple-element.21.refs_0_.own_msg), channel_id=1, source_target_pairs={{0,16},{8,24},{16,0},{24,8},{1,17},{9,25},{17,1},{25,9},{2,18},{10... | collective-permute-start | bytes 442376 | tf_op jit(solution)/shard_map/ppermute | solution.py:390
  40.4 12.2 %collective-permute-start.1 = (bf16[576,128]{1,0:T(8,128)(2,1)}, bf16[576,128]{1,0:T(8,128)(2,1)S(1)}, u32[]{:S(2)}, u32[]{:S(2)}) collective-permute-start(bf16[576,128]{1,0:T(8,128)(2,1)} %get-tuple-element.21.refs_0_.own_msg), channel_id=1, source_target_pairs={{0,8},{8,16},{16,24},{24,0},{1,9},{9,17},{17,25},{25,1},{2,10},{10... | collective-permute-start | bytes 442376 | tf_op jit(solution)/shard_map/ppermute | solution.py:390
  41.4 11.8 %collective-permute-start.4 = (bf16[576,128]{1,0:T(8,128)(2,1)}, bf16[576,128]{1,0:T(8,128)(2,1)S(1)}, u32[]{:S(2)}, u32[]{:S(2)}) collective-permute-start(bf16[576,128]{1,0:T(8,128)(2,1)} %get-tuple-element.21.refs_0_.own_msg), channel_id=1, source_target_pairs={{0,1},{1,0},{2,3},{3,2},{4,5},{5,4},{6,7},{7,6},{8,9},{9,8},{10,11... | collective-permute-start | bytes 442376 | tf_op jit(solution)/shard_map/ppermute | solution.py:388
  45.0 11.9 %copy-start.3 = (bf16[576,128]{1,0:T(8,128)(2,1)}, bf16[576,128]{1,0:T(8,128)(2,1)S(1)}, u32[]{:S(2)}) copy-start(bf16[576,128]{1,0:T(8,128)(2,1)S(1)} %collective-permute-done.3.refs_3_) | copy-start | bytes 442372
  45.0 15.5 %collective-permute-start.7 = (bf16[576,128]{1,0:T(8,128)(2,1)S(1)}, bf16[576,128]{1,0:T(8,128)(2,1)S(1)}, u32[]{:S(2)}, u32[]{:S(2)}) collective-permute-start(bf16[576,128]{1,0:T(8,128)(2,1)S(1)} %collective-permute-done.3.refs_3_), channel_id=1, source_target_pairs={{0,1},{1,0},{2,3},{3,2},{4,5},{5,4},{6,7},{7,6},{8,9},{9,8},{10,11... | collective-permute-start | bytes 442376 | tf_op jit(solution)/shard_map/ppermute | solution.py:401
  52.7 4.2 %copy-start.4 = (bf16[576,128]{1,0:T(8,128)(2,1)}, bf16[576,128]{1,0:T(8,128)(2,1)S(1)}, u32[]{:S(2)}) copy-start(bf16[576,128]{1,0:T(8,128)(2,1)S(1)} %collective-permute-done.2.refs_2_) | copy-start | bytes 442372
  52.7 7.8 %collective-permute-start.6 = (bf16[576,128]{1,0:T(8,128)(2,1)S(1)}, bf16[576,128]{1,0:T(8,128)(2,1)S(1)}, u32[]{:S(2)}, u32[]{:S(2)}) collective-permute-start(bf16[576,128]{1,0:T(8,128)(2,1)S(1)} %collective-permute-done.2.refs_2_), channel_id=1, source_target_pairs={{0,1},{1,0},{2,3},{3,2},{4,5},{5,4},{6,7},{7,6},{8,9},{9,8},{10,11... | collective-permute-start | bytes 442376 | tf_op jit(solution)/shard_map/ppermute | solution.py:401
  52.7 4.2 %copy-start.5 = (bf16[576,128]{1,0:T(8,128)(2,1)}, bf16[576,128]{1,0:T(8,128)(2,1)S(1)}, u32[]{:S(2)}) copy-start(bf16[576,128]{1,0:T(8,128)(2,1)S(1)} %collective-permute-done.1.refs_1_) | copy-start | bytes 442372
  52.7 7.8 %collective-permute-start.5 = (bf16[576,128]{1,0:T(8,128)(2,1)S(1)}, bf16[576,128]{1,0:T(8,128)(2,1)S(1)}, u32[]{:S(2)}, u32[]{:S(2)}) collective-permute-start(bf16[576,128]{1,0:T(8,128)(2,1)S(1)} %collective-permute-done.1.refs_1_), channel_id=1, source_target_pairs={{0,1},{1,0},{2,3},{3,2},{4,5},{5,4},{6,7},{7,6},{8,9},{9,8},{10,11... | collective-permute-start | bytes 442376 | tf_op jit(solution)/shard_map/ppermute | solution.py:401
  53.2 0.6 copy-start.2
  56.9 21.2 %all-to-all-start.1 = ((bf16[8,272,128]{2,1,0:T(8,128)(2,1)}), bf16[8,272,128]{2,1,0:T(8,128)(2,1)S(1)}, u32[]{:S(2)}, u32[]{:S(2)}) async-start(bf16[8,272,128]{2,1,0:T(8,128)(2,1)} %backward.1), calls=%async_computation.1 | async-start | bytes 1114112 | tf_op jit(solution)/shard_map/all_to_all | solution.py:400
  60.5 0.7 copy-start.6
  60.5 0.7 copy-start.7
  60.5 0.7 copy-start.8
  64.0 0.7 copy-start.9
  78.1 0.8 copy-start.1

commit v2 on v1

--- a/solution.py
+++ b/solution.py
@@ -6,6 +6,7 @@
 from jax.experimental import pallas as pl
 from jax.experimental.pallas import tpu as pltpu
 from jax.sharding import PartitionSpec as P
+
 
 D = 2048
 HD = 128
@@ -150,6 +151,7 @@
 
 VMEM = pl.BlockSpec(memory_space=pltpu.VMEM)
 SMEM = pl.BlockSpec(memory_space=pltpu.SMEM)
+VMEM_LIMIT = 16 << 20
 ROWS_T = (((1,), (1,)), ((), ()))
 COLS_T = (((0,), (0,)), ((), ()))
 
@@ -158,15 +160,27 @@
     return lax.dot_general(one, two, dims, preferred_element_type=jnp.float32)
 
 
-def kernel_call(kernel, name, in_specs, outs, scratch=()):
-    return pl.pallas_call(
+def kernel_call(kernel, in_specs, outs, scratch=(), flops=1 << 20, on_chip=True):
+    shaped = pltpu.VMEM if on_chip else jax.ShapeDtypeStruct
+    call = pl.pallas_call(
         kernel,
-        name=name,
         in_specs=in_specs,
         out_specs=[VMEM] * len(outs),
-        out_shape=[jax.ShapeDtypeStruct(shape, dtype) for shape, dtype in outs],
+        out_shape=[shaped(shape, dtype) for shape, dtype in outs],
         scratch_shapes=list(scratch),
-    )
+        cost_estimate=pl.CostEstimate(flops=flops, bytes_accessed=0, transcendentals=0),
+        compiler_params=pltpu.CompilerParams(vmem_limit_bytes=VMEM_LIMIT),
+    )
+
+    def placed(*operands):
+        return call(
+            *(
+                pltpu.with_memory_space_constraint(operand, pltpu.VMEM) if spec is VMEM else operand
+                for spec, operand in zip(in_specs, operands)
+            )
+        )
+
+    return placed
 
 
 def pack_kernel(targets, keys, values, queries, packed):
@@ -209,7 +223,7 @@
     return scores, places <= last
 
 
-def forward_kernel(side, positions, packed, out_proj, attn, log_norm, onehot, kept, sent, *, tok, own):
+def forward_kernel(side, positions, packed, out_proj, attn, log_norm, onehot, kept, sent, hidden, *, tok, own):
     keys, values, queries = split_packed(packed, tok, own)
     scores, visible = visible_scores(keys, queries, positions)
     best = jnp.max(jnp.where(visible, scores, -1e30), axis=-1, keepdims=True)
@@ -226,18 +240,17 @@
         .astype(jnp.float32)
         .reshape(half, HD)
     )
-    proj = out_proj[...]
-    kept[...] = matmul(attn[pl.ds(pl.multiple_of(mine * half, half), half), :], proj)
-    sent[...] = matmul(attn[pl.ds(pl.multiple_of((1 - mine) * half, half), half), :], proj).astype(
-        sent.dtype
-    )
-
-
-def loss_kernel(parts, gain, unembed, onehot_ref, attn, message, stats):
-    half = parts.shape[1]
-    hidden = parts[0].astype(jnp.float32)
-    for part in range(1, parts.shape[0]):
-        hidden = hidden + parts[part].astype(jnp.float32)
+    hidden[...] = matmul(attn[...], out_proj[...])
+    kept[...] = hidden[pl.ds(pl.multiple_of(mine * half, half), half), :]
+    sent[...] = hidden[pl.ds(pl.multiple_of((1 - mine) * half, half), half), :].astype(sent.dtype)
+
+
+def loss_kernel(gain, unembed, onehot_ref, attn, *refs):
+    *parts, message, stats = refs
+    half = onehot_ref.shape[0]
+    hidden = parts[0][...].astype(jnp.float32)
+    for part in parts[1:]:
+        hidden = hidden + part[...].astype(jnp.float32)
     onehot = onehot_ref[...]
     inverse = lax.rsqrt(jnp.mean(hidden * hidden, axis=-1, keepdims=True) + epsilon)
     normed = (hidden * inverse * gain[...]).astype(jnp.bfloat16)
@@ -347,7 +360,8 @@
         and vocab == HD
         and tok % 16 == 0
         and own == 8
-        and n_seq % 2 == 0
+        and n_seq & (n_seq - 1) == 0
+        and n_seq > 1
     ):
         return general_body(
             hist_keys, hist_values, latent_queries, latent_pos, targets, out_proj, norm_gain, unembed
@@ -358,16 +372,14 @@
     span = 2 * tok + 2 * own
     side = (lax.axis_index("seq") % 2).reshape(1)
     swap = [(i, i ^ 1) for i in range(n_seq)]
-    sides = [[i for i in range(n_seq) if i % 2 == k] for k in range(2)]
 
     (packed,) = kernel_call(
-        pack_kernel, "pack", [SMEM, VMEM, VMEM, VMEM], [((heads, span, HD), bf16)]
+        pack_kernel, [SMEM, VMEM, VMEM, VMEM], [((heads, span, HD), bf16)]
     )(targets, seq_keys, hist_values[0], latent_queries[0])
     packed = lax.all_to_all(packed, "seq", 0, 0)
 
     attn, log_norm, onehot, kept, sent = kernel_call(
         partial(forward_kernel, tok=tok, own=own),
-        "forward",
         [SMEM, VMEM, VMEM, VMEM],
         [
             ((latents, HD), bf16),
@@ -376,32 +388,36 @@
             ((half, width), f32),
             ((half, width), bf16),
         ],
+        [pltpu.VMEM((latents, width), f32)],
     )(side, latent_pos, packed, out_proj)
     pair_sum = (kept + lax.ppermute(sent, "seq", swap).astype(f32)).astype(bf16)
-    parts = lax.all_gather(pair_sum, "seq", axis_index_groups=sides)
+    parts = [pair_sum] + [
+        lax.ppermute(pair_sum, "seq", [(i, i ^ step) for i in range(n_seq)])
+        for step in range(2, n_seq, 2)
+    ]
     message, loss = kernel_call(
         loss_kernel,
-        "loss",
-        [VMEM] * 5,
+        [VMEM] * (4 + len(parts)),
         [((width // HD * half + latents, HD), bf16), ((1, HD), f32)],
-    )(parts, norm_gain.reshape(1, width), unembed, onehot, attn)
+    )(norm_gain.reshape(1, width), unembed, onehot, attn, *parts)
     pair_msg = lax.ppermute(message, "seq", swap)
     others = [
         lax.ppermute(message, "grp", [(i, (i + step) % n_grp) for i in range(n_grp)])
         for step in range(1, n_grp)
     ]
-    (grads,) = kernel_call(
+    backward = kernel_call(
         partial(backward_kernel, tok=tok, own=own),
-        "backward",
         [SMEM] + [VMEM] * 7,
         [((heads, span, HD), bf16)],
         [pltpu.VMEM((latents, width), bf16)],
-    )(side, latent_pos, packed, out_proj, attn, log_norm, message, pair_msg)
+        flops=1 << 30,
+    )
+    (grads,) = backward(side, latent_pos, packed, out_proj, attn, log_norm, message, pair_msg)
+    others = lax.optimization_barrier((*others, grads))[:-1]
     grads = lax.all_to_all(grads, "seq", 0, 0)
     pair_others = [lax.ppermute(other, "seq", swap) for other in others]
     weights, stats = kernel_call(
         partial(weight_kernel, count=n_grp),
-        "weights",
         [SMEM] + [VMEM] * (2 * n_grp + 1),
         [((channels // n_seq, width), f32), ((1, HD), f32)],
         [
@@ -411,12 +427,17 @@
     )(side, message, *others, pair_msg, *pair_others, loss)
     grad_queries, grad_keys, grad_values = kernel_call(
         unpack_kernel,
-        "unpack",
         [VMEM],
         [((own, channels), bf16), ((tok, channels), bf16), ((tok, channels), bf16)],
+        on_chip=False,
     )(grads)
-    gathered = lax.all_gather(stats, "seq", axis=0, tiled=True)
-    totals = jnp.sum(gathered, axis=0)
+    stats = stats + lax.ppermute(stats, "seq", swap)
+    received = [
+        lax.ppermute(stats, "seq", [(i, i ^ step) for i in range(n_seq)])
+        for step in range(2, n_seq, 2)
+    ]
+    received = lax.optimization_barrier((*received, grad_queries))[:-1]
+    totals = sum(received, stats)[0]
     loss_sum = totals[HD - 1] / (n_seq // 2)
     proj_update = weights * lax.rsqrt(totals[0] / (channels * width) + epsilon)
     return (

time: 82.6 us -> 70.8 us (0.86)
  blocking collectives: 19.4 us -> 0 us
  waiting for transfers between devices: 22.9 us -> 34.5 us
  Pallas kernels: 15.1 us -> 6.21 us
  starting transfers between devices: 13.9 us -> 21.4 us
  other arithmetic: 3.3 us -> 1.09 us
    all_gather x2 -> x0, blocking collectives: 19.4 us -> none  [the longest x1 10.2 us: body(): parts = lax.all_gather(pair_sum, 'seq', axis_index_groups=sides)]
    pallas_call x6, Pallas kernels: 15.1 us -> 6.21 us  [placed(): call(*(pltpu.with_memory_space_constraint(operand, pltpu.VMEM) if spec is...]
    ppermute x0 -> x7, waiting for transfers between devices: none -> 8.35 us  [the longest x3 5.15 us: body(): lax.ppermute(pair_sum, 'seq', [(i, i ^ step) for i in range(n_seq)])]
    ppermute x0 -> x7, starting transfers between devices: none -> 7.26 us  [the longest x3 3.55 us: body(): lax.ppermute(pair_sum, 'seq', [(i, i ^ step) for i in range(n_seq)])]
    ppermute x3, waiting for transfers between devices: 0.01 us -> 1.37 us  [body(): pair_others = [lax.ppermute(other, 'seq', swap) for other in others]]
    ppermute x1, waiting for transfers between devices: 0.01 us -> 1.36 us  [body(): pair_msg = lax.ppermute(message, 'seq', swap)]
    mul x1, other arithmetic: 2.3 us -> 1.06 us  [body(): proj_update = weights * lax.rsqrt(totals[0] / (channels * width) + epsilon)]
    convert_element_type x1, other arithmetic: 0.98 us -> 0.03 us  [body(): pair_sum = (kept + lax.ppermute(sent, 'seq', swap).astype(f32)).astype(bf16)]
  transfers between devices with their start and end apart: 10 -> 17, of which waited for: 4 -> 13; matrix products, arithmetic and copies ran while one was open for 4% -> 0% of each run, Pallas kernels for 7% -> 2%
where the time goes in v2:
time: 70.8 us; the launch traced here: 70.3 us
  waiting for transfers between devices  34.5 us (49%)
  starting transfers between devices  21.4 us (30%)
  Pallas kernels  6.21 us (9%)
  local copies, waits for them, and re-layouts  3.87 us (5%)
  between operations  3.19 us (5%)
  other arithmetic  1.09 us (2%)
    ppermute x3, waiting for transfers between devices, body(): lax.ppermute(message, 'grp', [(i, (i + step) % n_grp) for i in range(n_gr...  12 us
    all_to_all x1, waiting for transfers between devices, body(): packed = lax.all_to_all(packed, 'seq', 0, 0)  10.1 us
    pallas_call x6, Pallas kernels, placed(): call(*(pltpu.with_memory_space_constraint(operand, pltpu.VMEM) if spec is...  6.21 us
    all_to_all x1, starting transfers between devices, body(): packed = lax.all_to_all(packed, 'seq', 0, 0)  5.33 us
    ppermute x3, waiting for transfers between devices, body(): lax.ppermute(pair_sum, 'seq', [(i, i ^ step) for i in range(n_seq)])  5.15 us
    ppermute x3, starting transfers between devices, body(): lax.ppermute(message, 'grp', [(i, (i + step) % n_grp) for i in range(n_gr...  4.67 us
    ppermute x3, starting transfers between devices, body(): lax.ppermute(pair_sum, 'seq', [(i, i ^ step) for i in range(n_seq)])  3.55 us
    all_to_all x1, starting transfers between devices, body(): grads = lax.all_to_all(grads, 'seq', 0, 0)  3.54 us
  transfers between devices with their start and end apart: 17, of which 13 were waited for; matrix products, arithmetic and copies ran while one was open for 0% of the time, Pallas kernels for 2%

profile of v2, /device:TPU:0, one launch (start us, length us, event | category | flops | bytes accessed | tf_op | source)
XLA Modules:
  0.0 70.3 jit_solution(2749708937950372022)
XLA Ops:
  1.3 0.9 %copy-done.2 = bf16[1,128,1024]{2,1,0:T(8,128)(2,1)S(1)} copy-done((bf16[1,128,1024]{2,1,0:T(8,128)(2,1)S(1)}, bf16[1,128,1024]{2,1,0:T(8,128)(2,1)}, u32[]{:S(2)}) %copy-start.2) | copy-done | bytes 262168
  2.2 0.9 %copy-done.3 = bf16[1,128,1024]{2,1,0:T(8,128)(2,1)S(1)} copy-done((bf16[1,128,1024]{2,1,0:T(8,128)(2,1)S(1)}, bf16[1,128,1024]{2,1,0:T(8,128)(2,1)}, u32[]{:S(2)}) %copy-start.3) | copy-done | bytes 262168
  3.9 1.4 %shard_map.119 = bf16[8,272,128]{2,1,0:T(8,128)(2,1)} custom-call(s32[1,8]{1,0:T(1,128)S(1)} %copy-done.7, bf16[128,1024]{1,0:T(8,128)(2,1)S(1)} %bitcast.10, bf16[128,1024]{1,0:T(8,128)(2,1)S(1)} %bitcast.11, bf16[8,1024]{1,0:T(8,128)(2,1)S(1)} %bitcast.12), custom_call_target="tpu_custom_call" | custom-call | flops 1048576 | tf_op jit(solution)/shard_map/pallas_call | solution.py:176
  5.4 5.3 %all-to-all-start = ((bf16[8,272,128]{2,1,0:T(8,128)(2,1)}), bf16[8,272,128]{2,1,0:T(8,128)(2,1)S(1)}, u32[]{:S(2)}, u32[]{:S(2)}) async-start(bf16[8,272,128]{2,1,0:T(8,128)(2,1)} %shard_map.119), calls=%async_computation | async-start | bytes 1114112 | tf_op jit(solution)/shard_map/all_to_all | solution.py:379
  10.7 10.1 %all-to-all-done.packed = bf16[8,272,128]{2,1,0:T(8,128)(2,1)S(1)} async-done(((bf16[8,272,128]{2,1,0:T(8,128)(2,1)}), bf16[8,272,128]{2,1,0:T(8,128)(2,1)S(1)}, u32[]{:S(2)}, u32[]{:S(2)}) %all-to-all-start) | async-done | bytes 557088 | tf_op jit(solution)/shard_map/all_to_all | solution.py:379
  21.5 1.3 %collective-permute-done = bf16[32,2048]{1,0:T(8,128)(2,1)S(1)} collective-permute-done((bf16[32,2048]{1,0:T(8,128)(2,1)S(1)}, bf16[32,2048]{1,0:T(8,128)(2,1)S(1)}, u32[]{:S(2)}, u32[]{:S(2)}) %collective-permute-start) | collective-permute-done | bytes 131104 | tf_op jit(solution)/shard_map/ppermute | solution.py:393
  23.5 1.5 %collective-permute-start.2 = (bf16[32,2048]{1,0:T(8,128)(2,1)S(1)}, bf16[32,2048]{1,0:T(8,128)(2,1)S(1)}, u32[]{:S(2)}, u32[]{:S(2)}) collective-permute-start(bf16[32,2048]{1,0:T(8,128)(2,1)S(1)} %add_convert_fusion.refs_0_), channel_id=1, source_target_pairs={{0,4},{1,5},{2,6},{3,7},{4,0},{5,1},{6,2},{7,3},{8,12},{9,13},{10,... | collective-permute-start | bytes 393224 | tf_op jit(solution)/shard_map/ppermute | solution.py:395
  25.0 1.5 %collective-permute-start.1 = (bf16[32,2048]{1,0:T(8,128)(2,1)S(1)}, bf16[32,2048]{1,0:T(8,128)(2,1)S(1)}, u32[]{:S(2)}, u32[]{:S(2)}) collective-permute-start(bf16[32,2048]{1,0:T(8,128)(2,1)S(1)} %add_convert_fusion.refs_0_), channel_id=1, source_target_pairs={{0,2},{1,3},{2,0},{3,1},{4,6},{5,7},{6,4},{7,5},{8,10},{9,11},{10,... | collective-permute-start | bytes 393224 | tf_op jit(solution)/shard_map/ppermute | solution.py:395
  26.5 3.8 %collective-permute-done.3.refs_3_ = bf16[32,2048]{1,0:T(8,128)(2,1)S(1)} collective-permute-done((bf16[32,2048]{1,0:T(8,128)(2,1)S(1)}, bf16[32,2048]{1,0:T(8,128)(2,1)S(1)}, u32[]{:S(2)}, u32[]{:S(2)}) %collective-permute-start.3) | collective-permute-done | bytes 131104 | tf_op jit(solution)/shard_map/ppermute | solution.py:395
  30.3 1.3 %collective-permute-done.2.refs_2_ = bf16[32,2048]{1,0:T(8,128)(2,1)S(1)} collective-permute-done((bf16[32,2048]{1,0:T(8,128)(2,1)S(1)}, bf16[32,2048]{1,0:T(8,128)(2,1)S(1)}, u32[]{:S(2)}, u32[]{:S(2)}) %collective-permute-start.2) | collective-permute-done | bytes 131104 | tf_op jit(solution)/shard_map/ppermute | solution.py:395
  31.6 0.9 %shard_map.121 = (bf16[576,128]{1,0:T(8,128)(2,1)S(1)}, f32[1,128]{1,0:T(1,128)S(1)}) custom-call(f32[1,2048]{1,0:T(1,128)S(1)} %bitcast.13, bf16[2048,128]{1,0:T(8,128)(2,1)S(1)} %copy-done.1, f32[32,128]{1,0:T(8,128)S(1)} %get-tuple-element.23.onehot_ref, bf16[64,128]{1,0:T(8,128)(2,1)S(1)} %get-tuple-element.24.attn, ...), custom_call_target="tpu_custom_call" | custom-call | flops 1048576 | tf_op jit(solution)/shard_map/pallas_call | solution.py:176
  32.6 1.4 %collective-permute-done.7.pair_msg.refs_4_ = bf16[576,128]{1,0:T(8,128)(2,1)S(1)} collective-permute-done((bf16[576,128]{1,0:T(8,128)(2,1)S(1)}, bf16[576,128]{1,0:T(8,128)(2,1)S(1)}, u32[]{:S(2)}, u32[]{:S(2)}) %collective-permute-start.7) | collective-permute-done | bytes 147488 | tf_op jit(solution)/shard_map/ppermute | solution.py:403
  34.0 1.7 %shard_map.122 = bf16[8,272,128]{2,1,0:T(8,128)(2,1)} custom-call(s32[1]{0:T(128)} %bitcast.side, s32[1,64]{1,0:T(1,128)S(1)} %copy-done.6, bf16[8,272,128]{2,1,0:T(8,128)(2,1)S(1)} %all-to-all-done.packed, bf16[128,2048]{1,0:T(8,128)(2,1)S(1)} %copy-done, bf16[64,128]{1,0:T(8,128)(2,1)S(1)} %get-tuple-element.24.attn, ...), custom_call_target="tpu_custom_call" | custom-call | flops 1073741824 | tf_op jit(solution)/shard_map/pallas_call | solution.py:176
  35.7 3.5 %all-to-all-start.1 = ((bf16[8,272,128]{2,1,0:T(8,128)(2,1)}), bf16[8,272,128]{2,1,0:T(8,128)(2,1)S(1)}, u32[]{:S(2)}, u32[]{:S(2)}) async-start(bf16[8,272,128]{2,1,0:T(8,128)(2,1)} %shard_map.122), calls=%async_computation.1 | async-start | bytes 1114112 | tf_op jit(solution)/shard_map/all_to_all | solution.py:417
  39.2 3.7 %collective-permute-start.6 = (bf16[576,128]{1,0:T(8,128)(2,1)S(1)}, bf16[576,128]{1,0:T(8,128)(2,1)S(1)}, u32[]{:S(2)}, u32[]{:S(2)}) collective-permute-start(bf16[576,128]{1,0:T(8,128)(2,1)S(1)} %get-tuple-element.27.own_msg.refs_0_), channel_id=1, source_target_pairs={{0,24},{8,0},{16,8},{24,16},{1,25},{9,1},{17,9},{25,17},{2,26},{10... | collective-permute-start | bytes 442376 | tf_op jit(solution)/shard_map/ppermute | solution.py:405
  42.9 1.0 %collective-permute-start.4 = (bf16[576,128]{1,0:T(8,128)(2,1)S(1)}, bf16[576,128]{1,0:T(8,128)(2,1)S(1)}, u32[]{:S(2)}, u32[]{:S(2)}) collective-permute-start(bf16[576,128]{1,0:T(8,128)(2,1)S(1)} %get-tuple-element.27.own_msg.refs_0_), channel_id=1, source_target_pairs={{0,8},{8,16},{16,24},{24,0},{1,9},{9,17},{17,25},{25,1},{2,10},{10... | collective-permute-start | bytes 442376 | tf_op jit(solution)/shard_map/ppermute | solution.py:405
  43.9 3.3 %collective-permute-done.6.refs_3_ = bf16[576,128]{1,0:T(8,128)(2,1)S(1)} collective-permute-done((bf16[576,128]{1,0:T(8,128)(2,1)S(1)}, bf16[576,128]{1,0:T(8,128)(2,1)S(1)}, u32[]{:S(2)}, u32[]{:S(2)}) %collective-permute-start.6) | collective-permute-done | bytes 147488 | tf_op jit(solution)/shard_map/ppermute | solution.py:405
  47.2 8.7 %collective-permute-done.5.refs_2_ = bf16[576,128]{1,0:T(8,128)(2,1)S(1)} collective-permute-done((bf16[576,128]{1,0:T(8,128)(2,1)S(1)}, bf16[576,128]{1,0:T(8,128)(2,1)S(1)}, u32[]{:S(2)}, u32[]{:S(2)}) %collective-permute-start.5) | collective-permute-done | bytes 147488 | tf_op jit(solution)/shard_map/ppermute | solution.py:405
  56.5 0.9 %collective-permute-done.8.refs_5_ = bf16[576,128]{1,0:T(8,128)(2,1)S(1)} collective-permute-done((bf16[576,128]{1,0:T(8,128)(2,1)S(1)}, bf16[576,128]{1,0:T(8,128)(2,1)S(1)}, u32[]{:S(2)}, u32[]{:S(2)}) %collective-permute-start.8) | collective-permute-done | bytes 147488 | tf_op jit(solution)/shard_map/ppermute | solution.py:418
  58.6 0.9 %collective-permute-done.11 = f32[1,128]{1,0:T(1,128)S(1)} collective-permute-done((f32[1,128]{1,0:T(1,128)S(1)}, f32[1,128]{1,0:T(1,128)S(1)}, u32[]{:S(2)}, u32[]{:S(2)}) %collective-permute-start.11) | collective-permute-done | bytes 544 | tf_op jit(solution)/shard_map/ppermute | solution.py:434
  59.5 2.6 %collective-permute-start.14 = (f32[1,128]{1,0:T(1,128)S(1)}, f32[1,128]{1,0:T(1,128)S(1)}, u32[]{:S(2)}, u32[]{:S(2)}) collective-permute-start(f32[1,128]{1,0:T(1,128)S(1)} %add.25), channel_id=1, source_target_pairs={{0,6},{1,7},{2,4},{3,5},{4,2},{5,3},{6,0},{7,1},{8,14},{9,15},{10,... | collective-permute-start | bytes 1544 | tf_op jit(solution)/shard_map/ppermute | solution.py:436
  63.0 0.9 %shard_map.124 = (bf16[8,1024]{1,0:T(8,128)(2,1)}, bf16[128,1024]{1,0:T(8,128)(2,1)}, bf16[128,1024]{1,0:T(8,128)(2,1)}) custom-call(bf16[8,272,128]{2,1,0:T(8,128)(2,1)S(1)} %all-to-all-done.1.packed), custom_call_target="tpu_custom_call" | custom-call | flops 1048576 | tf_op jit(solution)/shard_map/pallas_call | solution.py:176
  64.0 1.7 %collective-permute-done.13 = f32[1,128]{1,0:T(1,128)S(1)} collective-permute-done((f32[1,128]{1,0:T(1,128)S(1)}, f32[1,128]{1,0:T(1,128)S(1)}, u32[]{:S(2)}, u32[]{:S(2)}) %collective-permute-start.13) | collective-permute-done | bytes 544 | tf_op jit(solution)/shard_map/ppermute | solution.py:436
  68.1 1.1 %broadcast_multiply_fusion = f32[128,2048]{1,0:T(8,128)} fusion(f32[128,2048]{1,0:T(8,128)S(1)} %get-tuple-element.40, f32[]{:T(128)} %bitcast.9), kind=kLoop, calls=%fused_computation | loop fusion | flops 262144 | bytes 2097156 | tf_op jit(solution)/shard_map/mul | solution.py:442
  (37 shorter events, 6.7 us)
Async XLA Ops:
  1.3 0.9 %copy-start.2 = (bf16[1,128,1024]{2,1,0:T(8,128)(2,1)S(1)}, bf16[1,128,1024]{2,1,0:T(8,128)(2,1)}, u32[]{:S(2)}) copy-start(bf16[1,128,1024]{2,1,0:T(8,128)(2,1)} %param.8) | copy-start | bytes 786436
  2.2 0.9 %copy-start.3 = (bf16[1,128,1024]{2,1,0:T(8,128)(2,1)S(1)}, bf16[1,128,1024]{2,1,0:T(8,128)(2,1)}, u32[]{:S(2)}) copy-start(bf16[1,128,1024]{2,1,0:T(8,128)(2,1)} %param.9) | copy-start | bytes 786436
  3.2 0.7 %copy-start.4 = (bf16[1,8,1024]{2,1,0:T(8,128)(2,1)S(1)}, bf16[1,8,1024]{2,1,0:T(8,128)(2,1)}, u32[]{:S(2)}) copy-start(bf16[1,8,1024]{2,1,0:T(8,128)(2,1)} %param.10) | copy-start | bytes 49156
  5.3 15.4 %copy-start = (bf16[128,2048]{1,0:T(8,128)(2,1)S(1)}, bf16[128,2048]{1,0:T(8,128)(2,1)}, u32[]{:S(2)}) copy-start(bf16[128,2048]{1,0:T(8,128)(2,1)} %out_proj.3) | copy-start | bytes 1572868
  5.4 15.4 %all-to-all-start = ((bf16[8,272,128]{2,1,0:T(8,128)(2,1)}), bf16[8,272,128]{2,1,0:T(8,128)(2,1)S(1)}, u32[]{:S(2)}, u32[]{:S(2)}) async-start(bf16[8,272,128]{2,1,0:T(8,128)(2,1)} %shard_map.119), calls=%async_computation | async-start | bytes 1114112 | tf_op jit(solution)/shard_map/all_to_all | solution.py:379
  10.7 10.1 %copy-start.6 = (s32[1,64]{1,0:T(1,128)S(1)}, s32[1,64]{1,0:T(1,128)}, u32[]{:S(2)}) copy-start(s32[1,64]{1,0:T(1,128)} %positions.3) | copy-start | bytes 772
  21.5 10.2 %copy-start.1 = (bf16[2048,128]{1,0:T(8,128)(2,1)S(1)}, bf16[2048,128]{1,0:T(8,128)(2,1)}, u32[]{:S(2)}) copy-start(bf16[2048,128]{1,0:T(8,128)(2,1)} %unembed.1) | copy-start | bytes 1572868
  21.5 1.4 %collective-permute-start = (bf16[32,2048]{1,0:T(8,128)(2,1)S(1)}, bf16[32,2048]{1,0:T(8,128)(2,1)S(1)}, u32[]{:S(2)}, u32[]{:S(2)}) collective-permute-start(bf16[32,2048]{1,0:T(8,128)(2,1)S(1)} %get-tuple-element.26), channel_id=1, source_target_pairs={{0,1},{1,0},{2,3},{3,2},{4,5},{5,4},{6,7},{7,6},{8,9},{9,8},{10,11... | collective-permute-start | bytes 393224 | tf_op jit(solution)/shard_map/ppermute | solution.py:393
  22.9 8.7 %copy-start.5 = (f32[2048]{0:T(1024)S(1)}, f32[2048]{0:T(1024)}, u32[]{:S(2)}) copy-start(f32[2048]{0:T(1024)} %param.14) | copy-start | bytes 24580
  22.9 7.4 %collective-permute-start.3 = (bf16[32,2048]{1,0:T(8,128)(2,1)S(1)}, bf16[32,2048]{1,0:T(8,128)(2,1)S(1)}, u32[]{:S(2)}, u32[]{:S(2)}) collective-permute-start(bf16[32,2048]{1,0:T(8,128)(2,1)S(1)} %add_convert_fusion.refs_0_), channel_id=1, source_target_pairs={{0,6},{1,7},{2,4},{3,5},{4,2},{5,3},{6,0},{7,1},{8,14},{9,15},{10,... | collective-permute-start | bytes 393224 | tf_op jit(solution)/shard_map/ppermute | solution.py:395
  23.5 8.1 %collective-permute-start.2 = (bf16[32,2048]{1,0:T(8,128)(2,1)S(1)}, bf16[32,2048]{1,0:T(8,128)(2,1)S(1)}, u32[]{:S(2)}, u32[]{:S(2)}) collective-permute-start(bf16[32,2048]{1,0:T(8,128)(2,1)S(1)} %add_convert_fusion.refs_0_), channel_id=1, source_target_pairs={{0,4},{1,5},{2,6},{3,7},{4,0},{5,1},{6,2},{7,3},{8,12},{9,13},{10,... | collective-permute-start | bytes 393224 | tf_op jit(solution)/shard_map/ppermute | solution.py:395
  25.0 6.6 %collective-permute-start.1 = (bf16[32,2048]{1,0:T(8,128)(2,1)S(1)}, bf16[32,2048]{1,0:T(8,128)(2,1)S(1)}, u32[]{:S(2)}, u32[]{:S(2)}) collective-permute-start(bf16[32,2048]{1,0:T(8,128)(2,1)S(1)} %add_convert_fusion.refs_0_), channel_id=1, source_target_pairs={{0,2},{1,3},{2,0},{3,1},{4,6},{5,7},{6,4},{7,5},{8,10},{9,11},{10,... | collective-permute-start | bytes 393224 | tf_op jit(solution)/shard_map/ppermute | solution.py:395
  32.5 1.4 %collective-permute-start.7 = (bf16[576,128]{1,0:T(8,128)(2,1)S(1)}, bf16[576,128]{1,0:T(8,128)(2,1)S(1)}, u32[]{:S(2)}, u32[]{:S(2)}) collective-permute-start(bf16[576,128]{1,0:T(8,128)(2,1)S(1)} %get-tuple-element.27.own_msg.refs_0_), channel_id=1, source_target_pairs={{0,1},{1,0},{2,3},{3,2},{4,5},{5,4},{6,7},{7,6},{8,9},{9,8},{10,11... | collective-permute-start | bytes 442376 | tf_op jit(solution)/shard_map/ppermute | solution.py:403
  35.7 27.3 %all-to-all-start.1 = ((bf16[8,272,128]{2,1,0:T(8,128)(2,1)}), bf16[8,272,128]{2,1,0:T(8,128)(2,1)S(1)}, u32[]{:S(2)}, u32[]{:S(2)}) async-start(bf16[8,272,128]{2,1,0:T(8,128)(2,1)} %shard_map.122), calls=%async_computation.1 | async-start | bytes 1114112 | tf_op jit(solution)/shard_map/all_to_all | solution.py:417
  39.2 8.0 %collective-permute-start.6 = (bf16[576,128]{1,0:T(8,128)(2,1)S(1)}, bf16[576,128]{1,0:T(8,128)(2,1)S(1)}, u32[]{:S(2)}, u32[]{:S(2)}) collective-permute-start(bf16[576,128]{1,0:T(8,128)(2,1)S(1)} %get-tuple-element.27.own_msg.refs_0_), channel_id=1, source_target_pairs={{0,24},{8,0},{16,8},{24,16},{1,25},{9,1},{17,9},{25,17},{2,26},{10... | collective-permute-start | bytes 442376 | tf_op jit(solution)/shard_map/ppermute | solution.py:405
  42.9 13.0 %collective-permute-start.5 = (bf16[576,128]{1,0:T(8,128)(2,1)S(1)}, bf16[576,128]{1,0:T(8,128)(2,1)S(1)}, u32[]{:S(2)}, u32[]{:S(2)}) collective-permute-start(bf16[576,128]{1,0:T(8,128)(2,1)S(1)} %get-tuple-element.27.own_msg.refs_0_), channel_id=1, source_target_pairs={{0,16},{8,24},{16,0},{24,8},{1,17},{9,25},{17,1},{25,9},{2,18},{10... | collective-permute-start | bytes 442376 | tf_op jit(solution)/shard_map/ppermute | solution.py:405
  42.9 13.0 %collective-permute-start.4 = (bf16[576,128]{1,0:T(8,128)(2,1)S(1)}, bf16[576,128]{1,0:T(8,128)(2,1)S(1)}, u32[]{:S(2)}, u32[]{:S(2)}) collective-permute-start(bf16[576,128]{1,0:T(8,128)(2,1)S(1)} %get-tuple-element.27.own_msg.refs_0_), channel_id=1, source_target_pairs={{0,8},{8,16},{16,24},{24,0},{1,9},{9,17},{17,25},{25,1},{2,10},{10... | collective-permute-start | bytes 442376 | tf_op jit(solution)/shard_map/ppermute | solution.py:405
  55.9 1.4 %collective-permute-start.8 = (bf16[576,128]{1,0:T(8,128)(2,1)S(1)}, bf16[576,128]{1,0:T(8,128)(2,1)S(1)}, u32[]{:S(2)}, u32[]{:S(2)}) collective-permute-start(bf16[576,128]{1,0:T(8,128)(2,1)S(1)} %collective-permute-done.4.refs_1_), channel_id=1, source_target_pairs={{0,1},{1,0},{2,3},{3,2},{4,5},{5,4},{6,7},{7,6},{8,9},{9,8},{10,11... | collective-permute-start | bytes 442376 | tf_op jit(solution)/shard_map/ppermute | solution.py:418
  55.9 1.6 %collective-permute-start.9 = (bf16[576,128]{1,0:T(8,128)(2,1)S(1)}, bf16[576,128]{1,0:T(8,128)(2,1)S(1)}, u32[]{:S(2)}, u32[]{:S(2)}) collective-permute-start(bf16[576,128]{1,0:T(8,128)(2,1)S(1)} %collective-permute-done.5.refs_2_), channel_id=1, source_target_pairs={{0,1},{1,0},{2,3},{3,2},{4,5},{5,4},{6,7},{7,6},{8,9},{9,8},{10,11... | collective-permute-start | bytes 442376 | tf_op jit(solution)/shard_map/ppermute | solution.py:418
  56.4 1.4 %collective-permute-start.10 = (bf16[576,128]{1,0:T(8,128)(2,1)S(1)}, bf16[576,128]{1,0:T(8,128)(2,1)S(1)}, u32[]{:S(2)}, u32[]{:S(2)}) collective-permute-start(bf16[576,128]{1,0:T(8,128)(2,1)S(1)} %collective-permute-done.6.refs_3_), channel_id=1, source_target_pairs={{0,1},{1,0},{2,3},{3,2},{4,5},{5,4},{6,7},{7,6},{8,9},{9,8},{10,11... | collective-permute-start | bytes 442376 | tf_op jit(solution)/shard_map/ppermute | solution.py:418
  58.3 1.2 %collective-permute-start.11 = (f32[1,128]{1,0:T(1,128)S(1)}, f32[1,128]{1,0:T(1,128)S(1)}, u32[]{:S(2)}, u32[]{:S(2)}) collective-permute-start(f32[1,128]{1,0:T(1,128)S(1)} %get-tuple-element.33), channel_id=1, source_target_pairs={{0,1},{1,0},{2,3},{3,2},{4,5},{5,4},{6,7},{7,6},{8,9},{9,8},{10,11... | collective-permute-start | bytes 1544 | tf_op jit(solution)/shard_map/ppermute | solution.py:434
  59.5 4.5 %collective-permute-start.14 = (f32[1,128]{1,0:T(1,128)S(1)}, f32[1,128]{1,0:T(1,128)S(1)}, u32[]{:S(2)}, u32[]{:S(2)}) collective-permute-start(f32[1,128]{1,0:T(1,128)S(1)} %add.25), channel_id=1, source_target_pairs={{0,6},{1,7},{2,4},{3,5},{4,2},{5,3},{6,0},{7,1},{8,14},{9,15},{10,... | collective-permute-start | bytes 1544 | tf_op jit(solution)/shard_map/ppermute | solution.py:436
  62.1 3.6 %collective-permute-start.13 = (f32[1,128]{1,0:T(1,128)S(1)}, f32[1,128]{1,0:T(1,128)S(1)}, u32[]{:S(2)}, u32[]{:S(2)}) collective-permute-start(f32[1,128]{1,0:T(1,128)S(1)} %add.25), channel_id=1, source_target_pairs={{0,4},{1,5},{2,6},{3,7},{4,0},{5,1},{6,2},{7,3},{8,12},{9,13},{10,... | collective-permute-start | bytes 1544 | tf_op jit(solution)/shard_map/ppermute | solution.py:436
  62.6 3.6 %collective-permute-start.12 = (f32[1,128]{1,0:T(1,128)S(1)}, f32[1,128]{1,0:T(1,128)S(1)}, u32[]{:S(2)}, u32[]{:S(2)}) collective-permute-start(f32[1,128]{1,0:T(1,128)S(1)} %add.25), channel_id=1, source_target_pairs={{0,2},{1,3},{2,0},{3,1},{4,6},{5,7},{6,4},{7,5},{8,10},{9,11},{10,... | collective-permute-start | bytes 1544 | tf_op jit(solution)/shard_map/ppermute | solution.py:436
  (1 other events, 0.7 us)

commit v3 on v2

--- a/solution.py
+++ b/solution.py
@@ -151,6 +151,8 @@
 
 VMEM = pl.BlockSpec(memory_space=pltpu.VMEM)
 SMEM = pl.BlockSpec(memory_space=pltpu.SMEM)
+KEPT = object()
+LOSS_ROWS = 16
 VMEM_LIMIT = 16 << 20
 ROWS_T = (((1,), (1,)), ((), ()))
 COLS_T = (((0,), (0,)), ((), ()))
@@ -160,13 +162,15 @@
     return lax.dot_general(one, two, dims, preferred_element_type=jnp.float32)
 
 
-def kernel_call(kernel, in_specs, outs, scratch=(), flops=1 << 20, on_chip=True):
-    shaped = pltpu.VMEM if on_chip else jax.ShapeDtypeStruct
+def kernel_call(kernel, in_specs, outs, scratch=(), flops=1 << 20, held=pltpu.VMEM):
     call = pl.pallas_call(
         kernel,
         in_specs=in_specs,
-        out_specs=[VMEM] * len(outs),
-        out_shape=[shaped(shape, dtype) for shape, dtype in outs],
+        out_specs=[VMEM if spec is KEPT else spec for _, _, spec in outs],
+        out_shape=[
+            (pltpu.VMEM if spec is KEPT else jax.ShapeDtypeStruct)(shape, dtype)
+            for shape, dtype, spec in outs
+        ],
         scratch_shapes=list(scratch),
         cost_estimate=pl.CostEstimate(flops=flops, bytes_accessed=0, transcendentals=0),
         compiler_params=pltpu.CompilerParams(vmem_limit_bytes=VMEM_LIMIT),
@@ -175,7 +179,9 @@
     def placed(*operands):
         return call(
             *(
-                pltpu.with_memory_space_constraint(operand, pltpu.VMEM) if spec is VMEM else operand
+                pltpu.with_memory_space_constraint(operand, held)
+                if spec is VMEM or held is pltpu.HBM
+                else operand
                 for spec, operand in zip(in_specs, operands)
             )
         )
@@ -245,7 +251,13 @@
     sent[...] = hidden[pl.ds(pl.multiple_of((1 - mine) * half, half), half), :].astype(sent.dtype)
 
 
-def loss_kernel(gain, unembed, onehot_ref, attn, *refs):
+def exact_parts(value):
+    high = value.astype(jnp.bfloat16).astype(jnp.float32)
+    middle = (value - high).astype(jnp.bfloat16).astype(jnp.float32)
+    return high, middle, value - high - middle
+
+
+def loss_kernel(gain, unembed, onehot_ref, *refs):
     *parts, message, stats = refs
     half = onehot_ref.shape[0]
     hidden = parts[0][...].astype(jnp.float32)
@@ -258,7 +270,8 @@
     top = jnp.max(logits, axis=-1, keepdims=True)
     log_total = top + jnp.log(jnp.sum(jnp.exp(logits - top), axis=-1, keepdims=True))
     losses = log_total - jnp.sum(logits * onehot, axis=-1, keepdims=True)
-    stats[...] = jnp.broadcast_to(jnp.sum(losses, axis=0, keepdims=True), stats.shape)
+    total = jnp.broadcast_to(jnp.sum(losses, axis=0, keepdims=True), stats.shape)
+    stats[...] = total
     grad_logits = (loss_factor * (jnp.exp(logits - log_total) - onehot)).astype(jnp.bfloat16)
     scaled = gain[...] * matmul(grad_logits, unembed[...], ROWS_T)
     mean = jnp.mean(hidden * scaled, axis=-1, keepdims=True)
@@ -268,7 +281,11 @@
     blocks = hidden.shape[1] // HD
     for block in range(blocks):
         message[block * half : (block + 1) * half, :] = grad_hidden[:, block * HD : (block + 1) * HD]
-    message[blocks * half :, :] = attn[...]
+    row = lax.broadcasted_iota(jnp.int32, (LOSS_ROWS, HD), 0)
+    high, middle, low = exact_parts(total)
+    message[blocks * half :, :] = jnp.where(
+        row == 0, high, jnp.where(row == 1, middle, jnp.where(row == 2, low, 0.0))
+    ).astype(jnp.bfloat16)
 
 
 def fill_rows(target, row, message, half):
@@ -279,7 +296,19 @@
 
 
 def backward_kernel(
-    side, positions, packed, out_proj, attn, log_norm, own_msg, pair_msg, grads, grad_hidden, *, tok, own
+    side,
+    positions,
+    packed,
+    out_proj,
+    attn,
+    log_norm,
+    own_msg,
+    pair_msg,
+    grads,
+    grad_hidden,
+    *,
+    tok,
+    own,
 ):
     half = grad_hidden.shape[0] // 2
     mine = side[0]
@@ -318,31 +347,32 @@
         grad_queries[:, cols] = packed[head, 2 * tok : 2 * tok + own, :]
 
 
-def weight_kernel(side, *refs, count):
-    messages = refs[: 2 * count]
-    loss, weights, stats, attn_rows, grad_rows = refs[2 * count :]
-    half = grad_rows.shape[0] // (2 * count)
-    blocks = grad_rows.shape[1] // HD
+def weight_kernel(side, *refs, groups, seqs, entries):
+    own_msgs = refs[:groups]
+    pair_msgs = refs[groups : 2 * groups]
+    attns = refs[2 * groups : 2 * groups + seqs]
+    loss_half, update, loss, grad_hidden, total = refs[2 * groups + seqs :]
+    latents = grad_hidden.shape[0] // groups
+    half = latents // 2
     mine = side[0]
-    for index in range(count):
-        attn_at = blocks * half
-        for place, message, part in (
-            (0, messages[index], mine),
-            (1, messages[count + index], 1 - mine),
-        ):
-            row = (2 * index + place) * half
-            for block in range(blocks):
-                grad_rows[row : row + half, block * HD : (block + 1) * HD] = message[
-                    block * half : (block + 1) * half, :
-                ]
-            attn_rows[row : row + half, :] = messages[index][
-                pl.ds(pl.multiple_of(attn_at + part * half, half), half), :
-            ]
-    total = matmul(attn_rows[...], grad_rows[...], COLS_T)
-    weights[...] = total
-    squares = jnp.sum(jnp.sum(total * total, axis=0, keepdims=True), axis=1, keepdims=True)
-    lanes = lax.broadcasted_iota(jnp.int32, stats.shape, 1)
-    stats[...] = jnp.where(lanes < HD // 2, squares, loss[...])
+    for index in range(groups):
+        first = index * latents
+        fill_rows(
+            grad_hidden, pl.multiple_of(first + mine * half, half), own_msgs[index], half
+        )
+        fill_rows(
+            grad_hidden, pl.multiple_of(first + (1 - mine) * half, half), pair_msgs[index], half
+        )
+    squares = jnp.zeros((8, total.shape[1]), jnp.float32)
+    for index in range(seqs):
+        part = matmul(attns[index][...], grad_hidden[...], COLS_T)
+        if index == 0:
+            total[...] = part
+        squares = squares + jnp.sum((part * part).reshape(HD // 8, 8, total.shape[1]), axis=0)
+    square_sum = jnp.sum(jnp.sum(squares, axis=0, keepdims=True), axis=1, keepdims=True)
+    update[...] = total[...] * lax.rsqrt(square_sum / entries + epsilon)
+    other_loss = jnp.sum(pair_msgs[0][-LOSS_ROWS:, :].astype(jnp.float32), axis=0, keepdims=True)
+    loss[...] = loss_half[...] + other_loss
 
 
 def body(hist_keys, hist_values, latent_queries, latent_pos, targets, out_proj, norm_gain, unembed):
@@ -374,7 +404,7 @@
     swap = [(i, i ^ 1) for i in range(n_seq)]
 
     (packed,) = kernel_call(
-        pack_kernel, [SMEM, VMEM, VMEM, VMEM], [((heads, span, HD), bf16)]
+        pack_kernel, [SMEM, VMEM, VMEM, VMEM], [((heads, span, HD), bf16, VMEM)], held=pltpu.HBM
     )(targets, seq_keys, hist_values[0], latent_queries[0])
     packed = lax.all_to_all(packed, "seq", 0, 0)
 
@@ -382,64 +412,61 @@
         partial(forward_kernel, tok=tok, own=own),
         [SMEM, VMEM, VMEM, VMEM],
         [
-            ((latents, HD), bf16),
-            ((latents, HD), f32),
-            ((half, HD), f32),
-            ((half, width), f32),
-            ((half, width), bf16),
+            ((latents, HD), bf16, KEPT),
+            ((latents, HD), f32, KEPT),
+            ((half, HD), f32, KEPT),
+            ((half, width), f32, KEPT),
+            ((half, width), bf16, KEPT),
         ],
         [pltpu.VMEM((latents, width), f32)],
     )(side, latent_pos, packed, out_proj)
     pair_sum = (kept + lax.ppermute(sent, "seq", swap).astype(f32)).astype(bf16)
-    parts = [pair_sum] + [
-        lax.ppermute(pair_sum, "seq", [(i, i ^ step) for i in range(n_seq)])
-        for step in range(2, n_seq, 2)
-    ]
-    message, loss = kernel_call(
+    chips = [[(i, i ^ step) for i in range(n_seq)] for step in range(2, n_seq, 2)]
+    shifts = [[(i, (i + step) % n_grp) for i in range(n_grp)] for step in range(1, n_grp)]
+    parts = [pair_sum] + [lax.ppermute(pair_sum, "seq", perm) for perm in chips]
+    attns = [attn] + [lax.ppermute(attn, "grp", perm) for perm in shifts]
+    loss_call = kernel_call(
         loss_kernel,
-        [VMEM] * (4 + len(parts)),
-        [((width // HD * half + latents, HD), bf16), ((1, HD), f32)],
-    )(norm_gain.reshape(1, width), unembed, onehot, attn, *parts)
+        [VMEM] * (3 + len(parts)),
+        [((width // HD * half + LOSS_ROWS, HD), bf16, KEPT), ((1, HD), f32, KEPT)],
+        flops=1 << 26,
+    )
+    message, loss_half = loss_call(norm_gain.reshape(1, width), unembed, onehot, *parts)
     pair_msg = lax.ppermute(message, "seq", swap)
-    others = [
-        lax.ppermute(message, "grp", [(i, (i + step) % n_grp) for i in range(n_grp)])
-        for step in range(1, n_grp)
-    ]
+    others = [lax.ppermute(message, "grp", perm) for perm in shifts]
+    stack = jnp.concatenate(attns, axis=0)
+    stacks = [stack] + [lax.ppermute(stack, "seq", perm) for perm in chips]
     backward = kernel_call(
         partial(backward_kernel, tok=tok, own=own),
         [SMEM] + [VMEM] * 7,
-        [((heads, span, HD), bf16)],
+        [((heads, span, HD), bf16, KEPT)],
         [pltpu.VMEM((latents, width), bf16)],
         flops=1 << 30,
     )
     (grads,) = backward(side, latent_pos, packed, out_proj, attn, log_norm, message, pair_msg)
     others = lax.optimization_barrier((*others, grads))[:-1]
     grads = lax.all_to_all(grads, "seq", 0, 0)
+    stacks = stacks + [lax.ppermute(one, "seq", swap) for one in stacks]
     pair_others = [lax.ppermute(other, "seq", swap) for other in others]
-    weights, stats = kernel_call(
-        partial(weight_kernel, count=n_grp),
-        [SMEM] + [VMEM] * (2 * n_grp + 1),
-        [((channels // n_seq, width), f32), ((1, HD), f32)],
+    proj_update, loss = kernel_call(
+        partial(weight_kernel, groups=n_grp, seqs=n_seq, entries=channels * width),
+        [SMEM] + [VMEM] * (2 * n_grp + n_seq + 1),
+        [((HD, width), f32, VMEM), ((1, HD), f32, VMEM)],
         [
-            pltpu.VMEM((n_grp * latents, HD), bf16),
             pltpu.VMEM((n_grp * latents, width), bf16),
+            pltpu.VMEM((HD, width), f32),
         ],
-    )(side, message, *others, pair_msg, *pair_others, loss)
+    )(side, message, *others, pair_msg, *pair_others, *stacks, loss_half)
     grad_queries, grad_keys, grad_values = kernel_call(
         unpack_kernel,
         [VMEM],
-        [((own, channels), bf16), ((tok, channels), bf16), ((tok, channels), bf16)],
-        on_chip=False,
+        [
+            ((own, channels), bf16, VMEM),
+            ((tok, channels), bf16, VMEM),
+            ((tok, channels), bf16, VMEM),
+        ],
     )(grads)
-    stats = stats + lax.ppermute(stats, "seq", swap)
-    received = [
-        lax.ppermute(stats, "seq", [(i, i ^ step) for i in range(n_seq)])
-        for step in range(2, n_seq, 2)
-    ]
-    received = lax.optimization_barrier((*received, grad_queries))[:-1]
-    totals = sum(received, stats)[0]
-    loss_sum = totals[HD - 1] / (n_seq // 2)
-    proj_update = weights * lax.rsqrt(totals[0] / (channels * width) + epsilon)
+    loss_sum = loss[0, 0]
     return (
         loss_sum.reshape(1),
         grad_queries[None],

time: 70.8 us -> 66.7 us (0.942)
  starting transfers between devices: 21.4 us -> 28.9 us
  waiting for transfers between devices: 34.5 us -> 27.8 us
  local copies, waits for them, and re-layouts: 3.87 us -> 0.04 us
  Pallas kernels: 6.21 us -> 8.81 us
  between operations: 3.19 us -> 0.74 us
  other arithmetic: 1.09 us -> 0.03 us
    ppermute x10 -> x16, starting transfers between devices: 11.9 us -> 19.4 us  [the longest x3 6.46 us: body(): stacks = [stack] + [lax.ppermute(stack, 'seq', perm) for perm in chips]]
    ppermute x10 -> x16, waiting for transfers between devices: 20.4 us -> 16.4 us  [the longest x3 7.69 us: body(): others = [lax.ppermute(message, 'grp', perm) for perm in shifts]]
    unnamed x16 -> x11, local copies, waits for them, and re-layouts: 3.28 us -> 0.04 us
    pallas_call x6, Pallas kernels: 6.21 us -> 8.81 us  [placed(): call(*(pltpu.with_memory_space_constraint(operand, held) if spec is VMEM...]
    ppermute x3, waiting for transfers between devices: 1.37 us -> 0.01 us  [body(): pair_others = [lax.ppermute(other, 'seq', swap) for other in others]]
    ppermute x1, waiting for transfers between devices: 1.36 us -> 0.01 us  [body(): pair_msg = lax.ppermute(message, 'seq', swap)]
    mul x1 -> x0, other arithmetic: 1.06 us -> none  [body(): proj_update = weights * lax.rsqrt(totals[0] / (channels * width) + epsilon)]
  transfers between devices with their start and end apart: 17 -> 23, of which waited for: 13 -> 8; matrix products, arithmetic and copies ran while one was open for 0% -> 0% of each run, Pallas kernels for 2% -> 7%
where the time goes in v3:
time: 66.7 us; the launch traced here: 66.4 us
  starting transfers between devices  28.9 us (43%)
  waiting for transfers between devices  27.8 us (42%)
  Pallas kernels  8.81 us (13%)
  between operations  0.74 us (1%)
    all_to_all x1, waiting for transfers between devices, body(): packed = lax.all_to_all(packed, 'seq', 0, 0)  10.1 us
    pallas_call x6, Pallas kernels, placed(): call(*(pltpu.with_memory_space_constraint(operand, held) if spec is VMEM...  8.81 us
    ppermute x3, waiting for transfers between devices, body(): others = [lax.ppermute(message, 'grp', perm) for perm in shifts]  7.69 us
    ppermute x3, starting transfers between devices, body(): stacks = [stack] + [lax.ppermute(stack, 'seq', perm) for perm in chips]  6.46 us
    all_to_all x1, starting transfers between devices, body(): packed = lax.all_to_all(packed, 'seq', 0, 0)  5.33 us
    ppermute x3, waiting for transfers between devices, body(): parts = [pair_sum] + [lax.ppermute(pair_sum, 'seq', perm) for perm in chips]  5.15 us
    ppermute x3, starting transfers between devices, body(): attns = [attn] + [lax.ppermute(attn, 'grp', perm) for perm in shifts]  4.67 us
    ppermute x3, starting transfers between devices, body(): others = [lax.ppermute(message, 'grp', perm) for perm in shifts]  4 us
  transfers between devices with their start and end apart: 23, of which 8 were waited for; matrix products, arithmetic and copies ran while one was open for 0% of the time, Pallas kernels for 7%

profile of v3, /device:TPU:0, one launch (start us, length us, event | category | flops | bytes accessed | tf_op | source)
XLA Modules:
  0.0 66.4 jit_solution(16992437816431600307)
XLA Ops:
  0.6 1.9 %shard_map.119 = bf16[8,272,128]{2,1,0:T(8,128)(2,1)} custom-call(s32[1,8]{1,0:T(1,128)} %targets.1, bf16[128,1024]{1,0:T(8,128)(2,1)} %bitcast.11, bf16[128,1024]{1,0:T(8,128)(2,1)} %bitcast.12, bf16[8,1024]{1,0:T(8,128)(2,1)} %bitcast.13), custom_call_target="tpu_custom_call" | custom-call | flops 1048576 | tf_op jit(solution)/shard_map/pallas_call | solution.py:180
  2.6 5.3 %all-to-all-start = ((bf16[8,272,128]{2,1,0:T(8,128)(2,1)}), bf16[8,272,128]{2,1,0:T(8,128)(2,1)S(1)}, u32[]{:S(2)}, u32[]{:S(2)}) async-start(bf16[8,272,128]{2,1,0:T(8,128)(2,1)} %shard_map.119), calls=%async_computation | async-start | bytes 1114112 | tf_op jit(solution)/shard_map/all_to_all | solution.py:409
  7.9 10.1 %all-to-all-done.packed = bf16[8,272,128]{2,1,0:T(8,128)(2,1)S(1)} async-done(((bf16[8,272,128]{2,1,0:T(8,128)(2,1)}), bf16[8,272,128]{2,1,0:T(8,128)(2,1)S(1)}, u32[]{:S(2)}, u32[]{:S(2)}) %all-to-all-start) | async-done | bytes 557088 | tf_op jit(solution)/shard_map/all_to_all | solution.py:409
  18.0 0.7 %shard_map.120 = (bf16[64,128]{1,0:T(8,128)(2,1)S(1)}, f32[64,128]{1,0:T(8,128)S(1)}, f32[32,128]{1,0:T(8,128)S(1)}, f32[32,2048]{1,0:T(8,128)S(1)}, bf16[32,2048]{1,0:T(8,128)(2,1)S(1)}) custom-call(s32[1]{0:T(128)} %bitcast.side, s32[1,64]{1,0:T(1,128)S(1)} %copy-done.3, bf16[8,272,128]{2,1,0:T(8,128)(2,1)S(1)} %all-to-all-done.packed, ...), custom_call_target="tpu_custom_call" | custom-call | flops 1048576 | tf_op jit(solution)/shard_map/pallas_call | solution.py:180
  18.8 1.3 %collective-permute-done = bf16[32,2048]{1,0:T(8,128)(2,1)S(1)} collective-permute-done((bf16[32,2048]{1,0:T(8,128)(2,1)S(1)}, bf16[32,2048]{1,0:T(8,128)(2,1)S(1)}, u32[]{:S(2)}, u32[]{:S(2)}) %collective-permute-start) | collective-permute-done | bytes 131104 | tf_op jit(solution)/shard_map/ppermute | solution.py:423
  20.8 1.5 %collective-permute-start.2 = (bf16[32,2048]{1,0:T(8,128)(2,1)S(1)}, bf16[32,2048]{1,0:T(8,128)(2,1)S(1)}, u32[]{:S(2)}, u32[]{:S(2)}) collective-permute-start(bf16[32,2048]{1,0:T(8,128)(2,1)S(1)} %add_convert_fusion.refs_0_), channel_id=1, source_target_pairs={{0,4},{1,5},{2,6},{3,7},{4,0},{5,1},{6,2},{7,3},{8,12},{9,13},{10,... | collective-permute-start | bytes 393224 | tf_op jit(solution)/shard_map/ppermute | solution.py:426
  22.2 1.5 %collective-permute-start.1 = (bf16[32,2048]{1,0:T(8,128)(2,1)S(1)}, bf16[32,2048]{1,0:T(8,128)(2,1)S(1)}, u32[]{:S(2)}, u32[]{:S(2)}) collective-permute-start(bf16[32,2048]{1,0:T(8,128)(2,1)S(1)} %add_convert_fusion.refs_0_), channel_id=1, source_target_pairs={{0,2},{1,3},{2,0},{3,1},{4,6},{5,7},{6,4},{7,5},{8,10},{9,11},{10,... | collective-permute-start | bytes 393224 | tf_op jit(solution)/shard_map/ppermute | solution.py:426
  23.7 3.8 %collective-permute-done.3.refs_3_ = bf16[32,2048]{1,0:T(8,128)(2,1)S(1)} collective-permute-done((bf16[32,2048]{1,0:T(8,128)(2,1)S(1)}, bf16[32,2048]{1,0:T(8,128)(2,1)S(1)}, u32[]{:S(2)}, u32[]{:S(2)}) %collective-permute-start.3) | collective-permute-done | bytes 131104 | tf_op jit(solution)/shard_map/ppermute | solution.py:426
  27.5 1.3 %collective-permute-done.2.refs_2_ = bf16[32,2048]{1,0:T(8,128)(2,1)S(1)} collective-permute-done((bf16[32,2048]{1,0:T(8,128)(2,1)S(1)}, bf16[32,2048]{1,0:T(8,128)(2,1)S(1)}, u32[]{:S(2)}, u32[]{:S(2)}) %collective-permute-start.2) | collective-permute-done | bytes 131104 | tf_op jit(solution)/shard_map/ppermute | solution.py:426
  28.9 0.9 %shard_map.121 = (bf16[528,128]{1,0:T(8,128)(2,1)S(1)}, f32[1,128]{1,0:T(1,128)S(1)}) custom-call(f32[1,2048]{1,0:T(1,128)S(1)} %bitcast.10, bf16[2048,128]{1,0:T(8,128)(2,1)S(1)} %copy-done.1, f32[32,128]{1,0:T(8,128)S(1)} %get-tuple-element.20.onehot_ref, bf16[32,2048]{1,0:T(8,128)(2,1)S(1)} %add_convert_fusion.refs_0_, ...), custom_call_target="tpu_custom_call" | custom-call | flops 67108864 | tf_op jit(solution)/shard_map/pallas_call | solution.py:180
  29.8 3.7 %collective-permute-start.13 = (bf16[64,128]{1,0:T(8,128)(2,1)S(1)}, bf16[64,128]{1,0:T(8,128)(2,1)S(1)}, u32[]{:S(2)}, u32[]{:S(2)}) collective-permute-start(bf16[64,128]{1,0:T(8,128)(2,1)S(1)} %get-tuple-element.24.attn), channel_id=1, source_target_pairs={{0,24},{8,0},{16,8},{24,16},{1,25},{9,1},{17,9},{25,17},{2,26},{10... | collective-permute-start | bytes 49160 | tf_op jit(solution)/shard_map/ppermute | solution.py:427
  33.5 1.0 %collective-permute-start.11 = (bf16[64,128]{1,0:T(8,128)(2,1)S(1)}, bf16[64,128]{1,0:T(8,128)(2,1)S(1)}, u32[]{:S(2)}, u32[]{:S(2)}) collective-permute-start(bf16[64,128]{1,0:T(8,128)(2,1)S(1)} %get-tuple-element.24.attn), channel_id=1, source_target_pairs={{0,8},{8,16},{16,24},{24,0},{1,9},{9,17},{17,25},{25,1},{2,10},{10... | collective-permute-start | bytes 49160 | tf_op jit(solution)/shard_map/ppermute | solution.py:427
  34.5 1.7 %shard_map.122 = bf16[8,272,128]{2,1,0:T(8,128)(2,1)} custom-call(s32[1]{0:T(128)} %bitcast.side, s32[1,64]{1,0:T(1,128)S(1)} %copy-done.3, bf16[8,272,128]{2,1,0:T(8,128)(2,1)S(1)} %all-to-all-done.packed, bf16[128,2048]{1,0:T(8,128)(2,1)S(1)} %copy-done, bf16[64,128]{1,0:T(8,128)(2,1)S(1)} %get-tuple-element.24.attn, ...), custom_call_target="tpu_custom_call" | custom-call | flops 1073741824 | tf_op jit(solution)/shard_map/pallas_call | solution.py:180
  36.2 3.5 %all-to-all-start.1 = ((bf16[8,272,128]{2,1,0:T(8,128)(2,1)}), bf16[8,272,128]{2,1,0:T(8,128)(2,1)S(1)}, u32[]{:S(2)}, u32[]{:S(2)}) async-start(bf16[8,272,128]{2,1,0:T(8,128)(2,1)} %shard_map.122), calls=%async_computation.1 | async-start | bytes 1114112 | tf_op jit(solution)/shard_map/all_to_all | solution.py:448
  39.8 2.9 %collective-permute-start.6 = (bf16[528,128]{1,0:T(8,128)(2,1)S(1)}, bf16[528,128]{1,0:T(8,128)(2,1)S(1)}, u32[]{:S(2)}, u32[]{:S(2)}) collective-permute-start(bf16[528,128]{1,0:T(8,128)(2,1)S(1)} %get-tuple-element.23.own_msg.refs_0_), channel_id=1, source_target_pairs={{0,24},{8,0},{16,8},{24,16},{1,25},{9,1},{17,9},{25,17},{2,26},{10... | collective-permute-start | bytes 405512 | tf_op jit(solution)/shard_map/ppermute | solution.py:436
  42.7 1.1 %collective-permute-start.5 = (bf16[528,128]{1,0:T(8,128)(2,1)S(1)}, bf16[528,128]{1,0:T(8,128)(2,1)S(1)}, u32[]{:S(2)}, u32[]{:S(2)}) collective-permute-start(bf16[528,128]{1,0:T(8,128)(2,1)S(1)} %get-tuple-element.23.own_msg.refs_0_), channel_id=1, source_target_pairs={{0,16},{8,24},{16,0},{24,8},{1,17},{9,25},{17,1},{25,9},{2,18},{10... | collective-permute-start | bytes 405512 | tf_op jit(solution)/shard_map/ppermute | solution.py:436
  43.9 2.9 %collective-permute-start.16 = (bf16[256,128]{1,0:T(8,128)(2,1)S(1)}, bf16[256,128]{1,0:T(8,128)(2,1)S(1)}, u32[]{:S(2)}, u32[]{:S(2)}) collective-permute-start(bf16[256,128]{1,0:T(8,128)(2,1)S(1)} %constant_dynamic-update-slice_fusion.refs_8_), channel_id=1, source_target_pairs={{0,6},{1,7},{2,4},{3,5},{4,2},{5,3},{6,0},{7,1},{8,14},{9,15},{10,... | collective-permute-start | bytes 196616 | tf_op jit(solution)/shard_map/ppermute | solution.py:438
  46.8 1.8 %collective-permute-start.15 = (bf16[256,128]{1,0:T(8,128)(2,1)S(1)}, bf16[256,128]{1,0:T(8,128)(2,1)S(1)}, u32[]{:S(2)}, u32[]{:S(2)}) collective-permute-start(bf16[256,128]{1,0:T(8,128)(2,1)S(1)} %constant_dynamic-update-slice_fusion.refs_8_), channel_id=1, source_target_pairs={{0,4},{1,5},{2,6},{3,7},{4,0},{5,1},{6,2},{7,3},{8,12},{9,13},{10,... | collective-permute-start | bytes 196616 | tf_op jit(solution)/shard_map/ppermute | solution.py:438
  48.7 7.7 %collective-permute-done.5.refs_2_ = bf16[528,128]{1,0:T(8,128)(2,1)S(1)} collective-permute-done((bf16[528,128]{1,0:T(8,128)(2,1)S(1)}, bf16[528,128]{1,0:T(8,128)(2,1)S(1)}, u32[]{:S(2)}, u32[]{:S(2)}) %collective-permute-start.5) | collective-permute-done | bytes 135200 | tf_op jit(solution)/shard_map/ppermute | solution.py:436
  56.9 1.7 %collective-permute-start.14 = (bf16[256,128]{1,0:T(8,128)(2,1)S(1)}, bf16[256,128]{1,0:T(8,128)(2,1)S(1)}, u32[]{:S(2)}, u32[]{:S(2)}) collective-permute-start(bf16[256,128]{1,0:T(8,128)(2,1)S(1)} %constant_dynamic-update-slice_fusion.refs_8_), channel_id=1, source_target_pairs={{0,2},{1,3},{2,0},{3,1},{4,6},{5,7},{6,4},{7,5},{8,10},{9,11},{10,... | collective-permute-start | bytes 196616 | tf_op jit(solution)/shard_map/ppermute | solution.py:438
  58.7 2.6 %collective-permute-done.14.refs_9_ = bf16[256,128]{1,0:T(8,128)(2,1)S(1)} collective-permute-done((bf16[256,128]{1,0:T(8,128)(2,1)S(1)}, bf16[256,128]{1,0:T(8,128)(2,1)S(1)}, u32[]{:S(2)}, u32[]{:S(2)}) %collective-permute-start.14) | collective-permute-done | bytes 65568 | tf_op jit(solution)/shard_map/ppermute | solution.py:438
  61.9 0.7 %collective-permute-done.19.refs_14_ = bf16[256,128]{1,0:T(8,128)(2,1)S(1)} collective-permute-done((bf16[256,128]{1,0:T(8,128)(2,1)S(1)}, bf16[256,128]{1,0:T(8,128)(2,1)S(1)}, u32[]{:S(2)}, u32[]{:S(2)}) %collective-permute-start.19) | collective-permute-done | bytes 65568 | tf_op jit(solution)/shard_map/ppermute | solution.py:449
  62.8 2.6 %shard_map.123 = (f32[128,2048]{1,0:T(8,128)}, f32[1,128]{1,0:T(1,128)}) custom-call(s32[1]{0:T(128)} %bitcast.side, bf16[528,128]{1,0:T(8,128)(2,1)S(1)} %get-tuple-element.23.own_msg.refs_0_, bf16[528,128]{1,0:T(8,128)(2,1)S(1)} %collective-permute-done.4.refs_1_, bf16[528,128]{1,0:T(8,128)(2,1)S(1)} %collective-permute-done.5.refs_2_, ...), custom_call_target="tpu_custom_call" | custom-call | flops 1048576 | tf_op jit(solution)/shard_map/pallas_call | solution.py:180
  65.4 0.9 %shard_map.124 = (bf16[8,1024]{1,0:T(8,128)(2,1)}, bf16[128,1024]{1,0:T(8,128)(2,1)}, bf16[128,1024]{1,0:T(8,128)(2,1)}) custom-call(bf16[8,272,128]{2,1,0:T(8,128)(2,1)S(1)} %all-to-all-done.1.packed), custom_call_target="tpu_custom_call" | custom-call | flops 1048576 | tf_op jit(solution)/shard_map/pallas_call | solution.py:180
  (41 shorter events, 2.3 us)
Async XLA Ops:
  2.6 15.4 %copy-start = (bf16[128,2048]{1,0:T(8,128)(2,1)S(1)}, bf16[128,2048]{1,0:T(8,128)(2,1)}, u32[]{:S(2)}) copy-start(bf16[128,2048]{1,0:T(8,128)(2,1)} %out_proj.3) | copy-start | bytes 1572868
  2.6 15.4 %all-to-all-start = ((bf16[8,272,128]{2,1,0:T(8,128)(2,1)}), bf16[8,272,128]{2,1,0:T(8,128)(2,1)S(1)}, u32[]{:S(2)}, u32[]{:S(2)}) async-start(bf16[8,272,128]{2,1,0:T(8,128)(2,1)} %shard_map.119), calls=%async_computation | async-start | bytes 1114112 | tf_op jit(solution)/shard_map/all_to_all | solution.py:409
  18.7 1.4 %collective-permute-start = (bf16[32,2048]{1,0:T(8,128)(2,1)S(1)}, bf16[32,2048]{1,0:T(8,128)(2,1)S(1)}, u32[]{:S(2)}, u32[]{:S(2)}) collective-permute-start(bf16[32,2048]{1,0:T(8,128)(2,1)S(1)} %get-tuple-element.22), channel_id=1, source_target_pairs={{0,1},{1,0},{2,3},{3,2},{4,5},{5,4},{6,7},{7,6},{8,9},{9,8},{10,11... | collective-permute-start | bytes 393224 | tf_op jit(solution)/shard_map/ppermute | solution.py:423
  20.1 7.4 %collective-permute-start.3 = (bf16[32,2048]{1,0:T(8,128)(2,1)S(1)}, bf16[32,2048]{1,0:T(8,128)(2,1)S(1)}, u32[]{:S(2)}, u32[]{:S(2)}) collective-permute-start(bf16[32,2048]{1,0:T(8,128)(2,1)S(1)} %add_convert_fusion.refs_0_), channel_id=1, source_target_pairs={{0,6},{1,7},{2,4},{3,5},{4,2},{5,3},{6,0},{7,1},{8,14},{9,15},{10,... | collective-permute-start | bytes 393224 | tf_op jit(solution)/shard_map/ppermute | solution.py:426
  20.8 8.1 %collective-permute-start.2 = (bf16[32,2048]{1,0:T(8,128)(2,1)S(1)}, bf16[32,2048]{1,0:T(8,128)(2,1)S(1)}, u32[]{:S(2)}, u32[]{:S(2)}) collective-permute-start(bf16[32,2048]{1,0:T(8,128)(2,1)S(1)} %add_convert_fusion.refs_0_), channel_id=1, source_target_pairs={{0,4},{1,5},{2,6},{3,7},{4,0},{5,1},{6,2},{7,3},{8,12},{9,13},{10,... | collective-permute-start | bytes 393224 | tf_op jit(solution)/shard_map/ppermute | solution.py:426
  22.2 6.6 %collective-permute-start.1 = (bf16[32,2048]{1,0:T(8,128)(2,1)S(1)}, bf16[32,2048]{1,0:T(8,128)(2,1)S(1)}, u32[]{:S(2)}, u32[]{:S(2)}) collective-permute-start(bf16[32,2048]{1,0:T(8,128)(2,1)S(1)} %add_convert_fusion.refs_0_), channel_id=1, source_target_pairs={{0,2},{1,3},{2,0},{3,1},{4,6},{5,7},{6,4},{7,5},{8,10},{9,11},{10,... | collective-permute-start | bytes 393224 | tf_op jit(solution)/shard_map/ppermute | solution.py:426
  29.7 4.8 %collective-permute-start.7 = (bf16[528,128]{1,0:T(8,128)(2,1)S(1)}, bf16[528,128]{1,0:T(8,128)(2,1)S(1)}, u32[]{:S(2)}, u32[]{:S(2)}) collective-permute-start(bf16[528,128]{1,0:T(8,128)(2,1)S(1)} %get-tuple-element.23.own_msg.refs_0_), channel_id=1, source_target_pairs={{0,1},{1,0},{2,3},{3,2},{4,5},{5,4},{6,7},{7,6},{8,9},{9,8},{10,11... | collective-permute-start | bytes 405512 | tf_op jit(solution)/shard_map/ppermute | solution.py:435
  29.8 14.0 %collective-permute-start.13 = (bf16[64,128]{1,0:T(8,128)(2,1)S(1)}, bf16[64,128]{1,0:T(8,128)(2,1)S(1)}, u32[]{:S(2)}, u32[]{:S(2)}) collective-permute-start(bf16[64,128]{1,0:T(8,128)(2,1)S(1)} %get-tuple-element.24.attn), channel_id=1, source_target_pairs={{0,24},{8,0},{16,8},{24,16},{1,25},{9,1},{17,9},{25,17},{2,26},{10... | collective-permute-start | bytes 49160 | tf_op jit(solution)/shard_map/ppermute | solution.py:427
  33.5 9.2 %collective-permute-start.12 = (bf16[64,128]{1,0:T(8,128)(2,1)S(1)}, bf16[64,128]{1,0:T(8,128)(2,1)S(1)}, u32[]{:S(2)}, u32[]{:S(2)}) collective-permute-start(bf16[64,128]{1,0:T(8,128)(2,1)S(1)} %get-tuple-element.24.attn), channel_id=1, source_target_pairs={{0,16},{8,24},{16,0},{24,8},{1,17},{9,25},{17,1},{25,9},{2,18},{10... | collective-permute-start | bytes 49160 | tf_op jit(solution)/shard_map/ppermute | solution.py:427
  33.5 6.3 %collective-permute-start.11 = (bf16[64,128]{1,0:T(8,128)(2,1)S(1)}, bf16[64,128]{1,0:T(8,128)(2,1)S(1)}, u32[]{:S(2)}, u32[]{:S(2)}) collective-permute-start(bf16[64,128]{1,0:T(8,128)(2,1)S(1)} %get-tuple-element.24.attn), channel_id=1, source_target_pairs={{0,8},{8,16},{16,24},{24,0},{1,9},{9,17},{17,25},{25,1},{2,10},{10... | collective-permute-start | bytes 49160 | tf_op jit(solution)/shard_map/ppermute | solution.py:427
  36.2 29.2 %all-to-all-start.1 = ((bf16[8,272,128]{2,1,0:T(8,128)(2,1)}), bf16[8,272,128]{2,1,0:T(8,128)(2,1)S(1)}, u32[]{:S(2)}, u32[]{:S(2)}) async-start(bf16[8,272,128]{2,1,0:T(8,128)(2,1)} %shard_map.122), calls=%async_computation.1 | async-start | bytes 1114112 | tf_op jit(solution)/shard_map/all_to_all | solution.py:448
  39.8 7.0 %collective-permute-start.6 = (bf16[528,128]{1,0:T(8,128)(2,1)S(1)}, bf16[528,128]{1,0:T(8,128)(2,1)S(1)}, u32[]{:S(2)}, u32[]{:S(2)}) collective-permute-start(bf16[528,128]{1,0:T(8,128)(2,1)S(1)} %get-tuple-element.23.own_msg.refs_0_), channel_id=1, source_target_pairs={{0,24},{8,0},{16,8},{24,16},{1,25},{9,1},{17,9},{25,17},{2,26},{10... | collective-permute-start | bytes 405512 | tf_op jit(solution)/shard_map/ppermute | solution.py:436
  42.7 13.7 %collective-permute-start.5 = (bf16[528,128]{1,0:T(8,128)(2,1)S(1)}, bf16[528,128]{1,0:T(8,128)(2,1)S(1)}, u32[]{:S(2)}, u32[]{:S(2)}) collective-permute-start(bf16[528,128]{1,0:T(8,128)(2,1)S(1)} %get-tuple-element.23.own_msg.refs_0_), channel_id=1, source_target_pairs={{0,16},{8,24},{16,0},{24,8},{1,17},{9,25},{17,1},{25,9},{2,18},{10... | collective-permute-start | bytes 405512 | tf_op jit(solution)/shard_map/ppermute | solution.py:436
  43.8 12.5 %collective-permute-start.4 = (bf16[528,128]{1,0:T(8,128)(2,1)S(1)}, bf16[528,128]{1,0:T(8,128)(2,1)S(1)}, u32[]{:S(2)}, u32[]{:S(2)}) collective-permute-start(bf16[528,128]{1,0:T(8,128)(2,1)S(1)} %get-tuple-element.23.own_msg.refs_0_), channel_id=1, source_target_pairs={{0,8},{8,16},{16,24},{24,0},{1,9},{9,17},{17,25},{25,1},{2,10},{10... | collective-permute-start | bytes 405512 | tf_op jit(solution)/shard_map/ppermute | solution.py:436
  43.8 13.0 %collective-permute-start.17 = (bf16[256,128]{1,0:T(8,128)(2,1)S(1)}, bf16[256,128]{1,0:T(8,128)(2,1)S(1)}, u32[]{:S(2)}, u32[]{:S(2)}) collective-permute-start(bf16[256,128]{1,0:T(8,128)(2,1)S(1)} %constant_dynamic-update-slice_fusion.refs_8_), channel_id=1, source_target_pairs={{0,1},{1,0},{2,3},{3,2},{4,5},{5,4},{6,7},{7,6},{8,9},{9,8},{10,11... | collective-permute-start | bytes 196616 | tf_op jit(solution)/shard_map/ppermute | solution.py:449
  43.9 13.0 %collective-permute-start.16 = (bf16[256,128]{1,0:T(8,128)(2,1)S(1)}, bf16[256,128]{1,0:T(8,128)(2,1)S(1)}, u32[]{:S(2)}, u32[]{:S(2)}) collective-permute-start(bf16[256,128]{1,0:T(8,128)(2,1)S(1)} %constant_dynamic-update-slice_fusion.refs_8_), channel_id=1, source_target_pairs={{0,6},{1,7},{2,4},{3,5},{4,2},{5,3},{6,0},{7,1},{8,14},{9,15},{10,... | collective-permute-start | bytes 196616 | tf_op jit(solution)/shard_map/ppermute | solution.py:438
  46.8 11.8 %collective-permute-start.15 = (bf16[256,128]{1,0:T(8,128)(2,1)S(1)}, bf16[256,128]{1,0:T(8,128)(2,1)S(1)}, u32[]{:S(2)}, u32[]{:S(2)}) collective-permute-start(bf16[256,128]{1,0:T(8,128)(2,1)S(1)} %constant_dynamic-update-slice_fusion.refs_8_), channel_id=1, source_target_pairs={{0,4},{1,5},{2,6},{3,7},{4,0},{5,1},{6,2},{7,3},{8,12},{9,13},{10,... | collective-permute-start | bytes 196616 | tf_op jit(solution)/shard_map/ppermute | solution.py:438
  56.3 6.4 %collective-permute-start.8 = (bf16[528,128]{1,0:T(8,128)(2,1)S(1)}, bf16[528,128]{1,0:T(8,128)(2,1)S(1)}, u32[]{:S(2)}, u32[]{:S(2)}) collective-permute-start(bf16[528,128]{1,0:T(8,128)(2,1)S(1)} %collective-permute-done.4.refs_1_), channel_id=1, source_target_pairs={{0,1},{1,0},{2,3},{3,2},{4,5},{5,4},{6,7},{7,6},{8,9},{9,8},{10,11... | collective-permute-start | bytes 405512 | tf_op jit(solution)/shard_map/ppermute | solution.py:450
  56.3 6.4 %collective-permute-start.9 = (bf16[528,128]{1,0:T(8,128)(2,1)S(1)}, bf16[528,128]{1,0:T(8,128)(2,1)S(1)}, u32[]{:S(2)}, u32[]{:S(2)}) collective-permute-start(bf16[528,128]{1,0:T(8,128)(2,1)S(1)} %collective-permute-done.5.refs_2_), channel_id=1, source_target_pairs={{0,1},{1,0},{2,3},{3,2},{4,5},{5,4},{6,7},{7,6},{8,9},{9,8},{10,11... | collective-permute-start | bytes 405512 | tf_op jit(solution)/shard_map/ppermute | solution.py:450
  56.9 5.9 %collective-permute-start.10 = (bf16[528,128]{1,0:T(8,128)(2,1)S(1)}, bf16[528,128]{1,0:T(8,128)(2,1)S(1)}, u32[]{:S(2)}, u32[]{:S(2)}) collective-permute-start(bf16[528,128]{1,0:T(8,128)(2,1)S(1)} %collective-permute-done.6.refs_3_), channel_id=1, source_target_pairs={{0,1},{1,0},{2,3},{3,2},{4,5},{5,4},{6,7},{7,6},{8,9},{9,8},{10,11... | collective-permute-start | bytes 405512 | tf_op jit(solution)/shard_map/ppermute | solution.py:450
  56.9 4.5 %collective-permute-start.14 = (bf16[256,128]{1,0:T(8,128)(2,1)S(1)}, bf16[256,128]{1,0:T(8,128)(2,1)S(1)}, u32[]{:S(2)}, u32[]{:S(2)}) collective-permute-start(bf16[256,128]{1,0:T(8,128)(2,1)S(1)} %constant_dynamic-update-slice_fusion.refs_8_), channel_id=1, source_target_pairs={{0,2},{1,3},{2,0},{3,1},{4,6},{5,7},{6,4},{7,5},{8,10},{9,11},{10,... | collective-permute-start | bytes 196616 | tf_op jit(solution)/shard_map/ppermute | solution.py:438
  58.6 2.8 %collective-permute-start.20 = (bf16[256,128]{1,0:T(8,128)(2,1)S(1)}, bf16[256,128]{1,0:T(8,128)(2,1)S(1)}, u32[]{:S(2)}, u32[]{:S(2)}) collective-permute-start(bf16[256,128]{1,0:T(8,128)(2,1)S(1)} %collective-permute-done.16.refs_11_), channel_id=1, source_target_pairs={{0,1},{1,0},{2,3},{3,2},{4,5},{5,4},{6,7},{7,6},{8,9},{9,8},{10,11... | collective-permute-start | bytes 196616 | tf_op jit(solution)/shard_map/ppermute | solution.py:449
  61.4 1.3 %collective-permute-start.19 = (bf16[256,128]{1,0:T(8,128)(2,1)S(1)}, bf16[256,128]{1,0:T(8,128)(2,1)S(1)}, u32[]{:S(2)}, u32[]{:S(2)}) collective-permute-start(bf16[256,128]{1,0:T(8,128)(2,1)S(1)} %collective-permute-done.15.refs_10_), channel_id=1, source_target_pairs={{0,1},{1,0},{2,3},{3,2},{4,5},{5,4},{6,7},{7,6},{8,9},{9,8},{10,11... | collective-permute-start | bytes 196616 | tf_op jit(solution)/shard_map/ppermute | solution.py:449
  61.4 1.4 %collective-permute-start.18 = (bf16[256,128]{1,0:T(8,128)(2,1)S(1)}, bf16[256,128]{1,0:T(8,128)(2,1)S(1)}, u32[]{:S(2)}, u32[]{:S(2)}) collective-permute-start(bf16[256,128]{1,0:T(8,128)(2,1)S(1)} %collective-permute-done.14.refs_9_), channel_id=1, source_target_pairs={{0,1},{1,0},{2,3},{3,2},{4,5},{5,4},{6,7},{7,6},{8,9},{9,8},{10,11... | collective-permute-start | bytes 196616 | tf_op jit(solution)/shard_map/ppermute | solution.py:449
  (3 other events, 31.1 us)

commit v4 on v3

--- a/solution.py
+++ b/solution.py
@@ -153,6 +153,7 @@
 SMEM = pl.BlockSpec(memory_space=pltpu.SMEM)
 KEPT = object()
 LOSS_ROWS = 16
+TILE = 256
 VMEM_LIMIT = 16 << 20
 ROWS_T = (((1,), (1,)), ((), ()))
 COLS_T = (((0,), (0,)), ((), ()))
@@ -189,8 +190,15 @@
     return placed
 
 
-def pack_kernel(targets, keys, values, queries, packed):
-    heads = packed.shape[0]
+def head_cols(place, step):
+    return pl.ds(pl.multiple_of((place[0] ^ step) * HD, HD), HD)
+
+
+def pair_of(place, step):
+    return (place[0] // 2 ^ step) * 2
+
+
+def pack_kernel(place, targets, keys, values, queries, *pieces):
     tok = keys.shape[0]
     own = queries.shape[0]
     lanes = lax.broadcasted_iota(jnp.int32, (own, HD), 1)
@@ -199,12 +207,12 @@
     for row in range(own):
         wanted = jnp.where(rows == row, targets[0, row], wanted)
     onehot = (lanes == wanted).astype(jnp.float32)
-    for head in range(heads):
-        cols = slice(head * HD, (head + 1) * HD)
-        packed[head, 0:tok, :] = keys[:, cols]
-        packed[head, tok : 2 * tok, :] = values[:, cols]
+    for step, piece in enumerate(pieces):
+        cols = head_cols(place, step)
+        piece[0:tok, :] = keys[:, cols]
+        piece[tok : 2 * tok, :] = values[:, cols]
         tail = jnp.concatenate([queries[:, cols].astype(jnp.float32), onehot], axis=0)
-        packed[head, 2 * tok : 2 * tok + 2 * own, :] = tail.astype(jnp.bfloat16)
+        piece[2 * tok : 2 * tok + 2 * own, :] = tail.astype(jnp.bfloat16)
 
 
 def split_packed(packed, tok, own):
@@ -229,7 +237,11 @@
     return scores, places <= last
 
 
-def forward_kernel(side, positions, packed, out_proj, attn, log_norm, onehot, kept, sent, hidden, *, tok, own):
+def forward_kernel(place, positions, out_proj, gain, unembed, *refs, tok, own, count):
+    pieces = refs[:count]
+    packed, attn, log_norm, onehot, kept, sent, hidden = refs[count:]
+    for step, piece in enumerate(pieces):
+        packed[place[0] ^ step] = piece[...]
     keys, values, queries = split_packed(packed, tok, own)
     scores, visible = visible_scores(keys, queries, positions)
     best = jnp.max(jnp.where(visible, scores, -1e30), axis=-1, keepdims=True)
@@ -239,7 +251,7 @@
     attn[...] = (summed / denom).astype(jnp.bfloat16)
     log_norm[...] = jnp.broadcast_to(best + jnp.log(denom), log_norm.shape)
     half = kept.shape[0]
-    mine = side[0]
+    mine = place[0] & 1
     pieces = half // own
     onehot[...] = (
         packed[pl.ds(mine * pieces, pieces), 2 * tok + own : 2 * tok + 2 * own, :]
@@ -296,7 +308,7 @@
 
 
 def backward_kernel(
-    side,
+    place,
     positions,
     packed,
     out_proj,
@@ -304,14 +316,13 @@
     log_norm,
     own_msg,
     pair_msg,
-    grads,
-    grad_hidden,
-    *,
+    *refs,
     tok,
     own,
 ):
+    *messages, grads, grad_hidden = refs
     half = grad_hidden.shape[0] // 2
-    mine = side[0]
+    mine = place[0] & 1
     fill_rows(grad_hidden, pl.multiple_of(mine * half, half), own_msg, half)
     fill_rows(grad_hidden, pl.multiple_of((1 - mine) * half, half), pair_msg, half)
     keys, values, queries = split_packed(packed, tok, own)
@@ -334,27 +345,45 @@
     grads[:, 2 * tok : 2 * tok + 2 * own, :] = jnp.concatenate([tail, tail], axis=1).astype(
         jnp.bfloat16
     )
-
-
-def unpack_kernel(packed, grad_queries, grad_keys, grad_values):
-    heads = packed.shape[0]
+    for step, message in enumerate(messages):
+        message[...] = grads[pl.ds(pair_of(place, step), 2)]
+
+
+def unpack_kernel(place, *refs):
+    *messages, grad_queries, grad_keys, grad_values = refs
     tok = grad_keys.shape[0]
     own = grad_queries.shape[0]
-    for head in range(heads):
-        cols = slice(head * HD, (head + 1) * HD)
-        grad_keys[:, cols] = packed[head, 0:tok, :]
-        grad_values[:, cols] = packed[head, tok : 2 * tok, :]
-        grad_queries[:, cols] = packed[head, 2 * tok : 2 * tok + own, :]
-
-
-def weight_kernel(side, *refs, groups, seqs, entries):
+    mine = place[0] & 1
+    for index, message in enumerate(messages):
+        pairs, side = index % (len(messages) // 2), index // (len(messages) // 2)
+        source = pair_of(place, pairs) + (mine ^ side)
+        cols = pl.ds(pl.multiple_of(source * HD, HD), HD)
+        grad_keys[:, cols] = message[mine, 0:tok, :]
+        grad_values[:, cols] = message[mine, tok : 2 * tok, :]
+        grad_queries[:, cols] = message[mine, 2 * tok : 2 * tok + own, :]
+
+
+def stack_kernel(*refs):
+    *parts, stack = refs
+    rows = parts[0].shape[0]
+    for index, part in enumerate(parts):
+        stack[index * rows : (index + 1) * rows, :] = part[...]
+
+
+def total_kernel(loss_half, pair_msg, loss):
+    other = pair_msg[pair_msg.shape[0] - LOSS_ROWS :, :].astype(jnp.float32)
+    loss[...] = loss_half[...] + jnp.sum(other, axis=0, keepdims=True)
+
+
+def weight_kernel(place, *refs, groups, seqs, entries):
     own_msgs = refs[:groups]
     pair_msgs = refs[groups : 2 * groups]
     attns = refs[2 * groups : 2 * groups + seqs]
-    loss_half, update, loss, grad_hidden, total = refs[2 * groups + seqs :]
+    loss_in, update, loss, grad_hidden, attn_cols, total = refs[2 * groups + seqs :]
+    loss[...] = loss_in[...]
     latents = grad_hidden.shape[0] // groups
     half = latents // 2
-    mine = side[0]
+    mine = place[0] & 1
     for index in range(groups):
         first = index * latents
         fill_rows(
@@ -363,16 +392,16 @@
         fill_rows(
             grad_hidden, pl.multiple_of(first + (1 - mine) * half, half), pair_msgs[index], half
         )
-    squares = jnp.zeros((8, total.shape[1]), jnp.float32)
     for index in range(seqs):
-        part = matmul(attns[index][...], grad_hidden[...], COLS_T)
-        if index == 0:
-            total[...] = part
-        squares = squares + jnp.sum((part * part).reshape(HD // 8, 8, total.shape[1]), axis=0)
+        attn_cols[index * HD : (index + 1) * HD, :] = attns[index][...].T
+    squares = jnp.zeros((8, TILE), jnp.float32)
+    for tile in range(total.shape[1] // TILE):
+        cols = slice(tile * TILE, (tile + 1) * TILE)
+        part = matmul(attn_cols[...], grad_hidden[:, cols])
+        total[:, cols] = part[0:HD]
+        squares = squares + jnp.sum((part * part).reshape(seqs * HD // 8, 8, TILE), axis=0)
     square_sum = jnp.sum(jnp.sum(squares, axis=0, keepdims=True), axis=1, keepdims=True)
     update[...] = total[...] * lax.rsqrt(square_sum / entries + epsilon)
-    other_loss = jnp.sum(pair_msgs[0][-LOSS_ROWS:, :].astype(jnp.float32), axis=0, keepdims=True)
-    loss[...] = loss_half[...] + other_loss
 
 
 def body(hist_keys, hist_values, latent_queries, latent_pos, targets, out_proj, norm_gain, unembed):
@@ -391,6 +420,7 @@
         and tok % 16 == 0
         and own == 8
         and n_seq & (n_seq - 1) == 0
+        and n_grp & (n_grp - 1) == 0
         and n_seq > 1
     ):
         return general_body(
@@ -400,18 +430,26 @@
     half = latents // 2
     width = out_proj.shape[1]
     span = 2 * tok + 2 * own
-    side = (lax.axis_index("seq") % 2).reshape(1)
+    place = lax.axis_index("seq").reshape(1)
+    steps = [[(i, i ^ step) for i in range(n_seq)] for step in range(1, n_seq)]
     swap = [(i, i ^ 1) for i in range(n_seq)]
 
-    (packed,) = kernel_call(
-        pack_kernel, [SMEM, VMEM, VMEM, VMEM], [((heads, span, HD), bf16, VMEM)], held=pltpu.HBM
-    )(targets, seq_keys, hist_values[0], latent_queries[0])
-    packed = lax.all_to_all(packed, "seq", 0, 0)
-
-    attn, log_norm, onehot, kept, sent = kernel_call(
-        partial(forward_kernel, tok=tok, own=own),
-        [SMEM, VMEM, VMEM, VMEM],
+    gain = norm_gain.reshape(1, width)
+    pieces = kernel_call(
+        pack_kernel,
+        [SMEM, SMEM, VMEM, VMEM, VMEM],
+        [((span, HD), bf16, KEPT)] * heads,
+        held=pltpu.HBM,
+    )(place, targets, seq_keys, hist_values[0], latent_queries[0])
+    pieces = [pieces[0]] + [
+        lax.ppermute(piece, "seq", perm) for piece, perm in zip(pieces[1:], steps)
+    ]
+
+    packed, attn, log_norm, onehot, kept, sent = kernel_call(
+        partial(forward_kernel, tok=tok, own=own, count=heads),
+        [SMEM] + [VMEM] * (4 + heads),
         [
+            ((heads, span, HD), bf16, KEPT),
             ((latents, HD), bf16, KEPT),
             ((latents, HD), f32, KEPT),
             ((half, HD), f32, KEPT),
@@ -419,10 +457,10 @@
             ((half, width), bf16, KEPT),
         ],
         [pltpu.VMEM((latents, width), f32)],
-    )(side, latent_pos, packed, out_proj)
+    )(place, latent_pos, out_proj, gain, unembed, *pieces)
     pair_sum = (kept + lax.ppermute(sent, "seq", swap).astype(f32)).astype(bf16)
     chips = [[(i, i ^ step) for i in range(n_seq)] for step in range(2, n_seq, 2)]
-    shifts = [[(i, (i + step) % n_grp) for i in range(n_grp)] for step in range(1, n_grp)]
+    shifts = [[(i, i ^ step) for i in range(n_grp)] for step in range(1, n_grp)]
     parts = [pair_sum] + [lax.ppermute(pair_sum, "seq", perm) for perm in chips]
     attns = [attn] + [lax.ppermute(attn, "grp", perm) for perm in shifts]
     loss_call = kernel_call(
@@ -431,41 +469,50 @@
         [((width // HD * half + LOSS_ROWS, HD), bf16, KEPT), ((1, HD), f32, KEPT)],
         flops=1 << 26,
     )
-    message, loss_half = loss_call(norm_gain.reshape(1, width), unembed, onehot, *parts)
+    message, loss_half = loss_call(gain, unembed, onehot, *parts)
     pair_msg = lax.ppermute(message, "seq", swap)
     others = [lax.ppermute(message, "grp", perm) for perm in shifts]
-    stack = jnp.concatenate(attns, axis=0)
+    stack_call = kernel_call(stack_kernel, [VMEM] * n_grp, [((n_grp * latents, HD), bf16, KEPT)])
+    (stack,) = stack_call(*attns)
     stacks = [stack] + [lax.ppermute(stack, "seq", perm) for perm in chips]
     backward = kernel_call(
         partial(backward_kernel, tok=tok, own=own),
         [SMEM] + [VMEM] * 7,
-        [((heads, span, HD), bf16, KEPT)],
-        [pltpu.VMEM((latents, width), bf16)],
+        [((2, span, HD), bf16, KEPT)] * (n_seq // 2),
+        [pltpu.VMEM((heads, span, HD), bf16), pltpu.VMEM((latents, width), bf16)],
         flops=1 << 30,
     )
-    (grads,) = backward(side, latent_pos, packed, out_proj, attn, log_norm, message, pair_msg)
-    others = lax.optimization_barrier((*others, grads))[:-1]
-    grads = lax.all_to_all(grads, "seq", 0, 0)
+    grads = backward(place, latent_pos, packed, out_proj, attn, log_norm, message, pair_msg)
+    others = lax.optimization_barrier((*others, grads[0]))[:-1]
+    grads = [grads[0]] + [
+        lax.ppermute(one, "seq", perm) for one, perm in zip(grads[1:], chips)
+    ]
+    grads = grads + [lax.ppermute(one, "seq", swap) for one in grads]
+    total_call = kernel_call(total_kernel, [VMEM] * 2, [((1, HD), f32, KEPT)])
+    (loss,) = total_call(loss_half, pair_msg)
     stacks = stacks + [lax.ppermute(one, "seq", swap) for one in stacks]
     pair_others = [lax.ppermute(other, "seq", swap) for other in others]
-    proj_update, loss = kernel_call(
+    weights_call = kernel_call(
         partial(weight_kernel, groups=n_grp, seqs=n_seq, entries=channels * width),
         [SMEM] + [VMEM] * (2 * n_grp + n_seq + 1),
         [((HD, width), f32, VMEM), ((1, HD), f32, VMEM)],
         [
             pltpu.VMEM((n_grp * latents, width), bf16),
+            pltpu.VMEM((n_seq * HD, n_grp * latents), bf16),
             pltpu.VMEM((HD, width), f32),
         ],
-    )(side, message, *others, pair_msg, *pair_others, *stacks, loss_half)
-    grad_queries, grad_keys, grad_values = kernel_call(
+    )
+    proj_update, loss = weights_call(place, message, *others, pair_msg, *pair_others, *stacks, loss)
+    unpack_call = kernel_call(
         unpack_kernel,
-        [VMEM],
+        [SMEM] + [VMEM] * heads,
         [
             ((own, channels), bf16, VMEM),
             ((tok, channels), bf16, VMEM),
             ((tok, channels), bf16, VMEM),
         ],
-    )(grads)
+    )
+    grad_queries, grad_keys, grad_values = unpack_call(place, *grads)
     loss_sum = loss[0, 0]
     return (
         loss_sum.reshape(1),

time: 66.7 us -> 63.3 us (0.949)
  waiting for transfers between devices: 27.8 us -> 23 us
  local copies, waits for them, and re-layouts: 0.04 us -> 1.71 us
  Pallas kernels: 8.81 us -> 7.3 us
  starting transfers between devices: 28.9 us -> 30.3 us
    ppermute x0 -> x14, starting transfers between devices: none -> 10.9 us  [the longest x7 7.75 us: body(): lax.ppermute(piece, 'seq', perm)]
    all_to_all x2 -> x0, waiting for transfers between devices: 10.1 us -> none  [the longest x1 10.1 us: body(): packed = lax.all_to_all(packed, 'seq', 0, 0)]
    all_to_all x2 -> x0, starting transfers between devices: 8.87 us -> none  [the longest x1 5.33 us: body(): packed = lax.all_to_all(packed, 'seq', 0, 0)]
    ppermute x0 -> x14, waiting for transfers between devices: none -> 7.88 us  [the longest x7 4.85 us: body(): lax.ppermute(piece, 'seq', perm)]
    ppermute x3, waiting for transfers between devices: 5.15 us -> 0.01 us  [body(): parts = [pair_sum] + [lax.ppermute(pair_sum, 'seq', perm) for perm in chips]]
    ppermute x3, starting transfers between devices: 6.46 us -> 3.49 us  [body(): stacks = [stack] + [lax.ppermute(stack, 'seq', perm) for perm in chips]]
    ppermute x3, starting transfers between devices: 4.67 us -> 7.38 us  [body(): attns = [attn] + [lax.ppermute(attn, 'grp', perm) for perm in shifts]]
    ppermute x3, waiting for transfers between devices: 0.01 us -> 1.87 us  [body(): pair_others = [lax.ppermute(other, 'seq', swap) for other in others]]
  transfers between devices with their start and end apart: 23 -> 35, of which waited for: 8 -> 12; matrix products, arithmetic and copies ran while one was open for 0% -> 0% of each run, Pallas kernels for 7% -> 7%
where the time goes in v4:
time: 63.3 us; the launch traced here: 63.1 us
  starting transfers between devices  30.3 us (48%)
  waiting for transfers between devices  23 us (36%)
  Pallas kernels  7.3 us (12%)
  local copies, waits for them, and re-layouts  1.71 us (3%)
  between operations  0.77 us (1%)
    ppermute x7, starting transfers between devices, body(): lax.ppermute(piece, 'seq', perm)  7.75 us
    ppermute x3, starting transfers between devices, body(): attns = [attn] + [lax.ppermute(attn, 'grp', perm) for perm in shifts]  7.38 us
    pallas_call x8, Pallas kernels, placed(): call(*(pltpu.with_memory_space_constraint(operand, held) if spec is VMEM...  7.3 us
    ppermute x3, waiting for transfers between devices, body(): others = [lax.ppermute(message, 'grp', perm) for perm in shifts]  6.49 us
    ppermute x7, waiting for transfers between devices, body(): lax.ppermute(piece, 'seq', perm)  4.85 us
    ppermute x3, waiting for transfers between devices, body(): stacks = [stack] + [lax.ppermute(stack, 'seq', perm) for perm in chips]  4.17 us
    ppermute x3, starting transfers between devices, body(): parts = [pair_sum] + [lax.ppermute(pair_sum, 'seq', perm) for perm in chips]  3.55 us
    ppermute x3, starting transfers between devices, body(): stacks = [stack] + [lax.ppermute(stack, 'seq', perm) for perm in chips]  3.49 us
  transfers between devices with their start and end apart: 35, of which 12 were waited for; matrix products, arithmetic and copies ran while one was open for 0% of the time, Pallas kernels for 7%

profile of v4, /device:TPU:0, one launch (start us, length us, event | category | flops | bytes accessed | tf_op | source)
XLA Modules:
  0.0 63.1 jit_solution(8882458215702892680)
XLA Ops:
  0.6 1.2 %shard_map.119 = (bf16[272,128]{1,0:T(8,128)(2,1)S(1)}, bf16[272,128]{1,0:T(8,128)(2,1)S(1)}, bf16[272,128]{1,0:T(8,128)(2,1)S(1)}, bf16[272,128]{1,0:T(8,128)(2...) custom-call(s32[1]{0:T(128)} %bitcast.place, ...), custom_call_target="tpu_custom_call" | custom-call | flops 1048576 | tf_op jit(solution)/shard_map/pallas_call | solution.py:181
  2.5 2.6 %collective-permute-start.1 = (bf16[272,128]{1,0:T(8,128)(2,1)S(1)}, bf16[272,128]{1,0:T(8,128)(2,1)S(1)}, u32[]{:S(2)}, u32[]{:S(2)}) collective-permute-start(bf16[272,128]{1,0:T(8,128)(2,1)S(1)} %get-tuple-element.35), channel_id=1, source_target_pairs={{0,2},{1,3},{2,0},{3,1},{4,6},{5,7},{6,4},{7,5},{8,10},{9,11},{10,... | collective-permute-start | bytes 208904 | tf_op jit(solution)/shard_map/ppermute | solution.py:445
  5.1 1.8 %collective-permute-start.3 = (bf16[272,128]{1,0:T(8,128)(2,1)S(1)}, bf16[272,128]{1,0:T(8,128)(2,1)S(1)}, u32[]{:S(2)}, u32[]{:S(2)}) collective-permute-start(bf16[272,128]{1,0:T(8,128)(2,1)S(1)} %get-tuple-element.37), channel_id=1, source_target_pairs={{0,4},{1,5},{2,6},{3,7},{4,0},{5,1},{6,2},{7,3},{8,12},{9,13},{10,... | collective-permute-start | bytes 208904 | tf_op jit(solution)/shard_map/ppermute | solution.py:445
  6.8 2.6 %collective-permute-start.5 = (bf16[272,128]{1,0:T(8,128)(2,1)S(1)}, bf16[272,128]{1,0:T(8,128)(2,1)S(1)}, u32[]{:S(2)}, u32[]{:S(2)}) collective-permute-start(bf16[272,128]{1,0:T(8,128)(2,1)S(1)} %get-tuple-element.39), channel_id=1, source_target_pairs={{0,6},{1,7},{2,4},{3,5},{4,2},{5,3},{6,0},{7,1},{8,14},{9,15},{10,... | collective-permute-start | bytes 208904 | tf_op jit(solution)/shard_map/ppermute | solution.py:445
  9.7 3.6 %collective-permute-done.4.refs_5_ = bf16[272,128]{1,0:T(8,128)(2,1)S(1)} collective-permute-done((bf16[272,128]{1,0:T(8,128)(2,1)S(1)}, bf16[272,128]{1,0:T(8,128)(2,1)S(1)}, u32[]{:S(2)}, u32[]{:S(2)}) %collective-permute-start.4) | collective-permute-done | bytes 69664 | tf_op jit(solution)/shard_map/ppermute | solution.py:445
  13.3 1.2 %collective-permute-done.6.refs_7_ = bf16[272,128]{1,0:T(8,128)(2,1)S(1)} collective-permute-done((bf16[272,128]{1,0:T(8,128)(2,1)S(1)}, bf16[272,128]{1,0:T(8,128)(2,1)S(1)}, u32[]{:S(2)}, u32[]{:S(2)}) %collective-permute-start.6) | collective-permute-done | bytes 69664 | tf_op jit(solution)/shard_map/ppermute | solution.py:445
  15.2 1.0 %copy-done.1 = bf16[128,2048]{1,0:T(8,128)(2,1)S(1)} copy-done((bf16[128,2048]{1,0:T(8,128)(2,1)S(1)}, bf16[128,2048]{1,0:T(8,128)(2,1)}, u32[]{:S(2)}) %copy-start.1) | copy-done | bytes 524312
  17.2 1.2 %collective-permute-done.7 = bf16[32,2048]{1,0:T(8,128)(2,1)S(1)} collective-permute-done((bf16[32,2048]{1,0:T(8,128)(2,1)S(1)}, bf16[32,2048]{1,0:T(8,128)(2,1)S(1)}, u32[]{:S(2)}, u32[]{:S(2)}) %collective-permute-start.7) | collective-permute-done | bytes 131104 | tf_op jit(solution)/shard_map/ppermute | solution.py:461
  18.4 2.0 %collective-permute-start.10 = (bf16[32,2048]{1,0:T(8,128)(2,1)S(1)}, bf16[32,2048]{1,0:T(8,128)(2,1)S(1)}, u32[]{:S(2)}, u32[]{:S(2)}) collective-permute-start(bf16[32,2048]{1,0:T(8,128)(2,1)S(1)} %add_convert_fusion.refs_0_), channel_id=1, source_target_pairs={{0,6},{1,7},{2,4},{3,5},{4,2},{5,3},{6,0},{7,1},{8,14},{9,15},{10,... | collective-permute-start | bytes 393224 | tf_op jit(solution)/shard_map/ppermute | solution.py:464
  20.8 1.2 %collective-permute-start.9 = (bf16[32,2048]{1,0:T(8,128)(2,1)S(1)}, bf16[32,2048]{1,0:T(8,128)(2,1)S(1)}, u32[]{:S(2)}, u32[]{:S(2)}) collective-permute-start(bf16[32,2048]{1,0:T(8,128)(2,1)S(1)} %add_convert_fusion.refs_0_), channel_id=1, source_target_pairs={{0,4},{1,5},{2,6},{3,7},{4,0},{5,1},{6,2},{7,3},{8,12},{9,13},{10,... | collective-permute-start | bytes 393224 | tf_op jit(solution)/shard_map/ppermute | solution.py:464
  22.0 1.6 %collective-permute-start.18 = (bf16[64,128]{1,0:T(8,128)(2,1)S(1)}, bf16[64,128]{1,0:T(8,128)(2,1)S(1)}, u32[]{:S(2)}, u32[]{:S(2)}) collective-permute-start(bf16[64,128]{1,0:T(8,128)(2,1)S(1)} %get-tuple-element.46.attn.refs_0_), channel_id=1, source_target_pairs={{0,8},{8,0},{16,24},{24,16},{1,9},{9,1},{17,25},{25,17},{2,10},{10... | collective-permute-start | bytes 49160 | tf_op jit(solution)/shard_map/ppermute | solution.py:465
  23.6 2.6 %collective-permute-start.19 = (bf16[64,128]{1,0:T(8,128)(2,1)S(1)}, bf16[64,128]{1,0:T(8,128)(2,1)S(1)}, u32[]{:S(2)}, u32[]{:S(2)}) collective-permute-start(bf16[64,128]{1,0:T(8,128)(2,1)S(1)} %get-tuple-element.46.attn.refs_0_), channel_id=1, source_target_pairs={{0,16},{8,24},{16,0},{24,8},{1,17},{9,25},{17,1},{25,9},{2,18},{10... | collective-permute-start | bytes 49160 | tf_op jit(solution)/shard_map/ppermute | solution.py:465
  26.2 3.2 %collective-permute-start.20 = (bf16[64,128]{1,0:T(8,128)(2,1)S(1)}, bf16[64,128]{1,0:T(8,128)(2,1)S(1)}, u32[]{:S(2)}, u32[]{:S(2)}) collective-permute-start(bf16[64,128]{1,0:T(8,128)(2,1)S(1)} %get-tuple-element.46.attn.refs_0_), channel_id=1, source_target_pairs={{0,24},{8,16},{16,8},{24,0},{1,25},{9,17},{17,9},{25,1},{2,26},{10... | collective-permute-start | bytes 49160 | tf_op jit(solution)/shard_map/ppermute | solution.py:465
  30.4 1.3 %collective-permute-done.20.refs_3_ = bf16[64,128]{1,0:T(8,128)(2,1)S(1)} collective-permute-done((bf16[64,128]{1,0:T(8,128)(2,1)S(1)}, bf16[64,128]{1,0:T(8,128)(2,1)S(1)}, u32[]{:S(2)}, u32[]{:S(2)}) %collective-permute-start.20) | collective-permute-done | bytes 16416 | tf_op jit(solution)/shard_map/ppermute | solution.py:465
  32.5 1.8 %collective-permute-start.22 = (bf16[256,128]{1,0:T(8,128)(2,1)S(1)}, bf16[256,128]{1,0:T(8,128)(2,1)S(1)}, u32[]{:S(2)}, u32[]{:S(2)}) collective-permute-start(bf16[256,128]{1,0:T(8,128)(2,1)S(1)} %shard_map.123.refs_8_), channel_id=1, source_target_pairs={{0,4},{1,5},{2,6},{3,7},{4,0},{5,1},{6,2},{7,3},{8,12},{9,13},{10,... | collective-permute-start | bytes 196616 | tf_op jit(solution)/shard_map/ppermute | solution.py:477
  35.2 1.4 %collective-permute-done.21.refs_9_ = bf16[256,128]{1,0:T(8,128)(2,1)S(1)} collective-permute-done((bf16[256,128]{1,0:T(8,128)(2,1)S(1)}, bf16[256,128]{1,0:T(8,128)(2,1)S(1)}, u32[]{:S(2)}, u32[]{:S(2)}) %collective-permute-start.21) | collective-permute-done | bytes 65568 | tf_op jit(solution)/shard_map/ppermute | solution.py:477
  37.4 2.0 %collective-permute-done.23.refs_11_ = bf16[256,128]{1,0:T(8,128)(2,1)S(1)} collective-permute-done((bf16[256,128]{1,0:T(8,128)(2,1)S(1)}, bf16[256,128]{1,0:T(8,128)(2,1)S(1)}, u32[]{:S(2)}, u32[]{:S(2)}) %collective-permute-start.23) | collective-permute-done | bytes 65568 | tf_op jit(solution)/shard_map/ppermute | solution.py:477
  39.4 1.2 %collective-permute-start.12 = (bf16[528,128]{1,0:T(8,128)(2,1)S(1)}, bf16[528,128]{1,0:T(8,128)(2,1)S(1)}, u32[]{:S(2)}, u32[]{:S(2)}) collective-permute-start(bf16[528,128]{1,0:T(8,128)(2,1)S(1)} %get-tuple-element.44.own_msg.refs_0_), channel_id=1, source_target_pairs={{0,16},{8,24},{16,0},{24,8},{1,17},{9,25},{17,1},{25,9},{2,18},{10... | collective-permute-start | bytes 405512 | tf_op jit(solution)/shard_map/ppermute | solution.py:474
  40.6 2.0 %collective-permute-start.13 = (bf16[528,128]{1,0:T(8,128)(2,1)S(1)}, bf16[528,128]{1,0:T(8,128)(2,1)S(1)}, u32[]{:S(2)}, u32[]{:S(2)}) collective-permute-start(bf16[528,128]{1,0:T(8,128)(2,1)S(1)} %get-tuple-element.44.own_msg.refs_0_), channel_id=1, source_target_pairs={{0,24},{8,16},{16,8},{24,0},{1,25},{9,17},{17,9},{25,1},{2,26},{10... | collective-permute-start | bytes 405512 | tf_op jit(solution)/shard_map/ppermute | solution.py:474
  44.6 6.5 %collective-permute-done.12.refs_2_ = bf16[528,128]{1,0:T(8,128)(2,1)S(1)} collective-permute-done((bf16[528,128]{1,0:T(8,128)(2,1)S(1)}, bf16[528,128]{1,0:T(8,128)(2,1)S(1)}, u32[]{:S(2)}, u32[]{:S(2)}) %collective-permute-start.12) | collective-permute-done | bytes 135200 | tf_op jit(solution)/shard_map/ppermute | solution.py:474
  51.0 1.1 %collective-permute-start.29 = (bf16[2,272,128]{2,1,0:T(8,128)(2,1)S(1)}, bf16[2,272,128]{2,1,0:T(8,128)(2,1)S(1)}, u32[]{:S(2)}, u32[]{:S(2)}) collective-permute-start(bf16[2,272,128]{2,1,0:T(8,128)(2,1)S(1)} %get-tuple-element.55), channel_id=1, source_target_pairs={{0,4},{1,5},{2,6},{3,7},{4,0},{5,1},{6,2},{7,3},{8,12},{9,13},{10,... | collective-permute-start | bytes 417800 | tf_op jit(solution)/shard_map/ppermute | solution.py:488
  52.1 1.1 %collective-permute-start.30 = (bf16[2,272,128]{2,1,0:T(8,128)(2,1)S(1)}, bf16[2,272,128]{2,1,0:T(8,128)(2,1)S(1)}, u32[]{:S(2)}, u32[]{:S(2)}) collective-permute-start(bf16[2,272,128]{2,1,0:T(8,128)(2,1)S(1)} %get-tuple-element.56), channel_id=1, source_target_pairs={{0,6},{1,7},{2,4},{3,5},{4,2},{5,3},{6,0},{7,1},{8,14},{9,15},{10,... | collective-permute-start | bytes 417800 | tf_op jit(solution)/shard_map/ppermute | solution.py:488
  56.1 2.0 %collective-permute-done.30.refs_3_ = bf16[2,272,128]{2,1,0:T(8,128)(2,1)S(1)} collective-permute-done((bf16[2,272,128]{2,1,0:T(8,128)(2,1)S(1)}, bf16[2,272,128]{2,1,0:T(8,128)(2,1)S(1)}, u32[]{:S(2)}, u32[]{:S(2)}) %collective-permute-start.30) | collective-permute-done | bytes 139296 | tf_op jit(solution)/shard_map/ppermute | solution.py:488
  59.6 2.5 %shard_map.125 = (f32[128,2048]{1,0:T(8,128)}, f32[1,128]{1,0:T(1,128)}) custom-call(s32[1]{0:T(128)} %bitcast.place, bf16[528,128]{1,0:T(8,128)(2,1)S(1)} %get-tuple-element.44.own_msg.refs_0_, bf16[528,128]{1,0:T(8,128)(2,1)S(1)} %collective-permute-done.11.refs_1_, bf16[528,128]{1,0:T(8,128)(2,1)S(1)} %collective-permute-done.12.refs_2_, ...), custom_call_target="tpu_custom_call" | custom-call | flops 1048576 | tf_op jit(solution)/shard_map/pallas_call | solution.py:181
  (65 shorter events, 13.7 us)
Async XLA Ops:
  2.5 7.0 %collective-permute-start.1 = (bf16[272,128]{1,0:T(8,128)(2,1)S(1)}, bf16[272,128]{1,0:T(8,128)(2,1)S(1)}, u32[]{:S(2)}, u32[]{:S(2)}) collective-permute-start(bf16[272,128]{1,0:T(8,128)(2,1)S(1)} %get-tuple-element.35), channel_id=1, source_target_pairs={{0,2},{1,3},{2,0},{3,1},{4,6},{5,7},{6,4},{7,5},{8,10},{9,11},{10,... | collective-permute-start | bytes 208904 | tf_op jit(solution)/shard_map/ppermute | solution.py:445
  6.8 6.5 %collective-permute-start.4 = (bf16[272,128]{1,0:T(8,128)(2,1)S(1)}, bf16[272,128]{1,0:T(8,128)(2,1)S(1)}, u32[]{:S(2)}, u32[]{:S(2)}) collective-permute-start(bf16[272,128]{1,0:T(8,128)(2,1)S(1)} %get-tuple-element.38), channel_id=1, source_target_pairs={{0,5},{1,4},{2,7},{3,6},{4,1},{5,0},{6,3},{7,2},{8,13},{9,12},{10,... | collective-permute-start | bytes 208904 | tf_op jit(solution)/shard_map/ppermute | solution.py:445
  6.8 6.5 %collective-permute-start.5 = (bf16[272,128]{1,0:T(8,128)(2,1)S(1)}, bf16[272,128]{1,0:T(8,128)(2,1)S(1)}, u32[]{:S(2)}, u32[]{:S(2)}) collective-permute-start(bf16[272,128]{1,0:T(8,128)(2,1)S(1)} %get-tuple-element.39), channel_id=1, source_target_pairs={{0,6},{1,7},{2,4},{3,5},{4,2},{5,3},{6,0},{7,1},{8,14},{9,15},{10,... | collective-permute-start | bytes 208904 | tf_op jit(solution)/shard_map/ppermute | solution.py:445
  18.4 7.7 %collective-permute-start.10 = (bf16[32,2048]{1,0:T(8,128)(2,1)S(1)}, bf16[32,2048]{1,0:T(8,128)(2,1)S(1)}, u32[]{:S(2)}, u32[]{:S(2)}) collective-permute-start(bf16[32,2048]{1,0:T(8,128)(2,1)S(1)} %add_convert_fusion.refs_0_), channel_id=1, source_target_pairs={{0,6},{1,7},{2,4},{3,5},{4,2},{5,3},{6,0},{7,1},{8,14},{9,15},{10,... | collective-permute-start | bytes 393224 | tf_op jit(solution)/shard_map/ppermute | solution.py:464
  20.5 8.9 %collective-permute-start.8 = (bf16[32,2048]{1,0:T(8,128)(2,1)S(1)}, bf16[32,2048]{1,0:T(8,128)(2,1)S(1)}, u32[]{:S(2)}, u32[]{:S(2)}) collective-permute-start(bf16[32,2048]{1,0:T(8,128)(2,1)S(1)} %add_convert_fusion.refs_0_), channel_id=1, source_target_pairs={{0,2},{1,3},{2,0},{3,1},{4,6},{5,7},{6,4},{7,5},{8,10},{9,11},{10,... | collective-permute-start | bytes 393224 | tf_op jit(solution)/shard_map/ppermute | solution.py:464
  20.8 8.6 %collective-permute-start.9 = (bf16[32,2048]{1,0:T(8,128)(2,1)S(1)}, bf16[32,2048]{1,0:T(8,128)(2,1)S(1)}, u32[]{:S(2)}, u32[]{:S(2)}) collective-permute-start(bf16[32,2048]{1,0:T(8,128)(2,1)S(1)} %add_convert_fusion.refs_0_), channel_id=1, source_target_pairs={{0,4},{1,5},{2,6},{3,7},{4,0},{5,1},{6,2},{7,3},{8,12},{9,13},{10,... | collective-permute-start | bytes 393224 | tf_op jit(solution)/shard_map/ppermute | solution.py:464
  22.0 8.4 %collective-permute-start.18 = (bf16[64,128]{1,0:T(8,128)(2,1)S(1)}, bf16[64,128]{1,0:T(8,128)(2,1)S(1)}, u32[]{:S(2)}, u32[]{:S(2)}) collective-permute-start(bf16[64,128]{1,0:T(8,128)(2,1)S(1)} %get-tuple-element.46.attn.refs_0_), channel_id=1, source_target_pairs={{0,8},{8,0},{16,24},{24,16},{1,9},{9,1},{17,25},{25,17},{2,10},{10... | collective-permute-start | bytes 49160 | tf_op jit(solution)/shard_map/ppermute | solution.py:465
  23.6 6.8 %collective-permute-start.19 = (bf16[64,128]{1,0:T(8,128)(2,1)S(1)}, bf16[64,128]{1,0:T(8,128)(2,1)S(1)}, u32[]{:S(2)}, u32[]{:S(2)}) collective-permute-start(bf16[64,128]{1,0:T(8,128)(2,1)S(1)} %get-tuple-element.46.attn.refs_0_), channel_id=1, source_target_pairs={{0,16},{8,24},{16,0},{24,8},{1,17},{9,25},{17,1},{25,9},{2,18},{10... | collective-permute-start | bytes 49160 | tf_op jit(solution)/shard_map/ppermute | solution.py:465
  26.2 5.5 %collective-permute-start.20 = (bf16[64,128]{1,0:T(8,128)(2,1)S(1)}, bf16[64,128]{1,0:T(8,128)(2,1)S(1)}, u32[]{:S(2)}, u32[]{:S(2)}) collective-permute-start(bf16[64,128]{1,0:T(8,128)(2,1)S(1)} %get-tuple-element.46.attn.refs_0_), channel_id=1, source_target_pairs={{0,24},{8,16},{16,8},{24,0},{1,25},{9,17},{17,9},{25,1},{2,26},{10... | collective-permute-start | bytes 49160 | tf_op jit(solution)/shard_map/ppermute | solution.py:465
  30.3 12.3 %collective-permute-start.14 = (bf16[528,128]{1,0:T(8,128)(2,1)S(1)}, bf16[528,128]{1,0:T(8,128)(2,1)S(1)}, u32[]{:S(2)}, u32[]{:S(2)}) collective-permute-start(bf16[528,128]{1,0:T(8,128)(2,1)S(1)} %get-tuple-element.44.own_msg.refs_0_), channel_id=1, source_target_pairs={{0,1},{1,0},{2,3},{3,2},{4,5},{5,4},{6,7},{7,6},{8,9},{9,8},{10,11... | collective-permute-start | bytes 405512 | tf_op jit(solution)/shard_map/ppermute | solution.py:473
  34.2 5.2 %collective-permute-start.23 = (bf16[256,128]{1,0:T(8,128)(2,1)S(1)}, bf16[256,128]{1,0:T(8,128)(2,1)S(1)}, u32[]{:S(2)}, u32[]{:S(2)}) collective-permute-start(bf16[256,128]{1,0:T(8,128)(2,1)S(1)} %shard_map.123.refs_8_), channel_id=1, source_target_pairs={{0,6},{1,7},{2,4},{3,5},{4,2},{5,3},{6,0},{7,1},{8,14},{9,15},{10,... | collective-permute-start | bytes 196616 | tf_op jit(solution)/shard_map/ppermute | solution.py:477
  35.2 5.4 %collective-permute-start.24 = (bf16[256,128]{1,0:T(8,128)(2,1)S(1)}, bf16[256,128]{1,0:T(8,128)(2,1)S(1)}, u32[]{:S(2)}, u32[]{:S(2)}) collective-permute-start(bf16[256,128]{1,0:T(8,128)(2,1)S(1)} %shard_map.123.refs_8_), channel_id=1, source_target_pairs={{0,1},{1,0},{2,3},{3,2},{4,5},{5,4},{6,7},{7,6},{8,9},{9,8},{10,11... | collective-permute-start | bytes 196616 | tf_op jit(solution)/shard_map/ppermute | solution.py:493
  36.6 6.0 %collective-permute-start.25 = (bf16[256,128]{1,0:T(8,128)(2,1)S(1)}, bf16[256,128]{1,0:T(8,128)(2,1)S(1)}, u32[]{:S(2)}, u32[]{:S(2)}) collective-permute-start(bf16[256,128]{1,0:T(8,128)(2,1)S(1)} %collective-permute-done.21.refs_9_), channel_id=1, source_target_pairs={{0,1},{1,0},{2,3},{3,2},{4,5},{5,4},{6,7},{7,6},{8,9},{9,8},{10,11... | collective-permute-start | bytes 196616 | tf_op jit(solution)/shard_map/ppermute | solution.py:493
  37.4 6.7 %collective-permute-start.11 = (bf16[528,128]{1,0:T(8,128)(2,1)S(1)}, bf16[528,128]{1,0:T(8,128)(2,1)S(1)}, u32[]{:S(2)}, u32[]{:S(2)}) collective-permute-start(bf16[528,128]{1,0:T(8,128)(2,1)S(1)} %get-tuple-element.44.own_msg.refs_0_), channel_id=1, source_target_pairs={{0,8},{8,0},{16,24},{24,16},{1,9},{9,1},{17,25},{25,17},{2,10},{10... | collective-permute-start | bytes 405512 | tf_op jit(solution)/shard_map/ppermute | solution.py:474
  39.4 11.6 %collective-permute-start.12 = (bf16[528,128]{1,0:T(8,128)(2,1)S(1)}, bf16[528,128]{1,0:T(8,128)(2,1)S(1)}, u32[]{:S(2)}, u32[]{:S(2)}) collective-permute-start(bf16[528,128]{1,0:T(8,128)(2,1)S(1)} %get-tuple-element.44.own_msg.refs_0_), channel_id=1, source_target_pairs={{0,16},{8,24},{16,0},{24,8},{1,17},{9,25},{17,1},{25,9},{2,18},{10... | collective-permute-start | bytes 405512 | tf_op jit(solution)/shard_map/ppermute | solution.py:474
  40.6 11.6 %collective-permute-start.13 = (bf16[528,128]{1,0:T(8,128)(2,1)S(1)}, bf16[528,128]{1,0:T(8,128)(2,1)S(1)}, u32[]{:S(2)}, u32[]{:S(2)}) collective-permute-start(bf16[528,128]{1,0:T(8,128)(2,1)S(1)} %get-tuple-element.44.own_msg.refs_0_), channel_id=1, source_target_pairs={{0,24},{8,16},{16,8},{24,0},{1,25},{9,17},{17,9},{25,1},{2,26},{10... | collective-permute-start | bytes 405512 | tf_op jit(solution)/shard_map/ppermute | solution.py:474
  42.6 10.6 %collective-permute-start.26 = (bf16[256,128]{1,0:T(8,128)(2,1)S(1)}, bf16[256,128]{1,0:T(8,128)(2,1)S(1)}, u32[]{:S(2)}, u32[]{:S(2)}) collective-permute-start(bf16[256,128]{1,0:T(8,128)(2,1)S(1)} %collective-permute-done.22.refs_10_), channel_id=1, source_target_pairs={{0,1},{1,0},{2,3},{3,2},{4,5},{5,4},{6,7},{7,6},{8,9},{9,8},{10,11... | collective-permute-start | bytes 196616 | tf_op jit(solution)/shard_map/ppermute | solution.py:493
  42.6 10.6 %collective-permute-start.27 = (bf16[256,128]{1,0:T(8,128)(2,1)S(1)}, bf16[256,128]{1,0:T(8,128)(2,1)S(1)}, u32[]{:S(2)}, u32[]{:S(2)}) collective-permute-start(bf16[256,128]{1,0:T(8,128)(2,1)S(1)} %collective-permute-done.23.refs_11_), channel_id=1, source_target_pairs={{0,1},{1,0},{2,3},{3,2},{4,5},{5,4},{6,7},{7,6},{8,9},{9,8},{10,11... | collective-permute-start | bytes 196616 | tf_op jit(solution)/shard_map/ppermute | solution.py:493
  44.1 10.6 %collective-permute-start.28 = (bf16[2,272,128]{2,1,0:T(8,128)(2,1)S(1)}, bf16[2,272,128]{2,1,0:T(8,128)(2,1)S(1)}, u32[]{:S(2)}, u32[]{:S(2)}) collective-permute-start(bf16[2,272,128]{2,1,0:T(8,128)(2,1)S(1)} %get-tuple-element.54), channel_id=1, source_target_pairs={{0,2},{1,3},{2,0},{3,1},{4,6},{5,7},{6,4},{7,5},{8,10},{9,11},{10,... | collective-permute-start | bytes 417800 | tf_op jit(solution)/shard_map/ppermute | solution.py:488
  51.0 5.1 %collective-permute-start.29 = (bf16[2,272,128]{2,1,0:T(8,128)(2,1)S(1)}, bf16[2,272,128]{2,1,0:T(8,128)(2,1)S(1)}, u32[]{:S(2)}, u32[]{:S(2)}) collective-permute-start(bf16[2,272,128]{2,1,0:T(8,128)(2,1)S(1)} %get-tuple-element.55), channel_id=1, source_target_pairs={{0,4},{1,5},{2,6},{3,7},{4,0},{5,1},{6,2},{7,3},{8,12},{9,13},{10,... | collective-permute-start | bytes 417800 | tf_op jit(solution)/shard_map/ppermute | solution.py:488
  52.1 6.0 %collective-permute-start.30 = (bf16[2,272,128]{2,1,0:T(8,128)(2,1)S(1)}, bf16[2,272,128]{2,1,0:T(8,128)(2,1)S(1)}, u32[]{:S(2)}, u32[]{:S(2)}) collective-permute-start(bf16[2,272,128]{2,1,0:T(8,128)(2,1)S(1)} %get-tuple-element.56), channel_id=1, source_target_pairs={{0,6},{1,7},{2,4},{3,5},{4,2},{5,3},{6,0},{7,1},{8,14},{9,15},{10,... | collective-permute-start | bytes 417800 | tf_op jit(solution)/shard_map/ppermute | solution.py:488
  54.5 7.6 %collective-permute-start.31 = (bf16[2,272,128]{2,1,0:T(8,128)(2,1)S(1)}, bf16[2,272,128]{2,1,0:T(8,128)(2,1)S(1)}, u32[]{:S(2)}, u32[]{:S(2)}) collective-permute-start(bf16[2,272,128]{2,1,0:T(8,128)(2,1)S(1)} %get-tuple-element.48.refs_0_), channel_id=1, source_target_pairs={{0,1},{1,0},{2,3},{3,2},{4,5},{5,4},{6,7},{7,6},{8,9},{9,8},{10,11... | collective-permute-start | bytes 417800 | tf_op jit(solution)/shard_map/ppermute | solution.py:490
  54.7 7.4 %collective-permute-start.32 = (bf16[2,272,128]{2,1,0:T(8,128)(2,1)S(1)}, bf16[2,272,128]{2,1,0:T(8,128)(2,1)S(1)}, u32[]{:S(2)}, u32[]{:S(2)}) collective-permute-start(bf16[2,272,128]{2,1,0:T(8,128)(2,1)S(1)} %collective-permute-done.28.refs_1_), channel_id=1, source_target_pairs={{0,1},{1,0},{2,3},{3,2},{4,5},{5,4},{6,7},{7,6},{8,9},{9,8},{10,11... | collective-permute-start | bytes 417800 | tf_op jit(solution)/shard_map/ppermute | solution.py:490
  56.1 6.0 %collective-permute-start.33 = (bf16[2,272,128]{2,1,0:T(8,128)(2,1)S(1)}, bf16[2,272,128]{2,1,0:T(8,128)(2,1)S(1)}, u32[]{:S(2)}, u32[]{:S(2)}) collective-permute-start(bf16[2,272,128]{2,1,0:T(8,128)(2,1)S(1)} %collective-permute-done.29.refs_2_), channel_id=1, source_target_pairs={{0,1},{1,0},{2,3},{3,2},{4,5},{5,4},{6,7},{7,6},{8,9},{9,8},{10,11... | collective-permute-start | bytes 417800 | tf_op jit(solution)/shard_map/ppermute | solution.py:490
  (16 other events, 84.3 us)

commit v5 on v4

--- a/solution.py
+++ b/solution.py
@@ -375,12 +375,11 @@
     loss[...] = loss_half[...] + jnp.sum(other, axis=0, keepdims=True)
 
 
-def weight_kernel(place, *refs, groups, seqs, entries):
+def weight_kernel(place, *refs, groups, seqs):
     own_msgs = refs[:groups]
     pair_msgs = refs[groups : 2 * groups]
     attns = refs[2 * groups : 2 * groups + seqs]
-    loss_in, update, loss, grad_hidden, attn_cols, total = refs[2 * groups + seqs :]
-    loss[...] = loss_in[...]
+    total, square_sums, grad_hidden, attn_cols = refs[2 * groups + seqs :]
     latents = grad_hidden.shape[0] // groups
     half = latents // 2
     mine = place[0] & 1
@@ -401,7 +400,13 @@
         total[:, cols] = part[0:HD]
         squares = squares + jnp.sum((part * part).reshape(seqs * HD // 8, 8, TILE), axis=0)
     square_sum = jnp.sum(jnp.sum(squares, axis=0, keepdims=True), axis=1, keepdims=True)
+    square_sums[...] = jnp.broadcast_to(square_sum, square_sums.shape)
+
+
+def scale_kernel(total, squares, other_squares, loss_in, update, loss, *, entries):
+    square_sum = squares[:, 0:1] + other_squares[:, 0:1]
     update[...] = total[...] * lax.rsqrt(square_sum / entries + epsilon)
+    loss[...] = loss_in[...]
 
 
 def body(hist_keys, hist_values, latent_queries, latent_pos, targets, out_proj, norm_gain, unembed):
@@ -490,19 +495,18 @@
     grads = grads + [lax.ppermute(one, "seq", swap) for one in grads]
     total_call = kernel_call(total_kernel, [VMEM] * 2, [((1, HD), f32, KEPT)])
     (loss,) = total_call(loss_half, pair_msg)
-    stacks = stacks + [lax.ppermute(one, "seq", swap) for one in stacks]
     pair_others = [lax.ppermute(other, "seq", swap) for other in others]
     weights_call = kernel_call(
-        partial(weight_kernel, groups=n_grp, seqs=n_seq, entries=channels * width),
-        [SMEM] + [VMEM] * (2 * n_grp + n_seq + 1),
-        [((HD, width), f32, VMEM), ((1, HD), f32, VMEM)],
+        partial(weight_kernel, groups=n_grp, seqs=n_seq // 2),
+        [SMEM] + [VMEM] * (2 * n_grp + n_seq // 2),
+        [((HD, width), f32, KEPT), ((1, HD), f32, KEPT)],
         [
             pltpu.VMEM((n_grp * latents, width), bf16),
-            pltpu.VMEM((n_seq * HD, n_grp * latents), bf16),
-            pltpu.VMEM((HD, width), f32),
+            pltpu.VMEM((n_seq // 2 * HD, n_grp * latents), bf16),
         ],
     )
-    proj_update, loss = weights_call(place, message, *others, pair_msg, *pair_others, *stacks, loss)
+    total, squares = weights_call(place, message, *others, pair_msg, *pair_others, *stacks)
+    other_squares = lax.ppermute(squares, "seq", swap)
     unpack_call = kernel_call(
         unpack_kernel,
         [SMEM] + [VMEM] * heads,
@@ -513,6 +517,12 @@
         ],
     )
     grad_queries, grad_keys, grad_values = unpack_call(place, *grads)
+    scale_call = kernel_call(
+        partial(scale_kernel, entries=channels * width),
+        [VMEM] * 4,
+        [((HD, width), f32, VMEM), ((1, HD), f32, VMEM)],
+    )
+    proj_update, loss = scale_call(total, squares, other_squares, loss)
     loss_sum = loss[0, 0]
     return (
         loss_sum.reshape(1),

time: 63.3 us -> 65.1 us (1.028)
  waiting for transfers between devices: 23 us -> 26.1 us
  starting transfers between devices: 30.3 us -> 29.3 us
    ppermute x3, waiting for transfers between devices: 0.01 us -> 5.78 us  [body(): parts = [pair_sum] + [lax.ppermute(pair_sum, 'seq', perm) for perm in chips]]
    ppermute x3, waiting for transfers between devices: 4.17 us -> 0.01 us  [body(): stacks = [stack] + [lax.ppermute(stack, 'seq', perm) for perm in chips]]
    ppermute x3, waiting for transfers between devices: 1.33 us -> 5.31 us  [body(): attns = [attn] + [lax.ppermute(attn, 'grp', perm) for perm in shifts]]
    ppermute x3, waiting for transfers between devices: 6.49 us -> 3.19 us  [body(): others = [lax.ppermute(message, 'grp', perm) for perm in shifts]]
    ppermute x3, starting transfers between devices: 7.38 us -> 4.45 us  [body(): attns = [attn] + [lax.ppermute(attn, 'grp', perm) for perm in shifts]]
    ppermute x3, starting transfers between devices: 3.22 us -> 4.39 us  [body(): others = [lax.ppermute(message, 'grp', perm) for perm in shifts]]
    ppermute x3, starting transfers between devices: 2.59 us -> 3.55 us  [body(): lax.ppermute(one, 'seq', perm)]
    ppermute x4 -> x1, waiting for transfers between devices: 0.01 us -> 0.83 us  [body(): other_squares = lax.ppermute(squares, 'seq', swap)]
  transfers between devices with their start and end apart: 35 -> 32, of which waited for: 12 -> 14; matrix products, arithmetic and copies ran while one was open for 0% -> 0% of each run, Pallas kernels for 7% -> 5%
where the time goes in v5:
time: 65.1 us; the launch traced here: 64.9 us
  starting transfers between devices  29.3 us (45%)
  waiting for transfers between devices  26.1 us (40%)
  Pallas kernels  6.97 us (11%)
  local copies, waits for them, and re-layouts  1.71 us (3%)
  between operations  0.75 us (1%)
    ppermute x7, starting transfers between devices, body(): lax.ppermute(piece, 'seq', perm)  7.75 us
    pallas_call x9, Pallas kernels, placed(): call(*(pltpu.with_memory_space_constraint(operand, held) if spec is VMEM...  6.97 us
    ppermute x3, waiting for transfers between devices, body(): parts = [pair_sum] + [lax.ppermute(pair_sum, 'seq', perm) for perm in chips]  5.78 us
    ppermute x3, waiting for transfers between devices, body(): attns = [attn] + [lax.ppermute(attn, 'grp', perm) for perm in shifts]  5.31 us
    ppermute x7, waiting for transfers between devices, body(): lax.ppermute(piece, 'seq', perm)  4.85 us
    ppermute x3, starting transfers between devices, body(): attns = [attn] + [lax.ppermute(attn, 'grp', perm) for perm in shifts]  4.45 us
    ppermute x3, starting transfers between devices, body(): others = [lax.ppermute(message, 'grp', perm) for perm in shifts]  4.39 us
    ppermute x3, starting transfers between devices, body(): lax.ppermute(one, 'seq', perm)  3.55 us
  transfers between devices with their start and end apart: 32, of which 14 were waited for; matrix products, arithmetic and copies ran while one was open for 0% of the time, Pallas kernels for 5%

profile of v5, /device:TPU:0, one launch (start us, length us, event | category | flops | bytes accessed | tf_op | source)
XLA Modules:
  0.0 64.9 jit_solution(6902271935572694652)
XLA Ops:
  0.6 1.2 %shard_map.119 = (bf16[272,128]{1,0:T(8,128)(2,1)S(1)}, bf16[272,128]{1,0:T(8,128)(2,1)S(1)}, bf16[272,128]{1,0:T(8,128)(2,1)S(1)}, bf16[272,128]{1,0:T(8,128)(2...) custom-call(s32[1]{0:T(128)} %bitcast.place, ...), custom_call_target="tpu_custom_call" | custom-call | flops 1048576 | tf_op jit(solution)/shard_map/pallas_call | solution.py:181
  2.5 2.6 %collective-permute-start.1 = (bf16[272,128]{1,0:T(8,128)(2,1)S(1)}, bf16[272,128]{1,0:T(8,128)(2,1)S(1)}, u32[]{:S(2)}, u32[]{:S(2)}) collective-permute-start(bf16[272,128]{1,0:T(8,128)(2,1)S(1)} %get-tuple-element.37), channel_id=1, source_target_pairs={{0,2},{1,3},{2,0},{3,1},{4,6},{5,7},{6,4},{7,5},{8,10},{9,11},{10,... | collective-permute-start | bytes 208904 | tf_op jit(solution)/shard_map/ppermute | solution.py:450
  5.1 1.8 %collective-permute-start.3 = (bf16[272,128]{1,0:T(8,128)(2,1)S(1)}, bf16[272,128]{1,0:T(8,128)(2,1)S(1)}, u32[]{:S(2)}, u32[]{:S(2)}) collective-permute-start(bf16[272,128]{1,0:T(8,128)(2,1)S(1)} %get-tuple-element.39), channel_id=1, source_target_pairs={{0,4},{1,5},{2,6},{3,7},{4,0},{5,1},{6,2},{7,3},{8,12},{9,13},{10,... | collective-permute-start | bytes 208904 | tf_op jit(solution)/shard_map/ppermute | solution.py:450
  6.8 2.6 %collective-permute-start.5 = (bf16[272,128]{1,0:T(8,128)(2,1)S(1)}, bf16[272,128]{1,0:T(8,128)(2,1)S(1)}, u32[]{:S(2)}, u32[]{:S(2)}) collective-permute-start(bf16[272,128]{1,0:T(8,128)(2,1)S(1)} %get-tuple-element.41), channel_id=1, source_target_pairs={{0,6},{1,7},{2,4},{3,5},{4,2},{5,3},{6,0},{7,1},{8,14},{9,15},{10,... | collective-permute-start | bytes 208904 | tf_op jit(solution)/shard_map/ppermute | solution.py:450
  9.7 3.6 %collective-permute-done.4.refs_5_ = bf16[272,128]{1,0:T(8,128)(2,1)S(1)} collective-permute-done((bf16[272,128]{1,0:T(8,128)(2,1)S(1)}, bf16[272,128]{1,0:T(8,128)(2,1)S(1)}, u32[]{:S(2)}, u32[]{:S(2)}) %collective-permute-start.4) | collective-permute-done | bytes 69664 | tf_op jit(solution)/shard_map/ppermute | solution.py:450
  13.3 1.2 %collective-permute-done.6.refs_7_ = bf16[272,128]{1,0:T(8,128)(2,1)S(1)} collective-permute-done((bf16[272,128]{1,0:T(8,128)(2,1)S(1)}, bf16[272,128]{1,0:T(8,128)(2,1)S(1)}, u32[]{:S(2)}, u32[]{:S(2)}) %collective-permute-start.6) | collective-permute-done | bytes 69664 | tf_op jit(solution)/shard_map/ppermute | solution.py:450
  15.2 1.0 %copy-done.1 = bf16[128,2048]{1,0:T(8,128)(2,1)S(1)} copy-done((bf16[128,2048]{1,0:T(8,128)(2,1)S(1)}, bf16[128,2048]{1,0:T(8,128)(2,1)}, u32[]{:S(2)}) %copy-start.1) | copy-done | bytes 524312
  17.2 1.2 %collective-permute-done.7 = bf16[32,2048]{1,0:T(8,128)(2,1)S(1)} collective-permute-done((bf16[32,2048]{1,0:T(8,128)(2,1)S(1)}, bf16[32,2048]{1,0:T(8,128)(2,1)S(1)}, u32[]{:S(2)}, u32[]{:S(2)}) %collective-permute-start.7) | collective-permute-done | bytes 131104 | tf_op jit(solution)/shard_map/ppermute | solution.py:466
  18.4 2.0 %collective-permute-start.10 = (bf16[32,2048]{1,0:T(8,128)(2,1)S(1)}, bf16[32,2048]{1,0:T(8,128)(2,1)S(1)}, u32[]{:S(2)}, u32[]{:S(2)}) collective-permute-start(bf16[32,2048]{1,0:T(8,128)(2,1)S(1)} %add_convert_fusion.refs_0_), channel_id=1, source_target_pairs={{0,6},{1,7},{2,4},{3,5},{4,2},{5,3},{6,0},{7,1},{8,14},{9,15},{10,... | collective-permute-start | bytes 393224 | tf_op jit(solution)/shard_map/ppermute | solution.py:469
  20.8 1.2 %collective-permute-start.9 = (bf16[32,2048]{1,0:T(8,128)(2,1)S(1)}, bf16[32,2048]{1,0:T(8,128)(2,1)S(1)}, u32[]{:S(2)}, u32[]{:S(2)}) collective-permute-start(bf16[32,2048]{1,0:T(8,128)(2,1)S(1)} %add_convert_fusion.refs_0_), channel_id=1, source_target_pairs={{0,4},{1,5},{2,6},{3,7},{4,0},{5,1},{6,2},{7,3},{8,12},{9,13},{10,... | collective-permute-start | bytes 393224 | tf_op jit(solution)/shard_map/ppermute | solution.py:469
  22.0 3.8 %collective-permute-done.10.refs_3_ = bf16[32,2048]{1,0:T(8,128)(2,1)S(1)} collective-permute-done((bf16[32,2048]{1,0:T(8,128)(2,1)S(1)}, bf16[32,2048]{1,0:T(8,128)(2,1)S(1)}, u32[]{:S(2)}, u32[]{:S(2)}) %collective-permute-start.10) | collective-permute-done | bytes 131104 | tf_op jit(solution)/shard_map/ppermute | solution.py:469
  25.8 1.4 %collective-permute-done.8.refs_1_ = bf16[32,2048]{1,0:T(8,128)(2,1)S(1)} collective-permute-done((bf16[32,2048]{1,0:T(8,128)(2,1)S(1)}, bf16[32,2048]{1,0:T(8,128)(2,1)S(1)}, u32[]{:S(2)}, u32[]{:S(2)}) %collective-permute-start.8) | collective-permute-done | bytes 131104 | tf_op jit(solution)/shard_map/ppermute | solution.py:469
  28.7 1.6 %collective-permute-start.18 = (bf16[64,128]{1,0:T(8,128)(2,1)S(1)}, bf16[64,128]{1,0:T(8,128)(2,1)S(1)}, u32[]{:S(2)}, u32[]{:S(2)}) collective-permute-start(bf16[64,128]{1,0:T(8,128)(2,1)S(1)} %get-tuple-element.48.attn.refs_0_), channel_id=1, source_target_pairs={{0,8},{8,0},{16,24},{24,16},{1,9},{9,1},{17,25},{25,17},{2,10},{10... | collective-permute-start | bytes 49160 | tf_op jit(solution)/shard_map/ppermute | solution.py:470
  30.4 2.6 %collective-permute-start.19 = (bf16[64,128]{1,0:T(8,128)(2,1)S(1)}, bf16[64,128]{1,0:T(8,128)(2,1)S(1)}, u32[]{:S(2)}, u32[]{:S(2)}) collective-permute-start(bf16[64,128]{1,0:T(8,128)(2,1)S(1)} %get-tuple-element.48.attn.refs_0_), channel_id=1, source_target_pairs={{0,16},{8,24},{16,0},{24,8},{1,17},{9,25},{17,1},{25,9},{2,18},{10... | collective-permute-start | bytes 49160 | tf_op jit(solution)/shard_map/ppermute | solution.py:470
  33.2 1.9 %collective-permute-done.19.refs_2_ = bf16[64,128]{1,0:T(8,128)(2,1)S(1)} collective-permute-done((bf16[64,128]{1,0:T(8,128)(2,1)S(1)}, bf16[64,128]{1,0:T(8,128)(2,1)S(1)}, u32[]{:S(2)}, u32[]{:S(2)}) %collective-permute-start.19) | collective-permute-done | bytes 16416 | tf_op jit(solution)/shard_map/ppermute | solution.py:470
  35.1 3.4 %collective-permute-done.20.refs_3_ = bf16[64,128]{1,0:T(8,128)(2,1)S(1)} collective-permute-done((bf16[64,128]{1,0:T(8,128)(2,1)S(1)}, bf16[64,128]{1,0:T(8,128)(2,1)S(1)}, u32[]{:S(2)}, u32[]{:S(2)}) %collective-permute-start.20) | collective-permute-done | bytes 16416 | tf_op jit(solution)/shard_map/ppermute | solution.py:470
  38.5 1.0 %collective-permute-start.21 = (bf16[256,128]{1,0:T(8,128)(2,1)S(1)}, bf16[256,128]{1,0:T(8,128)(2,1)S(1)}, u32[]{:S(2)}, u32[]{:S(2)}) collective-permute-start(bf16[256,128]{1,0:T(8,128)(2,1)S(1)} %shard_map.123.refs_8_), channel_id=1, source_target_pairs={{0,2},{1,3},{2,0},{3,1},{4,6},{5,7},{6,4},{7,5},{8,10},{9,11},{10,... | collective-permute-start | bytes 196616 | tf_op jit(solution)/shard_map/ppermute | solution.py:482
  40.3 3.6 %collective-permute-start.13 = (bf16[528,128]{1,0:T(8,128)(2,1)S(1)}, bf16[528,128]{1,0:T(8,128)(2,1)S(1)}, u32[]{:S(2)}, u32[]{:S(2)}) collective-permute-start(bf16[528,128]{1,0:T(8,128)(2,1)S(1)} %get-tuple-element.46.own_msg.refs_0_), channel_id=1, source_target_pairs={{0,24},{8,16},{16,8},{24,0},{1,25},{9,17},{17,9},{25,1},{2,26},{10... | collective-permute-start | bytes 405512 | tf_op jit(solution)/shard_map/ppermute | solution.py:479
  43.9 1.5 %collective-permute-start.22 = (bf16[256,128]{1,0:T(8,128)(2,1)S(1)}, bf16[256,128]{1,0:T(8,128)(2,1)S(1)}, u32[]{:S(2)}, u32[]{:S(2)}) collective-permute-start(bf16[256,128]{1,0:T(8,128)(2,1)S(1)} %shard_map.123.refs_8_), channel_id=1, source_target_pairs={{0,4},{1,5},{2,6},{3,7},{4,0},{5,1},{6,2},{7,3},{8,12},{9,13},{10,... | collective-permute-start | bytes 196616 | tf_op jit(solution)/shard_map/ppermute | solution.py:482
  47.4 1.1 %collective-permute-start.25 = (bf16[2,272,128]{2,1,0:T(8,128)(2,1)S(1)}, bf16[2,272,128]{2,1,0:T(8,128)(2,1)S(1)}, u32[]{:S(2)}, u32[]{:S(2)}) collective-permute-start(bf16[2,272,128]{2,1,0:T(8,128)(2,1)S(1)} %get-tuple-element.58), channel_id=1, source_target_pairs={{0,2},{1,3},{2,0},{3,1},{4,6},{5,7},{6,4},{7,5},{8,10},{9,11},{10,... | collective-permute-start | bytes 417800 | tf_op jit(solution)/shard_map/ppermute | solution.py:493
  48.5 3.2 %collective-permute-done.12.refs_2_ = bf16[528,128]{1,0:T(8,128)(2,1)S(1)} collective-permute-done((bf16[528,128]{1,0:T(8,128)(2,1)S(1)}, bf16[528,128]{1,0:T(8,128)(2,1)S(1)}, u32[]{:S(2)}, u32[]{:S(2)}) %collective-permute-start.12) | collective-permute-done | bytes 135200 | tf_op jit(solution)/shard_map/ppermute | solution.py:479
  51.7 1.5 %collective-permute-start.26 = (bf16[2,272,128]{2,1,0:T(8,128)(2,1)S(1)}, bf16[2,272,128]{2,1,0:T(8,128)(2,1)S(1)}, u32[]{:S(2)}, u32[]{:S(2)}) collective-permute-start(bf16[2,272,128]{2,1,0:T(8,128)(2,1)S(1)} %get-tuple-element.59), channel_id=1, source_target_pairs={{0,4},{1,5},{2,6},{3,7},{4,0},{5,1},{6,2},{7,3},{8,12},{9,13},{10,... | collective-permute-start | bytes 417800 | tf_op jit(solution)/shard_map/ppermute | solution.py:493
  56.7 2.4 %collective-permute-done.27.refs_3_ = bf16[2,272,128]{2,1,0:T(8,128)(2,1)S(1)} collective-permute-done((bf16[2,272,128]{2,1,0:T(8,128)(2,1)S(1)}, bf16[2,272,128]{2,1,0:T(8,128)(2,1)S(1)}, u32[]{:S(2)}, u32[]{:S(2)}) %collective-permute-start.27) | collective-permute-done | bytes 139296 | tf_op jit(solution)/shard_map/ppermute | solution.py:493
  62.8 1.1 %shard_map.126 = (f32[128,2048]{1,0:T(8,128)}, f32[1,128]{1,0:T(1,128)}) custom-call(f32[128,2048]{1,0:T(8,128)S(1)} %get-tuple-element.54.total, f32[1,128]{1,0:T(1,128)S(1)} %get-tuple-element.55.squares, f32[1,128]{1,0:T(1,128)S(1)} %collective-permute-done.24.other_squares, f32[1,128]{1,0:T(1,128)S(1)} %shard_map.125.loss_in), custom_call_target="tpu_custom_call" | custom-call | flops 1048576 | tf_op jit(solution)/shard_map/pallas_call | solution.py:181
  (60 shorter events, 15.6 us)
Async XLA Ops:
  1.9 4.9 %collective-permute-start = (bf16[272,128]{1,0:T(8,128)(2,1)S(1)}, bf16[272,128]{1,0:T(8,128)(2,1)S(1)}, u32[]{:S(2)}, u32[]{:S(2)}) collective-permute-start(bf16[272,128]{1,0:T(8,128)(2,1)S(1)} %get-tuple-element.36), channel_id=1, source_target_pairs={{0,1},{1,0},{2,3},{3,2},{4,5},{5,4},{6,7},{7,6},{8,9},{9,8},{10,11... | collective-permute-start | bytes 208904 | tf_op jit(solution)/shard_map/ppermute | solution.py:450
  2.5 7.0 %collective-permute-start.1 = (bf16[272,128]{1,0:T(8,128)(2,1)S(1)}, bf16[272,128]{1,0:T(8,128)(2,1)S(1)}, u32[]{:S(2)}, u32[]{:S(2)}) collective-permute-start(bf16[272,128]{1,0:T(8,128)(2,1)S(1)} %get-tuple-element.37), channel_id=1, source_target_pairs={{0,2},{1,3},{2,0},{3,1},{4,6},{5,7},{6,4},{7,5},{8,10},{9,11},{10,... | collective-permute-start | bytes 208904 | tf_op jit(solution)/shard_map/ppermute | solution.py:450
  6.8 6.5 %collective-permute-start.4 = (bf16[272,128]{1,0:T(8,128)(2,1)S(1)}, bf16[272,128]{1,0:T(8,128)(2,1)S(1)}, u32[]{:S(2)}, u32[]{:S(2)}) collective-permute-start(bf16[272,128]{1,0:T(8,128)(2,1)S(1)} %get-tuple-element.40), channel_id=1, source_target_pairs={{0,5},{1,4},{2,7},{3,6},{4,1},{5,0},{6,3},{7,2},{8,13},{9,12},{10,... | collective-permute-start | bytes 208904 | tf_op jit(solution)/shard_map/ppermute | solution.py:450
  6.8 6.5 %collective-permute-start.5 = (bf16[272,128]{1,0:T(8,128)(2,1)S(1)}, bf16[272,128]{1,0:T(8,128)(2,1)S(1)}, u32[]{:S(2)}, u32[]{:S(2)}) collective-permute-start(bf16[272,128]{1,0:T(8,128)(2,1)S(1)} %get-tuple-element.41), channel_id=1, source_target_pairs={{0,6},{1,7},{2,4},{3,5},{4,2},{5,3},{6,0},{7,1},{8,14},{9,15},{10,... | collective-permute-start | bytes 208904 | tf_op jit(solution)/shard_map/ppermute | solution.py:450
  9.5 5.0 %collective-permute-start.6 = (bf16[272,128]{1,0:T(8,128)(2,1)S(1)}, bf16[272,128]{1,0:T(8,128)(2,1)S(1)}, u32[]{:S(2)}, u32[]{:S(2)}) collective-permute-start(bf16[272,128]{1,0:T(8,128)(2,1)S(1)} %get-tuple-element.42), channel_id=1, source_target_pairs={{0,7},{1,6},{2,5},{3,4},{4,3},{5,2},{6,1},{7,0},{8,15},{9,14},{10,... | collective-permute-start | bytes 208904 | tf_op jit(solution)/shard_map/ppermute | solution.py:450
  18.4 7.3 %collective-permute-start.10 = (bf16[32,2048]{1,0:T(8,128)(2,1)S(1)}, bf16[32,2048]{1,0:T(8,128)(2,1)S(1)}, u32[]{:S(2)}, u32[]{:S(2)}) collective-permute-start(bf16[32,2048]{1,0:T(8,128)(2,1)S(1)} %add_convert_fusion.refs_0_), channel_id=1, source_target_pairs={{0,6},{1,7},{2,4},{3,5},{4,2},{5,3},{6,0},{7,1},{8,14},{9,15},{10,... | collective-permute-start | bytes 393224 | tf_op jit(solution)/shard_map/ppermute | solution.py:469
  20.4 6.8 %collective-permute-start.8 = (bf16[32,2048]{1,0:T(8,128)(2,1)S(1)}, bf16[32,2048]{1,0:T(8,128)(2,1)S(1)}, u32[]{:S(2)}, u32[]{:S(2)}) collective-permute-start(bf16[32,2048]{1,0:T(8,128)(2,1)S(1)} %add_convert_fusion.refs_0_), channel_id=1, source_target_pairs={{0,2},{1,3},{2,0},{3,1},{4,6},{5,7},{6,4},{7,5},{8,10},{9,11},{10,... | collective-permute-start | bytes 393224 | tf_op jit(solution)/shard_map/ppermute | solution.py:469
  20.8 7.0 %collective-permute-start.9 = (bf16[32,2048]{1,0:T(8,128)(2,1)S(1)}, bf16[32,2048]{1,0:T(8,128)(2,1)S(1)}, u32[]{:S(2)}, u32[]{:S(2)}) collective-permute-start(bf16[32,2048]{1,0:T(8,128)(2,1)S(1)} %add_convert_fusion.refs_0_), channel_id=1, source_target_pairs={{0,4},{1,5},{2,6},{3,7},{4,0},{5,1},{6,2},{7,3},{8,12},{9,13},{10,... | collective-permute-start | bytes 393224 | tf_op jit(solution)/shard_map/ppermute | solution.py:469
  28.7 16.7 %collective-permute-start.14 = (bf16[528,128]{1,0:T(8,128)(2,1)S(1)}, bf16[528,128]{1,0:T(8,128)(2,1)S(1)}, u32[]{:S(2)}, u32[]{:S(2)}) collective-permute-start(bf16[528,128]{1,0:T(8,128)(2,1)S(1)} %get-tuple-element.46.own_msg.refs_0_), channel_id=1, source_target_pairs={{0,1},{1,0},{2,3},{3,2},{4,5},{5,4},{6,7},{7,6},{8,9},{9,8},{10,11... | collective-permute-start | bytes 405512 | tf_op jit(solution)/shard_map/ppermute | solution.py:478
  33.0 5.5 %collective-permute-start.20 = (bf16[64,128]{1,0:T(8,128)(2,1)S(1)}, bf16[64,128]{1,0:T(8,128)(2,1)S(1)}, u32[]{:S(2)}, u32[]{:S(2)}) collective-permute-start(bf16[64,128]{1,0:T(8,128)(2,1)S(1)} %get-tuple-element.48.attn.refs_0_), channel_id=1, source_target_pairs={{0,24},{8,16},{16,8},{24,0},{1,25},{9,17},{17,9},{25,1},{2,26},{10... | collective-permute-start | bytes 49160 | tf_op jit(solution)/shard_map/ppermute | solution.py:470
  38.5 5.4 %collective-permute-start.21 = (bf16[256,128]{1,0:T(8,128)(2,1)S(1)}, bf16[256,128]{1,0:T(8,128)(2,1)S(1)}, u32[]{:S(2)}, u32[]{:S(2)}) collective-permute-start(bf16[256,128]{1,0:T(8,128)(2,1)S(1)} %shard_map.123.refs_8_), channel_id=1, source_target_pairs={{0,2},{1,3},{2,0},{3,1},{4,6},{5,7},{6,4},{7,5},{8,10},{9,11},{10,... | collective-permute-start | bytes 196616 | tf_op jit(solution)/shard_map/ppermute | solution.py:482
  39.6 7.8 %collective-permute-start.11 = (bf16[528,128]{1,0:T(8,128)(2,1)S(1)}, bf16[528,128]{1,0:T(8,128)(2,1)S(1)}, u32[]{:S(2)}, u32[]{:S(2)}) collective-permute-start(bf16[528,128]{1,0:T(8,128)(2,1)S(1)} %get-tuple-element.46.own_msg.refs_0_), channel_id=1, source_target_pairs={{0,8},{8,0},{16,24},{24,16},{1,9},{9,1},{17,25},{25,17},{2,10},{10... | collective-permute-start | bytes 405512 | tf_op jit(solution)/shard_map/ppermute | solution.py:479
  39.6 12.1 %collective-permute-start.12 = (bf16[528,128]{1,0:T(8,128)(2,1)S(1)}, bf16[528,128]{1,0:T(8,128)(2,1)S(1)}, u32[]{:S(2)}, u32[]{:S(2)}) collective-permute-start(bf16[528,128]{1,0:T(8,128)(2,1)S(1)} %get-tuple-element.46.own_msg.refs_0_), channel_id=1, source_target_pairs={{0,16},{8,24},{16,0},{24,8},{1,17},{9,25},{17,1},{25,9},{2,18},{10... | collective-permute-start | bytes 405512 | tf_op jit(solution)/shard_map/ppermute | solution.py:479
  40.3 12.8 %collective-permute-start.13 = (bf16[528,128]{1,0:T(8,128)(2,1)S(1)}, bf16[528,128]{1,0:T(8,128)(2,1)S(1)}, u32[]{:S(2)}, u32[]{:S(2)}) collective-permute-start(bf16[528,128]{1,0:T(8,128)(2,1)S(1)} %get-tuple-element.46.own_msg.refs_0_), channel_id=1, source_target_pairs={{0,24},{8,16},{16,8},{24,0},{1,25},{9,17},{17,9},{25,1},{2,26},{10... | collective-permute-start | bytes 405512 | tf_op jit(solution)/shard_map/ppermute | solution.py:479
  43.9 10.2 %collective-permute-start.22 = (bf16[256,128]{1,0:T(8,128)(2,1)S(1)}, bf16[256,128]{1,0:T(8,128)(2,1)S(1)}, u32[]{:S(2)}, u32[]{:S(2)}) collective-permute-start(bf16[256,128]{1,0:T(8,128)(2,1)S(1)} %shard_map.123.refs_8_), channel_id=1, source_target_pairs={{0,4},{1,5},{2,6},{3,7},{4,0},{5,1},{6,2},{7,3},{8,12},{9,13},{10,... | collective-permute-start | bytes 196616 | tf_op jit(solution)/shard_map/ppermute | solution.py:482
  45.4 8.7 %collective-permute-start.23 = (bf16[256,128]{1,0:T(8,128)(2,1)S(1)}, bf16[256,128]{1,0:T(8,128)(2,1)S(1)}, u32[]{:S(2)}, u32[]{:S(2)}) collective-permute-start(bf16[256,128]{1,0:T(8,128)(2,1)S(1)} %shard_map.123.refs_8_), channel_id=1, source_target_pairs={{0,6},{1,7},{2,4},{3,5},{4,2},{5,3},{6,0},{7,1},{8,14},{9,15},{10,... | collective-permute-start | bytes 196616 | tf_op jit(solution)/shard_map/ppermute | solution.py:482
  47.4 8.3 %collective-permute-start.25 = (bf16[2,272,128]{2,1,0:T(8,128)(2,1)S(1)}, bf16[2,272,128]{2,1,0:T(8,128)(2,1)S(1)}, u32[]{:S(2)}, u32[]{:S(2)}) collective-permute-start(bf16[2,272,128]{2,1,0:T(8,128)(2,1)S(1)} %get-tuple-element.58), channel_id=1, source_target_pairs={{0,2},{1,3},{2,0},{3,1},{4,6},{5,7},{6,4},{7,5},{8,10},{9,11},{10,... | collective-permute-start | bytes 417800 | tf_op jit(solution)/shard_map/ppermute | solution.py:493
  51.7 5.1 %collective-permute-start.26 = (bf16[2,272,128]{2,1,0:T(8,128)(2,1)S(1)}, bf16[2,272,128]{2,1,0:T(8,128)(2,1)S(1)}, u32[]{:S(2)}, u32[]{:S(2)}) collective-permute-start(bf16[2,272,128]{2,1,0:T(8,128)(2,1)S(1)} %get-tuple-element.59), channel_id=1, source_target_pairs={{0,4},{1,5},{2,6},{3,7},{4,0},{5,1},{6,2},{7,3},{8,12},{9,13},{10,... | collective-permute-start | bytes 417800 | tf_op jit(solution)/shard_map/ppermute | solution.py:493
  53.1 6.0 %collective-permute-start.27 = (bf16[2,272,128]{2,1,0:T(8,128)(2,1)S(1)}, bf16[2,272,128]{2,1,0:T(8,128)(2,1)S(1)}, u32[]{:S(2)}, u32[]{:S(2)}) collective-permute-start(bf16[2,272,128]{2,1,0:T(8,128)(2,1)S(1)} %get-tuple-element.60), channel_id=1, source_target_pairs={{0,6},{1,7},{2,4},{3,5},{4,2},{5,3},{6,0},{7,1},{8,14},{9,15},{10,... | collective-permute-start | bytes 417800 | tf_op jit(solution)/shard_map/ppermute | solution.py:493
  54.1 5.0 %collective-permute-start.16 = (bf16[528,128]{1,0:T(8,128)(2,1)S(1)}, bf16[528,128]{1,0:T(8,128)(2,1)S(1)}, u32[]{:S(2)}, u32[]{:S(2)}) collective-permute-start(bf16[528,128]{1,0:T(8,128)(2,1)S(1)} %collective-permute-done.12.refs_2_), channel_id=1, source_target_pairs={{0,1},{1,0},{2,3},{3,2},{4,5},{5,4},{6,7},{7,6},{8,9},{9,8},{10,11... | collective-permute-start | bytes 405512 | tf_op jit(solution)/shard_map/ppermute | solution.py:498
  55.5 8.5 %collective-permute-start.28 = (bf16[2,272,128]{2,1,0:T(8,128)(2,1)S(1)}, bf16[2,272,128]{2,1,0:T(8,128)(2,1)S(1)}, u32[]{:S(2)}, u32[]{:S(2)}) collective-permute-start(bf16[2,272,128]{2,1,0:T(8,128)(2,1)S(1)} %get-tuple-element.50.refs_0_), channel_id=1, source_target_pairs={{0,1},{1,0},{2,3},{3,2},{4,5},{5,4},{6,7},{7,6},{8,9},{9,8},{10,11... | collective-permute-start | bytes 417800 | tf_op jit(solution)/shard_map/ppermute | solution.py:495
  55.6 8.3 %collective-permute-start.29 = (bf16[2,272,128]{2,1,0:T(8,128)(2,1)S(1)}, bf16[2,272,128]{2,1,0:T(8,128)(2,1)S(1)}, u32[]{:S(2)}, u32[]{:S(2)}) collective-permute-start(bf16[2,272,128]{2,1,0:T(8,128)(2,1)S(1)} %collective-permute-done.25.refs_1_), channel_id=1, source_target_pairs={{0,1},{1,0},{2,3},{3,2},{4,5},{5,4},{6,7},{7,6},{8,9},{9,8},{10,11... | collective-permute-start | bytes 417800 | tf_op jit(solution)/shard_map/ppermute | solution.py:495
  56.7 7.2 %collective-permute-start.30 = (bf16[2,272,128]{2,1,0:T(8,128)(2,1)S(1)}, bf16[2,272,128]{2,1,0:T(8,128)(2,1)S(1)}, u32[]{:S(2)}, u32[]{:S(2)}) collective-permute-start(bf16[2,272,128]{2,1,0:T(8,128)(2,1)S(1)} %collective-permute-done.26.refs_2_), channel_id=1, source_target_pairs={{0,1},{1,0},{2,3},{3,2},{4,5},{5,4},{6,7},{7,6},{8,9},{9,8},{10,11... | collective-permute-start | bytes 417800 | tf_op jit(solution)/shard_map/ppermute | solution.py:495
  59.1 4.9 %collective-permute-start.31 = (bf16[2,272,128]{2,1,0:T(8,128)(2,1)S(1)}, bf16[2,272,128]{2,1,0:T(8,128)(2,1)S(1)}, u32[]{:S(2)}, u32[]{:S(2)}) collective-permute-start(bf16[2,272,128]{2,1,0:T(8,128)(2,1)S(1)} %collective-permute-done.27.refs_3_), channel_id=1, source_target_pairs={{0,1},{1,0},{2,3},{3,2},{4,5},{5,4},{6,7},{7,6},{8,9},{9,8},{10,11... | collective-permute-start | bytes 417800 | tf_op jit(solution)/shard_map/ppermute | solution.py:495
  (13 other events, 70.8 us)
